TPU v7x, 128 devices: a whole 4x4x4 slice. The times are simulated.
128 devices in a mesh: dom: 128 (over y, z, x, core).
Axes of the slice: x: 4, y: 4, z: 4, core: 2. Of those that a mesh axis runs over, the one named last changes fastest.
Arguments:
- concentration: float32 [4096, 128], P('dom'), may hold values from 0 to 1
- reaction_rate: float32 [4096, 128], P('dom'), may hold values from 0.5 to 4
- step_size: float32 [1], replicated, may hold values from 1 to 2
- block_values: float32 [4096, 5, 128, 128], P('dom'), may hold values from -40 to 48, as said below
- block_columns: int32 [4096, 5], P('dom'), may hold values from 0 to 95, as said below
- row_lengths: int32 [4096], P('dom'), may hold values from 2 to 5, as said below
- send_lists: int32 [128, 4, 16], P('dom'), may hold values from 0 to 31, as said below
Outputs:
- next_concentration: float32 [4096, 128], P('dom')
Inputs may be any that keep to these rules, and one draw needn't show every extreme that they name: `send_lists`: for every partition and offset index q (offsets -2, -1, +1, +2), 16 distinct local block indices. `block_columns`: slot 0 of a block row is the row's own local block; live slots name a local block (below 32) or a ghost slot 32 + q * 16 + g of a block that the partition at offset index q sends; slot 1 of local block row q, for q = 0..3, is a ghost slot of offset index q; slots at or past the row's length repeat the row's own local block. `row_lengths`: some block row has all 5 slots live. `block_values`: slot 0 of every block row holds 8 times the identity plus a full random block; the other slots hold full random blocks.
All inputs are finite; a program needn't handle non-finite values.
Results may differ from a plain program's by a relative error of at most 0.00016.
Values sent between devices are 32-bit elements; how exact they have to be, the bound alone decides.
No kernel may reach another device: no remote copies, remote signals or barrier semaphores. Data moves between devices by JAX's collectives and lax.ppermute only.
A program may use at most 64 MiB of HBM per device.

v0:
```python
import jax
import jax.numpy as jnp
from jax import lax
from jax.sharding import Mesh
from jax.sharding import PartitionSpec as P

KRYLOV = 3
RESTARTS = 2
DOM = ("dom_0", "dom_1", "dom_2", "dom_3")


epsilon = 1e-06


def passed_along(value, axis, by):
    length = lax.axis_size(axis)
    return lax.ppermute(value, axis, [(i, (i + by) % length) for i in range(length)])


def from_everyone(value, axis):
    copies = jnp.broadcast_to(value, (lax.axis_size(axis), *value.shape))
    return lax.all_to_all(copies, axis, split_axis=0, concat_axis=0, tiled=True)


def over_copies(value, axis):
    everything = from_everyone(value, axis)
    return jnp.sum(everything, axis=0)


def one_axis_at_a_time(value, axes):
    far, near = axes
    nearer = over_copies(value, near)
    return over_copies(nearer, far)


def in_one(arrays, axis):
    line, at, done = (jnp.concatenate([a.reshape(-1) for a in arrays]), 0, [])
    total = one_axis_at_a_time(line, axis)
    for a in arrays:
        done.append(total[at : at + a.size].reshape(a.shape))
        at += a.size
    return tuple(done)


def extend_field(field, send_lists):
    packets = field[send_lists[0]]
    from_minus_two = passed_along(packets[0], DOM, -2)
    from_minus_one = passed_along(packets[1], DOM, -1)
    from_plus_one = passed_along(packets[2], DOM, 1)
    from_plus_two = passed_along(packets[3], DOM, 2)
    ghosts = [from_minus_two, from_minus_one, from_plus_one, from_plus_two]
    return jnp.concatenate([field] + ghosts, axis=0)


def product(block_values, block_columns, active, send_lists, field):
    extended = extend_field(field, send_lists)
    gathered = extended[block_columns] * active[:, :, None]
    return jnp.einsum("bsij,bsj->bi", block_values, gathered, precision=lax.Precision.HIGHEST)


def phi_column(hessenberg, substep):
    order = hessenberg.shape[0]
    augmented = jnp.zeros((order + 1, order + 1), jnp.float32)
    augmented = augmented.at[:order, :order].set(substep * hessenberg).at[0, order].set(1.0)
    reduced = augmented / 64.0
    identity = jnp.eye(order + 1, dtype=jnp.float32)
    series = identity
    for degree in range(12, 0, -1):
        series = identity + jnp.dot(reduced, series, precision=lax.Precision.HIGHEST) / degree
    for square_turn in range(6):
        series = jnp.dot(series, series, precision=lax.Precision.HIGHEST)
    return series[:order, order]


def local_dots(vectors, mapped):
    return jnp.einsum("kbi,bi->k", vectors, mapped, precision=lax.Precision.HIGHEST)


def combine(weights, vectors):
    return jnp.einsum("k,kbi->bi", weights, vectors, precision=lax.Precision.HIGHEST)


def krylov(start, apply):
    squared = one_axis_at_a_time(jnp.sum(start * start), (("dom_0", "dom_1", "dom_2"), "dom_3"))
    magnitude = jnp.sqrt(squared + epsilon)
    vectors = jnp.zeros((KRYLOV,) + start.shape, jnp.float32).at[0].set(start / magnitude)
    hessenberg = jnp.zeros((KRYLOV, KRYLOV), jnp.float32)
    mapped = apply(vectors[0])
    projection = one_axis_at_a_time(
        local_dots(vectors, mapped), (("dom_0", "dom_1", "dom_2"), "dom_3")
    )
    residue = mapped - combine(projection, vectors)
    hessenberg = hessenberg.at[:, 0].set(projection)
    for column in range(1, KRYLOV):
        mapped = apply(residue)
        inner, self_term, residue_square = in_one(
            (local_dots(vectors, mapped), jnp.sum(residue * mapped), jnp.sum(residue * residue)),
            (("dom_0", "dom_1", "dom_2"), "dom_3"),
        )
        length = jnp.sqrt(residue_square + epsilon)
        vectors = vectors.at[column].set(residue / length)
        projection = (inner / length).at[column].set(self_term / (length * length))
        hessenberg = hessenberg.at[column, column - 1].set(length).at[:, column].set(projection)
        residue = mapped / length - combine(projection, vectors)
    return (magnitude, vectors, hessenberg)


def shards(
    concentration, reaction_rate, step_size, block_values, block_columns, row_lengths, send_lists
):
    slot_count = block_columns.shape[1]
    active = (jnp.arange(slot_count, dtype=jnp.int32)[None, :] < row_lengths[:, None]).astype(
        jnp.float32
    )
    slope = reaction_rate * (1.0 - 2.0 * concentration)

    def operator(field):
        return product(block_values, block_columns, active, send_lists, field)

    def apply(field):
        return slope * field - operator(field)

    forcing = reaction_rate * concentration * (1.0 - concentration) - operator(concentration)
    substep = step_size[0] / RESTARTS
    increment = jnp.zeros_like(concentration)
    for restart in range(RESTARTS):
        start = forcing if restart == 0 else apply(increment) + forcing
        magnitude, vectors, hessenberg = krylov(start, apply)
        weights = phi_column(hessenberg, substep)
        increment = increment + substep * magnitude * combine(weights, vectors)
    return concentration + increment


def solution(mesh):
    torus = Mesh(mesh.devices.reshape(4, 4, 4, 2), ("dom_0", "dom_1", "dom_2", "dom_3"))
    placed = (
        P(DOM, None),
        P(DOM, None),
        P(),
        P(DOM, None, None, None),
        P(DOM, None),
        P(DOM),
        P(DOM, None, None),
    )
    return jax.shard_map(
        shards, mesh=torus, in_specs=placed, out_specs=P(DOM, None), check_vma=False
    )
```

profile of v0, /device:TPU:0, one launch (start us, length us, event | category | flops | bytes accessed | tf_op | source)
XLA Modules:
  0.0 408.0 jit_solution(3137005875486056520)
XLA Ops:
  2.1 8.9 %collective-permute-start = (f32[16,128]{1,0:T(8,128)S(1)}, f32[16,128]{1,0:T(8,128)S(1)}, u32[]{:S(2)}, u32[]{:S(2)}) collective-permute-start(f32[16,128]{1,0:T(8,128)S(1)} %get-tuple-element.356), channel_id=1, source_target_pairs={{0,126},{1,127},{2,0},{3,1},{4,2},{5,3},{6,4},{7,5},{8,6},{9,7},{1... | collective-permute-start | bytes 24584 | tf_op jit(solution)/shard_map/ppermute | solution.py:17
  21.4 12.6 %fusion.36 = f32[32,1,128,1]{2,1,3,0:T(1,128)S(1)} fusion(f32[32,5,128,128]{3,2,1,0:T(8,128)} %param.58, f32[32,5,128,1]{2,1,0,3:T(8,128)S(1)} %multiply_bitcast_fusion.7), kind=kOutput, calls=%fused_computation.132 | convolution fusion | flops 31457280 | bytes 10584064 | tf_op jit(solution)/shard_map/bsij,bsj->bi/dot_general | solution.py:58
  40.3 13.4 %all_to_all.97 = f32[64,1,1]{2,1,0:T(1,128)S(1)} all-to-all(f32[64,1,1]{2,1,0:T(1,128)S(1)} %broadcast_in_dim.36), channel_id=1, replica_groups=mesh['dom_0'=4,'dom_1'=4,'dom_2'=4,'dom_3'=2] {'dom_0','dom_1','dom_2'}, dimensions={0} | all-to-all | bytes 512 | tf_op jit(solution)/shard_map/all_to_all | solution.py:22
  59.5 7.1 %collective-permute-done.6 = f32[16,128]{1,0:T(8,128)S(1)} collective-permute-done((f32[16,128]{1,0:T(8,128)S(1)}, f32[16,128]{1,0:T(8,128)S(1)}, u32[]{:S(2)}, u32[]{:S(2)}) %collective-permute-start.6) | collective-permute-done | bytes 8224 | tf_op jit(solution)/shard_map/ppermute | solution.py:17
  68.6 12.6 %fusion.34 = f32[32,1,128,1]{2,1,3,0:T(1,128)S(1)} fusion(f32[32,5,128,128]{3,2,1,0:T(8,128)} %param.58, f32[32,5,128,1]{2,1,0,3:T(8,128)S(1)} %multiply_bitcast_fusion.6), kind=kOutput, calls=%fused_computation.130 | convolution fusion | flops 31457280 | bytes 10584064 | tf_op jit(solution)/shard_map/bsij,bsj->bi/dot_general | solution.py:58
  85.5 13.4 %all_to_all.99 = f32[64,1,3]{2,1,0:T(1,128)S(1)} all-to-all(f32[64,1,3]{2,1,0:T(1,128)S(1)} %broadcast_in_dim.38), channel_id=1, replica_groups=mesh['dom_0'=4,'dom_1'=4,'dom_2'=4,'dom_3'=2] {'dom_0','dom_1','dom_2'}, dimensions={0} | all-to-all | bytes 1536 | tf_op jit(solution)/shard_map/all_to_all | solution.py:22
  103.7 7.1 %collective-permute-done.10 = f32[16,128]{1,0:T(8,128)S(1)} collective-permute-done((f32[16,128]{1,0:T(8,128)S(1)}, f32[16,128]{1,0:T(8,128)S(1)}, u32[]{:S(2)}, u32[]{:S(2)}) %collective-permute-start.10) | collective-permute-done | bytes 8224 | tf_op jit(solution)/shard_map/ppermute | solution.py:17
  112.6 12.6 %fusion.32 = f32[32,1,128,1]{2,1,3,0:T(1,128)S(1)} fusion(f32[32,5,128,128]{3,2,1,0:T(8,128)} %param.58, f32[32,5,128,1]{2,1,0,3:T(8,128)S(1)} %multiply_bitcast_fusion.5), kind=kOutput, calls=%fused_computation.128 | convolution fusion | flops 31457280 | bytes 10584064 | tf_op jit(solution)/shard_map/bsij,bsj->bi/dot_general | solution.py:58
  140.3 6.4 %all-to-all-done.5 = f32[64,1,5]{2,1,0:T(1,128)S(1)} async-done(((f32[64,1,5]{2,1,0:T(1,128)}), f32[64,1,5]{2,1,0:T(1,128)S(1)}, u32[]{:S(2)}, u32[]{:S(2)}) %all-to-all-start.5) | async-done | bytes 1312 | tf_op jit(solution)/shard_map/all_to_all | solution.py:22
  154.2 7.2 %collective-permute-done.14 = f32[16,128]{1,0:T(8,128)S(1)} collective-permute-done((f32[16,128]{1,0:T(8,128)S(1)}, f32[16,128]{1,0:T(8,128)S(1)}, u32[]{:S(2)}, u32[]{:S(2)}) %collective-permute-start.14) | collective-permute-done | bytes 8224 | tf_op jit(solution)/shard_map/ppermute | solution.py:17
  163.2 12.6 %fusion.30 = f32[32,1,128,1]{2,1,3,0:T(1,128)S(1)} fusion(f32[32,5,128,128]{3,2,1,0:T(8,128)} %param.58, f32[32,5,128,1]{2,1,0,3:T(8,128)S(1)} %multiply_bitcast_fusion.4), kind=kOutput, calls=%fused_computation.126 | convolution fusion | flops 31457280 | bytes 10584064 | tf_op jit(solution)/shard_map/bsij,bsj->bi/dot_general | solution.py:58
  187.9 8.9 %all-to-all-done.7 = f32[64,1,5]{2,1,0:T(1,128)S(1)} async-done(((f32[64,1,5]{2,1,0:T(1,128)}), f32[64,1,5]{2,1,0:T(1,128)S(1)}, u32[]{:S(2)}, u32[]{:S(2)}) %all-to-all-start.7) | async-done | bytes 1312 | tf_op jit(solution)/shard_map/all_to_all | solution.py:22
  211.9 7.1 %collective-permute-done.18 = f32[16,128]{1,0:T(8,128)S(1)} collective-permute-done((f32[16,128]{1,0:T(8,128)S(1)}, f32[16,128]{1,0:T(8,128)S(1)}, u32[]{:S(2)}, u32[]{:S(2)}) %collective-permute-start.18) | collective-permute-done | bytes 8224 | tf_op jit(solution)/shard_map/ppermute | solution.py:17
  221.0 12.6 %fusion.28 = f32[32,1,128,1]{2,1,3,0:T(1,128)S(1)} fusion(f32[32,5,128,128]{3,2,1,0:T(8,128)} %param.58, f32[32,5,128,1]{2,1,0,3:T(8,128)S(1)} %multiply_bitcast_fusion.3), kind=kOutput, calls=%fused_computation.124 | convolution fusion | flops 31457280 | bytes 10584064 | tf_op jit(solution)/shard_map/bsij,bsj->bi/dot_general | solution.py:58
  240.1 13.4 %all_to_all.103 = f32[64,1,1]{2,1,0:T(1,128)S(1)} all-to-all(f32[64,1,1]{2,1,0:T(1,128)S(1)} %broadcast_in_dim.86), channel_id=1, replica_groups=mesh['dom_0'=4,'dom_1'=4,'dom_2'=4,'dom_3'=2] {'dom_0','dom_1','dom_2'}, dimensions={0} | all-to-all | bytes 512 | tf_op jit(solution)/shard_map/all_to_all | solution.py:22
  259.5 7.1 %collective-permute-done.22 = f32[16,128]{1,0:T(8,128)S(1)} collective-permute-done((f32[16,128]{1,0:T(8,128)S(1)}, f32[16,128]{1,0:T(8,128)S(1)}, u32[]{:S(2)}, u32[]{:S(2)}) %collective-permute-start.22) | collective-permute-done | bytes 8224 | tf_op jit(solution)/shard_map/ppermute | solution.py:17
  268.4 12.6 %fusion.26 = f32[32,1,128,1]{2,1,3,0:T(1,128)S(1)} fusion(f32[32,5,128,128]{3,2,1,0:T(8,128)} %param.58, f32[32,5,128,1]{2,1,0,3:T(8,128)S(1)} %multiply_bitcast_fusion.2), kind=kOutput, calls=%fused_computation.122 | convolution fusion | flops 31457280 | bytes 10584064 | tf_op jit(solution)/shard_map/bsij,bsj->bi/dot_general | solution.py:58
  285.2 13.6 %all_to_all.105 = f32[64,1,3]{2,1,0:T(1,128)S(1)} all-to-all(f32[64,1,3]{2,1,0:T(1,128)S(1)} %broadcast_in_dim.88), channel_id=1, replica_groups=mesh['dom_0'=4,'dom_1'=4,'dom_2'=4,'dom_3'=2] {'dom_0','dom_1','dom_2'}, dimensions={0} | all-to-all | bytes 1536 | tf_op jit(solution)/shard_map/all_to_all | solution.py:22
  303.7 7.1 %collective-permute-done.26 = f32[16,128]{1,0:T(8,128)S(1)} collective-permute-done((f32[16,128]{1,0:T(8,128)S(1)}, f32[16,128]{1,0:T(8,128)S(1)}, u32[]{:S(2)}, u32[]{:S(2)}) %collective-permute-start.26) | collective-permute-done | bytes 8224 | tf_op jit(solution)/shard_map/ppermute | solution.py:17
  312.6 12.6 %fusion.24 = f32[32,1,128,1]{2,1,3,0:T(1,128)S(1)} fusion(f32[32,5,128,128]{3,2,1,0:T(8,128)} %param.58, f32[32,5,128,1]{2,1,0,3:T(8,128)S(1)} %multiply_bitcast_fusion.1), kind=kOutput, calls=%fused_computation.120 | convolution fusion | flops 31457280 | bytes 10584064 | tf_op jit(solution)/shard_map/bsij,bsj->bi/dot_general | solution.py:58
  336.6 9.5 %all-to-all-done.13 = f32[64,1,5]{2,1,0:T(1,128)S(1)} async-done(((f32[64,1,5]{2,1,0:T(1,128)}), f32[64,1,5]{2,1,0:T(1,128)S(1)}, u32[]{:S(2)}, u32[]{:S(2)}) %all-to-all-start.13) | async-done | bytes 1312 | tf_op jit(solution)/shard_map/all_to_all | solution.py:22
  353.7 7.2 %collective-permute-done.30 = f32[16,128]{1,0:T(8,128)S(1)} collective-permute-done((f32[16,128]{1,0:T(8,128)S(1)}, f32[16,128]{1,0:T(8,128)S(1)}, u32[]{:S(2)}, u32[]{:S(2)}) %collective-permute-start.30) | collective-permute-done | bytes 8224 | tf_op jit(solution)/shard_map/ppermute | solution.py:17
  362.7 12.6 %fusion.22 = f32[32,1,128,1]{2,1,3,0:T(1,128)S(1)} fusion(f32[32,5,128,128]{3,2,1,0:T(8,128)} %param.58, f32[32,5,128,1]{2,1,0,3:T(8,128)S(1)} %multiply_bitcast_fusion), kind=kOutput, calls=%fused_computation.118 | convolution fusion | flops 31457280 | bytes 10584064 | tf_op jit(solution)/shard_map/bsij,bsj->bi/dot_general | solution.py:58
  387.4 8.9 %all-to-all-done.15 = f32[64,1,5]{2,1,0:T(1,128)S(1)} async-done(((f32[64,1,5]{2,1,0:T(1,128)}), f32[64,1,5]{2,1,0:T(1,128)S(1)}, u32[]{:S(2)}, u32[]{:S(2)}) %all-to-all-start.15) | async-done | bytes 1312 | tf_op jit(solution)/shard_map/all_to_all | solution.py:22
  (298 shorter events, 152.2 us)
Async XLA Ops:
  2.1 12.4 %collective-permute-start = (f32[16,128]{1,0:T(8,128)S(1)}, f32[16,128]{1,0:T(8,128)S(1)}, u32[]{:S(2)}, u32[]{:S(2)}) collective-permute-start(f32[16,128]{1,0:T(8,128)S(1)} %get-tuple-element.356), channel_id=1, source_target_pairs={{0,126},{1,127},{2,0},{3,1},{4,2},{5,3},{6,4},{7,5},{8,6},{9,7},{1... | collective-permute-start | bytes 24584 | tf_op jit(solution)/shard_map/ppermute | solution.py:17
  11.0 8.5 %collective-permute-start.2 = (f32[16,128]{1,0:T(8,128)S(1)}, f32[16,128]{1,0:T(8,128)S(1)}, u32[]{:S(2)}, u32[]{:S(2)}) collective-permute-start(f32[16,128]{1,0:T(8,128)S(1)} %get-tuple-element.354), channel_id=1, source_target_pairs={{0,1},{1,2},{2,3},{3,4},{4,5},{5,6},{6,7},{7,8},{8,9},{9,10},{10,1... | collective-permute-start | bytes 24584 | tf_op jit(solution)/shard_map/ppermute | solution.py:17
  11.5 9.1 %collective-permute-start.3 = (f32[16,128]{1,0:T(8,128)S(1)}, f32[16,128]{1,0:T(8,128)S(1)}, u32[]{:S(2)}, u32[]{:S(2)}) collective-permute-start(f32[16,128]{1,0:T(8,128)S(1)} %get-tuple-element.353), channel_id=1, source_target_pairs={{0,2},{1,3},{2,4},{3,5},{4,6},{5,7},{6,8},{7,9},{8,10},{9,11},{10,... | collective-permute-start | bytes 24584 | tf_op jit(solution)/shard_map/ppermute | solution.py:17
  58.1 8.5 %collective-permute-start.6 = (f32[16,128]{1,0:T(8,128)S(1)}, f32[16,128]{1,0:T(8,128)S(1)}, u32[]{:S(2)}, u32[]{:S(2)}) collective-permute-start(f32[16,128]{1,0:T(8,128)S(1)} %get-tuple-element.350), channel_id=1, source_target_pairs={{0,1},{1,2},{2,3},{3,4},{4,5},{5,6},{6,7},{7,8},{8,9},{9,10},{10,1... | collective-permute-start | bytes 24584 | tf_op jit(solution)/shard_map/ppermute | solution.py:17
  58.6 9.3 %collective-permute-start.7 = (f32[16,128]{1,0:T(8,128)S(1)}, f32[16,128]{1,0:T(8,128)S(1)}, u32[]{:S(2)}, u32[]{:S(2)}) collective-permute-start(f32[16,128]{1,0:T(8,128)S(1)} %get-tuple-element.349), channel_id=1, source_target_pairs={{0,2},{1,3},{2,4},{3,5},{4,6},{5,7},{6,8},{7,9},{8,10},{9,11},{10,... | collective-permute-start | bytes 24584 | tf_op jit(solution)/shard_map/ppermute | solution.py:17
  102.2 8.5 %collective-permute-start.10 = (f32[16,128]{1,0:T(8,128)S(1)}, f32[16,128]{1,0:T(8,128)S(1)}, u32[]{:S(2)}, u32[]{:S(2)}) collective-permute-start(f32[16,128]{1,0:T(8,128)S(1)} %get-tuple-element.346), channel_id=1, source_target_pairs={{0,1},{1,2},{2,3},{3,4},{4,5},{5,6},{6,7},{7,8},{8,9},{9,10},{10,1... | collective-permute-start | bytes 24584 | tf_op jit(solution)/shard_map/ppermute | solution.py:17
  102.7 9.1 %collective-permute-start.11 = (f32[16,128]{1,0:T(8,128)S(1)}, f32[16,128]{1,0:T(8,128)S(1)}, u32[]{:S(2)}, u32[]{:S(2)}) collective-permute-start(f32[16,128]{1,0:T(8,128)S(1)} %get-tuple-element.345), channel_id=1, source_target_pairs={{0,2},{1,3},{2,4},{3,5},{4,6},{5,7},{6,8},{7,9},{8,10},{9,11},{10,... | collective-permute-start | bytes 24584 | tf_op jit(solution)/shard_map/ppermute | solution.py:17
  132.5 14.2 %all-to-all-start.5 = ((f32[64,1,5]{2,1,0:T(1,128)}), f32[64,1,5]{2,1,0:T(1,128)S(1)}, u32[]{:S(2)}, u32[]{:S(2)}) async-start(f32[64,1,5]{2,1,0:T(1,128)} %broadcast_in_dim.40), calls=%async_computation.5 | async-start | bytes 65536 | tf_op jit(solution)/shard_map/all_to_all | solution.py:22
  149.7 3.8 collective-permute-start.12
  152.8 8.6 %collective-permute-start.14 = (f32[16,128]{1,0:T(8,128)S(1)}, f32[16,128]{1,0:T(8,128)S(1)}, u32[]{:S(2)}, u32[]{:S(2)}) collective-permute-start(f32[16,128]{1,0:T(8,128)S(1)} %get-tuple-element.342), channel_id=1, source_target_pairs={{0,1},{1,2},{2,3},{3,4},{4,5},{5,6},{6,7},{7,8},{8,9},{9,10},{10,1... | collective-permute-start | bytes 24584 | tf_op jit(solution)/shard_map/ppermute | solution.py:17
  153.3 9.1 %collective-permute-start.15 = (f32[16,128]{1,0:T(8,128)S(1)}, f32[16,128]{1,0:T(8,128)S(1)}, u32[]{:S(2)}, u32[]{:S(2)}) collective-permute-start(f32[16,128]{1,0:T(8,128)S(1)} %get-tuple-element.341), channel_id=1, source_target_pairs={{0,2},{1,3},{2,4},{3,5},{4,6},{5,7},{6,8},{7,9},{8,10},{9,11},{10,... | collective-permute-start | bytes 24584 | tf_op jit(solution)/shard_map/ppermute | solution.py:17
  182.6 14.2 %all-to-all-start.7 = ((f32[64,1,5]{2,1,0:T(1,128)}), f32[64,1,5]{2,1,0:T(1,128)S(1)}, u32[]{:S(2)}, u32[]{:S(2)}) async-start(f32[64,1,5]{2,1,0:T(1,128)} %broadcast_in_dim.84), calls=%async_computation.7 | async-start | bytes 65536 | tf_op jit(solution)/shard_map/all_to_all | solution.py:22
  208.0 3.8 collective-permute-start.16
  210.5 8.5 %collective-permute-start.18 = (f32[16,128]{1,0:T(8,128)S(1)}, f32[16,128]{1,0:T(8,128)S(1)}, u32[]{:S(2)}, u32[]{:S(2)}) collective-permute-start(f32[16,128]{1,0:T(8,128)S(1)} %get-tuple-element.338), channel_id=1, source_target_pairs={{0,1},{1,2},{2,3},{3,4},{4,5},{5,6},{6,7},{7,8},{8,9},{9,10},{10,1... | collective-permute-start | bytes 24584 | tf_op jit(solution)/shard_map/ppermute | solution.py:17
  211.0 9.2 %collective-permute-start.19 = (f32[16,128]{1,0:T(8,128)S(1)}, f32[16,128]{1,0:T(8,128)S(1)}, u32[]{:S(2)}, u32[]{:S(2)}) collective-permute-start(f32[16,128]{1,0:T(8,128)S(1)} %get-tuple-element.337), channel_id=1, source_target_pairs={{0,2},{1,3},{2,4},{3,5},{4,6},{5,7},{6,8},{7,9},{8,10},{9,11},{10,... | collective-permute-start | bytes 24584 | tf_op jit(solution)/shard_map/ppermute | solution.py:17
  258.0 8.5 %collective-permute-start.22 = (f32[16,128]{1,0:T(8,128)S(1)}, f32[16,128]{1,0:T(8,128)S(1)}, u32[]{:S(2)}, u32[]{:S(2)}) collective-permute-start(f32[16,128]{1,0:T(8,128)S(1)} %get-tuple-element.334), channel_id=1, source_target_pairs={{0,1},{1,2},{2,3},{3,4},{4,5},{5,6},{6,7},{7,8},{8,9},{9,10},{10,1... | collective-permute-start | bytes 24584 | tf_op jit(solution)/shard_map/ppermute | solution.py:17
  258.5 9.1 %collective-permute-start.23 = (f32[16,128]{1,0:T(8,128)S(1)}, f32[16,128]{1,0:T(8,128)S(1)}, u32[]{:S(2)}, u32[]{:S(2)}) collective-permute-start(f32[16,128]{1,0:T(8,128)S(1)} %get-tuple-element.333), channel_id=1, source_target_pairs={{0,2},{1,3},{2,4},{3,5},{4,6},{5,7},{6,8},{7,9},{8,10},{9,11},{10,... | collective-permute-start | bytes 24584 | tf_op jit(solution)/shard_map/ppermute | solution.py:17
  302.2 8.5 %collective-permute-start.26 = (f32[16,128]{1,0:T(8,128)S(1)}, f32[16,128]{1,0:T(8,128)S(1)}, u32[]{:S(2)}, u32[]{:S(2)}) collective-permute-start(f32[16,128]{1,0:T(8,128)S(1)} %get-tuple-element.330), channel_id=1, source_target_pairs={{0,1},{1,2},{2,3},{3,4},{4,5},{5,6},{6,7},{7,8},{8,9},{9,10},{10,1... | collective-permute-start | bytes 24584 | tf_op jit(solution)/shard_map/ppermute | solution.py:17
  302.7 9.1 %collective-permute-start.27 = (f32[16,128]{1,0:T(8,128)S(1)}, f32[16,128]{1,0:T(8,128)S(1)}, u32[]{:S(2)}, u32[]{:S(2)}) collective-permute-start(f32[16,128]{1,0:T(8,128)S(1)} %get-tuple-element.329), channel_id=1, source_target_pairs={{0,2},{1,3},{2,4},{3,5},{4,6},{5,7},{6,8},{7,9},{8,10},{9,11},{10,... | collective-permute-start | bytes 24584 | tf_op jit(solution)/shard_map/ppermute | solution.py:17
  332.0 14.2 %all-to-all-start.13 = ((f32[64,1,5]{2,1,0:T(1,128)}), f32[64,1,5]{2,1,0:T(1,128)S(1)}, u32[]{:S(2)}, u32[]{:S(2)}) async-start(f32[64,1,5]{2,1,0:T(1,128)} %broadcast_in_dim.90), calls=%async_computation.13 | async-start | bytes 65536 | tf_op jit(solution)/shard_map/all_to_all | solution.py:22
  349.1 4.1 collective-permute-start.28
  352.3 8.6 %collective-permute-start.30 = (f32[16,128]{1,0:T(8,128)S(1)}, f32[16,128]{1,0:T(8,128)S(1)}, u32[]{:S(2)}, u32[]{:S(2)}) collective-permute-start(f32[16,128]{1,0:T(8,128)S(1)} %get-tuple-element.326), channel_id=1, source_target_pairs={{0,1},{1,2},{2,3},{3,4},{4,5},{5,6},{6,7},{7,8},{8,9},{9,10},{10,1... | collective-permute-start | bytes 24584 | tf_op jit(solution)/shard_map/ppermute | solution.py:17
  352.8 9.1 %collective-permute-start.31 = (f32[16,128]{1,0:T(8,128)S(1)}, f32[16,128]{1,0:T(8,128)S(1)}, u32[]{:S(2)}, u32[]{:S(2)}) collective-permute-start(f32[16,128]{1,0:T(8,128)S(1)} %get-tuple-element.325), channel_id=1, source_target_pairs={{0,2},{1,3},{2,4},{3,5},{4,6},{5,7},{6,8},{7,9},{8,10},{9,11},{10,... | collective-permute-start | bytes 24584 | tf_op jit(solution)/shard_map/ppermute | solution.py:17
  382.2 14.2 %all-to-all-start.15 = ((f32[64,1,5]{2,1,0:T(1,128)}), f32[64,1,5]{2,1,0:T(1,128)S(1)}, u32[]{:S(2)}, u32[]{:S(2)}) async-start(f32[64,1,5]{2,1,0:T(1,128)} %broadcast_in_dim.92), calls=%async_computation.15 | async-start | bytes 65536 | tf_op jit(solution)/shard_map/all_to_all | solution.py:22
  (14 other events, 96.8 us)
where the time goes:
time: 416 us; the launch traced here: 408 us
  matrix products  112 us (27%)
  waiting for transfers between devices  103 us (25%)
  blocking collectives  83.7 us (20%)
  starting transfers between devices  49.6 us (12%)
  other arithmetic  26.1 us (6%)
  local copies, waits for them, and re-layouts  25.7 us (6%)
  between operations  8.55 us (2%)
    dot_general x8, matrix products, product(): jnp.einsum('bsij,bsj->bi', block_values, gathered, precision=lax.Precisio...  101 us
    all_to_all x12, blocking collectives, from_everyone(): return lax.all_to_all(copies, axis, split_axis=0, concat_axis=0, tiled=True)  83.7 us
    ppermute x32, waiting for transfers between devices, passed_along(): lax.ppermute(value, axis, [(i, (i + by) % length) for i in range(length)])  69 us
    all_to_all x4, waiting for transfers between devices, from_everyone(): return lax.all_to_all(copies, axis, split_axis=0, concat_axis=0, tiled=True)  33.8 us
    ppermute x32, starting transfers between devices, passed_along(): lax.ppermute(value, axis, [(i, (i + by) % length) for i in range(length)])  31.1 us
    all_to_all x4, starting transfers between devices, from_everyone(): return lax.all_to_all(copies, axis, split_axis=0, concat_axis=0, tiled=True)  18.5 us
    another operation x12, other arithmetic  9.37 us
  transfers between devices with their start and end apart: 36, of which 32 were waited for; matrix products, arithmetic and copies ran while one was open for 2% of the time, Pallas kernels for 0%

commit v1 on v0

v1 whole, which is shorter than its diff:
```python
import jax
import jax.numpy as jnp
from jax import lax
from jax.experimental import pallas as pl
from jax.experimental.pallas import tpu as pltpu
from jax.sharding import PartitionSpec as P

BLK = 128
ROWS = 32
SLOTS = 5
GHOST = 16
ENTRIES = ROWS * SLOTS
DEGREE = 6
SHIFT = 8.0
SCALE = 0.25
PAIRS = [(a, b) for b in range(DEGREE + 1) for a in range(min(b, DEGREE - 1) + 1)]

FIRST = 0
LAST = 32
REMOTE = 64
COLUMN = 128
SEND = 288
TABLE = 384

f32 = jnp.float32
bf16 = jnp.bfloat16


def vmem(n=1):
    return [pl.BlockSpec(memory_space=pltpu.VMEM)] * n


def smem(n=1):
    return [pl.BlockSpec(memory_space=pltpu.SMEM)] * n


def exchanges(devices):
    two = [(p, (p + 2) % devices) for p in range(devices)]
    one = [(p, (p + 1) % devices) for p in range(devices)]
    picked = (
        [e for e in two if e[0] % 4 >= 2],
        [e for e in one if e[0] % 2 == 1],
        [e for e in two if e[0] % 4 < 2],
        [e for e in one if e[0] % 2 == 0],
    )
    return [[(a, b) for a, b in es] + [(b, a) for a, b in es] for es in picked]


def roles():
    place = lax.axis_index("dom")
    even = (place % 2) == 0
    low = (place % 4) < 2
    pick = lambda c, a, b: jnp.where(c, jnp.int32(a), jnp.int32(b))
    return pick(low, 0, 3), pick(even, 1, 2), pick(low, 3, 0), pick(even, 2, 1)


def write_packets(field, row_of, packets):
    for t in range(4):
        for g in range(GHOST):
            packets[t][g : g + 1, :] = field[pl.ds(row_of(t, g), 1), :]


def first_packets(send, field, *packets):
    by = roles()
    write_packets(field, lambda t, g: send[0, by[t], g], packets)


def partial_products(table, begin, end, place, blocks, field, pieces):
    def row(b, carry):
        def entry(e, total):
            at = place(e)
            return total + blocks[at] * field[pl.ds(table[COLUMN + at], 1), :]

        total = lax.fori_loop(begin(b), end(b), entry, jnp.zeros((BLK, BLK), f32))
        span = pl.ds(pl.multiple_of(b * BLK, BLK), BLK)
        high = total.astype(bf16)
        rest = total - high.astype(f32)
        middle = rest.astype(bf16)
        pieces[0, span, :] = high
        pieces[1, span, :] = middle
        pieces[2, span, :] = (rest - middle.astype(f32)).astype(bf16)
        return carry

    lax.fori_loop(0, ROWS, row, 0)


def column_sums(pieces, out):
    ones = jnp.ones((8, BLK), bf16)
    for b in range(ROWS):
        total = sum(
            lax.dot_general(
                ones,
                pieces[k, b * BLK : (b + 1) * BLK, :],
                (((1,), (1,)), ((), ())),
                preferred_element_type=f32,
            )
            for k in range(3)
        )
        out[b : b + 1, :] = total[0:1]


def local_product(table, blocks, field, pieces, out):
    partial_products(
        table,
        lambda b: table[FIRST + b],
        lambda b: table[LAST + b],
        lambda e: e,
        blocks,
        field,
        pieces,
    )
    column_sums(pieces, out)


def setup(columns, lengths, send, values, field, rate, blocks, table, out, pieces, done):
    by = roles()
    place = lax.axis_index("dom")
    even = (place % 2) == 0
    low = (place % 4) < 2
    at = (
        jnp.where(low, 2, 0),
        jnp.where(even, 3, 1),
        jnp.where(even, 1, 3),
        jnp.where(low, 0, 2),
    )

    def row(b, carry):
        near, far = carry
        length = lengths[b]
        table[FIRST + b] = near
        table[REMOTE + b] = far
        last = near
        for s in range(SLOTS):
            column = columns[b, s]
            live = s < length
            ghost = jnp.logical_and(live, column >= ROWS)
            index = jnp.maximum(column - ROWS, 0)
            q = index // GHOST
            spot = jnp.where(q < 2, jnp.where(q == 0, at[0], at[1]), jnp.where(q == 2, at[2], at[3]))
            target = jnp.where(ghost, ENTRIES - 1 - far, near)
            table[COLUMN + target] = jnp.where(ghost, spot * GHOST + index % GHOST, column)
            pltpu.make_async_copy(values.at[b, s], blocks.at[target], done).start()
            one = ghost.astype(jnp.int32)
            far = far + one
            near = near + 1 - one
            last = jnp.where(live, near, last)
        table[LAST + b] = last
        return near, far

    _, far = lax.fori_loop(0, ROWS, row, (jnp.int32(0), jnp.int32(0)))
    table[REMOTE + ROWS] = far
    for t in range(4):
        for g in range(GHOST):
            table[SEND + t * GHOST + g] = send[0, by[t], g]
    pltpu.make_async_copy(blocks, blocks, done).wait()
    local_product(table, blocks, field, pieces, out)
    out[...] = rate[...] * field[...] * (1.0 - field[...]) - out[...]


def near_part(table, blocks, field, rate, concentration, out, pieces):
    local_product(table, blocks, field, pieces, out)
    slope = rate[...] * (1.0 - 2.0 * concentration[...]) + SHIFT
    out[...] = slope * field[...] - out[...]


def ghost_product(table, blocks, near, arrived, out, ghosts, pieces, scale):
    for t in range(4):
        ghosts[t * GHOST : (t + 1) * GHOST, :] = arrived[t][...]
    partial_products(
        table,
        lambda b: table[REMOTE + b],
        lambda b: table[REMOTE + b + 1],
        lambda e: ENTRIES - 1 - e,
        blocks,
        ghosts,
        pieces,
    )
    column_sums(pieces, out)
    out[...] = (near[...] - out[...]) * scale


def far_part(scale):
    def kernel(table, blocks, near, g0, g1, g2, g3, out, p0, p1, p2, p3, ghosts, pieces):
        ghost_product(table, blocks, near, (g0, g1, g2, g3), out, ghosts, pieces, scale)
        write_packets(out, lambda t, g: table[SEND + t * GHOST + g], (p0, p1, p2, p3))

    return kernel


def last_part(table, blocks, near, g0, g1, g2, g3, *rest):
    basis = rest[:DEGREE]
    sums, out, ghosts, pieces, rows = rest[DEGREE:]
    ghost_product(table, blocks, near, (g0, g1, g2, g3), out, ghosts, pieces, SCALE)
    basis = basis + (out,)
    rows[...] = jnp.zeros((BLK, BLK), f32)
    for k, (a, b) in enumerate(PAIRS):
        both = basis[a][...] * basis[b][...]
        rows[k : k + 1, :] = jnp.sum(both, axis=0, keepdims=True)
    line = lax.dot_general(
        jnp.ones((8, BLK), f32),
        rows[...],
        (((1,), (1,)), ((), ())),
        precision=lax.Precision.HIGHEST,
        preferred_element_type=f32,
    )
    sums[...] = jnp.broadcast_to(line[0:1], sums.shape)


def add(x, y):
    if x is None:
        return y
    return x if y is None else x + y


def times(x, y):
    return None if x is None or y is None else x * y


def minus(x, y):
    if y is None:
        return x
    return -y if x is None else x - y


def jacobian(v):
    out = [None if x is None else x * -SHIFT for x in v]
    for k in range(DEGREE):
        if v[k] is not None:
            out[k + 1] = add(out[k + 1], v[k] * (1.0 / SCALE))
    return out


def through(gram, v):
    return [
        (lambda terms: None if not terms else sum(terms[1:], terms[0]))(
            [gram[min(a, b), max(a, b)] * v[b] for b in range(DEGREE + 1) if v[b] is not None and (a, b) != (DEGREE, DEGREE)]
        )
        for a in range(DEGREE + 1)
    ]


def dot(u, v):
    terms = [x * y for x, y in zip(u, v) if x is not None and y is not None]
    return sum(terms[1:], terms[0])


def scaled(v, x):
    return [None if y is None else y * x for y in v]


def phi_weights(h, substep):
    n = len(h)
    reduced = [[None if x is None else x * substep * (1.0 / 64.0) for x in r] for r in h]
    matmul = lambda p, q: [
        [
            (lambda ts: None if not ts else sum(ts[1:], ts[0]))(
                [p[i][k] * q[k][j] for k in range(n) if p[i][k] is not None and q[k][j] is not None]
            )
            for j in range(n)
        ]
        for i in range(n)
    ]
    apply = lambda p, q: [
        (lambda ts: None if not ts else sum(ts[1:], ts[0]))(
            [p[i][k] * q[k] for k in range(n) if p[i][k] is not None and q[k] is not None]
        )
        for i in range(n)
    ]
    block = [[1.0 if i == j else None for j in range(n)] for i in range(n)]
    column = [None] * n
    for degree in range(12, 0, -1):
        inverse = 1.0 / degree
        block = matmul(reduced, block)
        block = [[None if x is None else x * inverse for x in r] for r in block]
        for i in range(n):
            block[i][i] = add(block[i][i], 1.0)
        column = apply(reduced, column)
        column[0] = add(column[0], 1.0 / 64.0)
        column = [None if x is None else x * inverse for x in column]
    for turn in range(6):
        moved = apply(block, column)
        column = [add(x, y) for x, y in zip(moved, column)]
        block = matmul(block, block)
    return column


def finish(step, everyone, concentration, *rest):
    basis, out = rest[:DEGREE], rest[DEGREE]
    total = jnp.sum(everyone[...], axis=0, keepdims=True)
    gram = {
        pair: jnp.broadcast_to(total[:, k : k + 1], (8, BLK)) for k, pair in enumerate(PAIRS)
    }
    substep = jnp.full((8, BLK), step[0] * 0.5, f32)
    one = jnp.ones((8, BLK), f32)
    forcing = [one] + [None] * DEGREE
    increment = [None] * (DEGREE + 1)
    for restart in range(2):
        start = forcing if restart == 0 else [add(x, y) for x, y in zip(jacobian(increment), forcing)]
        magnitude = jnp.sqrt(dot(start, through(gram, start)) + 1e-6)
        vectors = [scaled(start, 1.0 / magnitude)]
        hessenberg = [[None] * 3 for _ in range(3)]
        for j in range(3):
            mapped = jacobian(vectors[j])
            seen = through(gram, mapped)
            weights = [dot(v, seen) for v in vectors]
            for k, weight in enumerate(weights):
                hessenberg[k][j] = weight
            if j < 2:
                for v, weight in zip(vectors, weights):
                    mapped = [minus(x, times(y, weight)) for x, y in zip(mapped, v)]
                length = jnp.sqrt(dot(mapped, through(gram, mapped)) + 1e-6)
                hessenberg[j + 1][j] = length
                vectors.append(scaled(mapped, 1.0 / length))
        phi = phi_weights(hessenberg, substep)
        for v, weight in zip(vectors, phi):
            factor = substep * magnitude * weight
            increment = [add(x, times(y, factor)) for x, y in zip(increment, v)]
    for i in range(ROWS // 8):
        span = slice(8 * i, 8 * i + 8)
        line = concentration[span, :]
        for k in range(DEGREE):
            if increment[k] is not None:
                line = line + increment[k] * basis[k][span, :]
        out[span, :] = line


LIMIT = 16 << 20
FIELD = jax.ShapeDtypeStruct((ROWS, BLK), f32)
PACKETS = [jax.ShapeDtypeStruct((GHOST, BLK), f32)] * 4
PIECES = pltpu.VMEM((3, ROWS * BLK, BLK), bf16)
GHOSTS = pltpu.VMEM((4 * GHOST, BLK), f32)


def params():
    return pltpu.CompilerParams(vmem_limit_bytes=LIMIT)


def cost(flops):
    return pl.CostEstimate(flops=flops, bytes_accessed=0, transcendentals=0)


def shards(pairs, concentration, rate, step, values, columns, lengths, send):
    devices = BLK

    def exchange(packets):
        return [lax.ppermute(x, "dom", by) for x, by in zip(packets, pairs)]

    packets = pl.pallas_call(
        first_packets,
        out_shape=PACKETS,
        in_specs=smem() + vmem(),
        out_specs=vmem(4),
        compiler_params=params(),
        name="first_packets",
    )(send, concentration)
    arrived = exchange(packets)
    blocks, table, near = pl.pallas_call(
        setup,
        out_shape=[pltpu.VMEM((ENTRIES, BLK, BLK), f32), pltpu.SMEM((TABLE,), jnp.int32), FIELD],
        in_specs=smem(3) + [pl.BlockSpec(memory_space=pl.ANY)] + vmem(2),
        out_specs=vmem() + smem() + vmem(),
        scratch_shapes=[PIECES, pltpu.SemaphoreType.DMA(())],
        compiler_params=params(),
        cost_estimate=cost(10**10),
        name="setup",
    )(columns, lengths, send, values, concentration, rate)
    blocks = pltpu.with_memory_space_constraint(blocks, pltpu.VMEM)
    table = pltpu.with_memory_space_constraint(table, pltpu.SMEM)
    basis = []
    for k in range(DEGREE):
        field, *packets = pl.pallas_call(
            far_part(1.0 if k == 0 else SCALE),
            out_shape=[FIELD] + PACKETS,
            in_specs=smem() + vmem(6),
            out_specs=vmem(5),
            scratch_shapes=[GHOSTS, PIECES],
            compiler_params=params(),
            name="far_part",
        )(table, blocks, near, *arrived)
        basis.append(field)
        arrived = exchange(packets)
        near = pl.pallas_call(
            near_part,
            out_shape=FIELD,
            in_specs=smem() + vmem(4),
            out_specs=vmem()[0],
            scratch_shapes=[PIECES],
            compiler_params=params(),
            cost_estimate=cost(10**10),
            name="near_part",
        )(table, blocks, field, rate, concentration)
    sums = pl.pallas_call(
        last_part,
        out_shape=jax.ShapeDtypeStruct((devices, BLK), f32),
        in_specs=smem() + vmem(6 + DEGREE),
        out_specs=vmem()[0],
        scratch_shapes=[pltpu.VMEM((ROWS, BLK), f32), GHOSTS, PIECES, pltpu.VMEM((BLK, BLK), f32)],
        compiler_params=params(),
        name="last_part",
    )(table, blocks, near, *arrived, *basis)
    everyone = lax.all_to_all(sums, "dom", split_axis=0, concat_axis=0, tiled=True)
    return pl.pallas_call(
        finish,
        out_shape=FIELD,
        in_specs=smem() + vmem(2 + DEGREE),
        out_specs=vmem()[0],
        compiler_params=params(),
        name="finish",
    )(step, everyone, concentration, *basis)


def solution(mesh):
    pairs = exchanges(mesh.shape["dom"])

    def run(*arrays):
        return shards(pairs, *arrays)

    split = P("dom")
    return jax.shard_map(
        run,
        mesh=mesh,
        in_specs=(split, split, P(), split, split, split, split),
        out_specs=split,
        check_vma=False,
    )
```

time: 416 us -> 149 us (0.36); the launches traced: 408 us -> 148 us
  matrix products: 112 us -> 0 us
  blocking collectives: 83.7 us -> 0 us
  waiting for transfers between devices: 103 us -> 20.9 us
  Pallas kernels: 0 us -> 62.6 us
  other arithmetic: 26.1 us -> 0 us
  local copies, waits for them, and re-layouts: 25.7 us -> 8.93 us
  between operations: 8.55 us -> 0.84 us
  starting transfers between devices: 49.6 us -> 54.6 us
    dot_general x56 -> x0, matrix products: 112 us -> none  [the longest x8 101 us: product(): jnp.einsum('bsij,bsj->bi', block_values, gathered, precision=lax.Precisio...]
    all_to_all x12 -> x0, blocking collectives: 83.7 us -> none  [from_everyone(): return lax.all_to_all(copies, axis, split_axis=0, concat_axis=0, tiled=True)]
    pallas_call x0 -> x16, Pallas kernels: none -> 62.6 us  [the longest x1 20.2 us: shards(): pl.pallas_call(setup, out_shape=[pltpu.VMEM((ENTRIES, BLK, BLK), f32), pl...]
    ppermute x32 -> x28, waiting for transfers between devices: 69 us -> 12.2 us  [exchange(): return [lax.ppermute(x, 'dom', by) for x, by in zip(packets, pairs)]]
    all_to_all x4 -> x1, waiting for transfers between devices: 33.8 us -> 8.68 us  [shards(): lax.all_to_all(sums, 'dom', split_axis=0, concat_axis=0, tiled=True)]
    ppermute x32 -> x28, starting transfers between devices: 31.1 us -> 49 us  [exchange(): return [lax.ppermute(x, 'dom', by) for x, by in zip(packets, pairs)]]
    all_to_all x4 -> x1, starting transfers between devices: 18.5 us -> 5.54 us  [shards(): lax.all_to_all(sums, 'dom', split_axis=0, concat_axis=0, tiled=True)]
    gather x24 -> x0, local copies, waits for them, and re-layouts: 11 us -> none  [the longest x16 5.51 us: product(): gathered = extended[block_columns] * active[:, :, None]]
  transfers between devices with their start and end apart: 36 -> 29, of which waited for: 32 -> 9; matrix products, arithmetic and copies ran while one was open for 2% -> 1% of each run, Pallas kernels for 0% -> 26%
where the time goes in v1:
time: 149 us; the launch traced here: 148 us
  Pallas kernels  62.6 us (42%)
  starting transfers between devices  54.6 us (37%)
  waiting for transfers between devices  20.9 us (14%)
  local copies, waits for them, and re-layouts  8.93 us (6%)
    ppermute x28, starting transfers between devices, exchange(): return [lax.ppermute(x, 'dom', by) for x, by in zip(packets, pairs)]  49 us
    pallas_call x1, Pallas kernels, shards(): pl.pallas_call(setup, out_shape=[pltpu.VMEM((ENTRIES, BLK, BLK), f32), pl...  20.2 us
    pallas_call x6, Pallas kernels, shards(): pl.pallas_call(near_part, out_shape=FIELD, in_specs=smem() + vmem(4), out...  18.8 us
    pallas_call x6, Pallas kernels, shards(): pl.pallas_call(far_part(1.0 if k == 0 else SCALE), out_shape=[FIELD] + PA...  17.7 us
    ppermute x28, waiting for transfers between devices, exchange(): return [lax.ppermute(x, 'dom', by) for x, by in zip(packets, pairs)]  12.2 us
    unnamed x19, local copies, waits for them, and re-layouts  8.93 us
    all_to_all x1, waiting for transfers between devices, shards(): lax.all_to_all(sums, 'dom', split_axis=0, concat_axis=0, tiled=True)  8.68 us
    all_to_all x1, starting transfers between devices, shards(): lax.all_to_all(sums, 'dom', split_axis=0, concat_axis=0, tiled=True)  5.54 us
  transfers between devices with their start and end apart: 29, of which 9 were waited for; matrix products, arithmetic and copies ran while one was open for 1% of the time, Pallas kernels for 26%

profile of v1, /device:TPU:0, one launch (start us, length us, event | category | flops | bytes accessed | tf_op | source)
XLA Modules:
  0.0 147.8 jit_solution(4836434744742198944)
XLA Ops:
  2.0 8.9 %collective-permute-start = (f32[16,128]{1,0:T(8,128)S(1)}, f32[16,128]{1,0:T(8,128)S(1)}, u32[]{:S(2)}, u32[]{:S(2)}) collective-permute-start(f32[16,128]{1,0:T(8,128)S(1)} %get-tuple-element.45), channel_id=1, source_target_pairs={{2,4},{3,5},{6,8},{7,9},{10,12},{11,13},{14,16},{15,17},{18,20},{1... | collective-permute-start | bytes 24584 | tf_op jit(solution)/shard_map/ppermute | solution.py:346
  14.3 4.0 %copy-done.5 = f32[32,5,128,128]{3,2,1,0:T(8,128)S(1)} copy-done((f32[32,5,128,128]{3,2,1,0:T(8,128)S(1)}, f32[32,5,128,128]{3,2,1,0:T(8,128)}, u32[]{:S(2)}) %copy-start.5) | copy-done | bytes 10485784
  19.6 20.2 %setup.1 = (f32[160,128,128]{2,1,0:T(8,128)S(1)}, s32[384]{0:T(512)S(4)}, f32[32,128]{1,0:T(8,128)S(1)}) custom-call(s32[32,5]{1,0:T(8,128)S(1)} %copy.9.columns, s32[32]{0:T(128)S(1)} %copy-done.8, s32[1,4,16]{2,1,0:T(4,128)S(1)} %copy-done.4, f32[32,5,128,128]{3,2,1,0:T(8,128)S(1)} %copy-done.5, f32[32,128]{1,0:T(8,128)S(1)} %copy-done.1, ...), custom_call_target="tpu_custom_call" | custom-call | flops 10000000000 | tf_op jit(solution)/shard_map/setup/pallas_call | solution.py:357
  39.9 3.0 %far_part.6 = (f32[32,128]{1,0:T(8,128)S(1)}, f32[16,128]{1,0:T(8,128)S(1)}, f32[16,128]{1,0:T(8,128)S(1)}, f32[16,128]{1,0:T(8,128)S(1)}, f32[16,128]{1,0:T(8,128)S(1)}) custom-call(s32[384]{0:T(512)S(4)} %get-tuple-element.42.table, f32[160,128,128]{2,1,0:T(8,128)S(1)} %get-tuple-element.43.blocks, f32[32,128]{1,0:T(8,128)S(1)} %get-tuple-element.44.near, ...), custom_call_target="tpu_custom_call" | custom-call | tf_op jit(solution)/shard_map/far_part/pallas_call | solution.py:371
  42.9 6.4 %collective-permute-start.4 = (f32[16,128]{1,0:T(8,128)S(1)}, f32[16,128]{1,0:T(8,128)S(1)}, u32[]{:S(2)}, u32[]{:S(2)}) collective-permute-start(f32[16,128]{1,0:T(8,128)S(1)} %get-tuple-element.50), channel_id=1, source_target_pairs={{2,4},{3,5},{6,8},{7,9},{10,12},{11,13},{14,16},{15,17},{18,20},{1... | collective-permute-start | bytes 24584 | tf_op jit(solution)/shard_map/ppermute | solution.py:346
  50.7 3.1 %near_part.6.near = f32[32,128]{1,0:T(8,128)S(1)} custom-call(s32[384]{0:T(512)S(4)} %get-tuple-element.42.table, f32[160,128,128]{2,1,0:T(8,128)S(1)} %get-tuple-element.43.blocks, f32[32,128]{1,0:T(8,128)S(1)} %get-tuple-element.49.field.rest_0_, f32[32,128]{1,0:T(8,128)S(1)} %copy-done.7, f32[32,128]{1,0:T(8,128)S(1)} %copy-done.2), custom_call_target="tpu_custom_call" | custom-call | flops 10000000000 | tf_op jit(solution)/shard_map/near_part/pallas_call | solution.py:382
  53.9 3.9 %collective-permute-done.5.g1 = f32[16,128]{1,0:T(8,128)S(1)} collective-permute-done((f32[16,128]{1,0:T(8,128)S(1)}, f32[16,128]{1,0:T(8,128)S(1)}, u32[]{:S(2)}, u32[]{:S(2)}) %collective-permute-start.5) | collective-permute-done | bytes 8224 | tf_op jit(solution)/shard_map/ppermute | solution.py:346
  57.8 3.0 %far_part.7 = (f32[32,128]{1,0:T(8,128)S(1)}, f32[16,128]{1,0:T(8,128)S(1)}, f32[16,128]{1,0:T(8,128)S(1)}, f32[16,128]{1,0:T(8,128)S(1)}, f32[16,128]{1,0:T(8,128)S(1)}) custom-call(s32[384]{0:T(512)S(4)} %get-tuple-element.42.table, f32[160,128,128]{2,1,0:T(8,128)S(1)} %get-tuple-element.43.blocks, f32[32,128]{1,0:T(8,128)S(1)} %near_part.6.near, ...), custom_call_target="tpu_custom_call" | custom-call | tf_op jit(solution)/shard_map/far_part/pallas_call | solution.py:371
  60.9 3.9 %collective-permute-start.8 = (f32[16,128]{1,0:T(8,128)S(1)}, f32[16,128]{1,0:T(8,128)S(1)}, u32[]{:S(2)}, u32[]{:S(2)}) collective-permute-start(f32[16,128]{1,0:T(8,128)S(1)} %get-tuple-element.55), channel_id=1, source_target_pairs={{2,4},{3,5},{6,8},{7,9},{10,12},{11,13},{14,16},{15,17},{18,20},{1... | collective-permute-start | bytes 24584 | tf_op jit(solution)/shard_map/ppermute | solution.py:346
  64.8 3.4 %collective-permute-start.9 = (f32[16,128]{1,0:T(8,128)S(1)}, f32[16,128]{1,0:T(8,128)S(1)}, u32[]{:S(2)}, u32[]{:S(2)}) collective-permute-start(f32[16,128]{1,0:T(8,128)S(1)} %get-tuple-element.56), channel_id=1, source_target_pairs={{1,2},{3,4},{5,6},{7,8},{9,10},{11,12},{13,14},{15,16},{17,18},{19... | collective-permute-start | bytes 24584 | tf_op jit(solution)/shard_map/ppermute | solution.py:346
  68.2 3.1 %near_part.7.near = f32[32,128]{1,0:T(8,128)S(1)} custom-call(s32[384]{0:T(512)S(4)} %get-tuple-element.42.table, f32[160,128,128]{2,1,0:T(8,128)S(1)} %get-tuple-element.43.blocks, f32[32,128]{1,0:T(8,128)S(1)} %get-tuple-element.54.field.rest_1_, f32[32,128]{1,0:T(8,128)S(1)} %copy-done.7, f32[32,128]{1,0:T(8,128)S(1)} %copy-done.2), custom_call_target="tpu_custom_call" | custom-call | flops 10000000000 | tf_op jit(solution)/shard_map/near_part/pallas_call | solution.py:382
  76.9 3.0 %collective-permute-start.13 = (f32[16,128]{1,0:T(8,128)S(1)}, f32[16,128]{1,0:T(8,128)S(1)}, u32[]{:S(2)}, u32[]{:S(2)}) collective-permute-start(f32[16,128]{1,0:T(8,128)S(1)} %get-tuple-element.61), channel_id=1, source_target_pairs={{1,2},{3,4},{5,6},{7,8},{9,10},{11,12},{13,14},{15,16},{17,18},{19... | collective-permute-start | bytes 24584 | tf_op jit(solution)/shard_map/ppermute | solution.py:346
  81.6 3.1 %near_part.8.near = f32[32,128]{1,0:T(8,128)S(1)} custom-call(s32[384]{0:T(512)S(4)} %get-tuple-element.42.table, f32[160,128,128]{2,1,0:T(8,128)S(1)} %get-tuple-element.43.blocks, f32[32,128]{1,0:T(8,128)S(1)} %get-tuple-element.59.field.rest_2_, f32[32,128]{1,0:T(8,128)S(1)} %copy-done.7, f32[32,128]{1,0:T(8,128)S(1)} %copy-done.2), custom_call_target="tpu_custom_call" | custom-call | flops 10000000000 | tf_op jit(solution)/shard_map/near_part/pallas_call | solution.py:382
  85.5 3.0 %far_part.9 = (f32[32,128]{1,0:T(8,128)S(1)}, f32[16,128]{1,0:T(8,128)S(1)}, f32[16,128]{1,0:T(8,128)S(1)}, f32[16,128]{1,0:T(8,128)S(1)}, f32[16,128]{1,0:T(8,128)S(1)}) custom-call(s32[384]{0:T(512)S(4)} %get-tuple-element.42.table, f32[160,128,128]{2,1,0:T(8,128)S(1)} %get-tuple-element.43.blocks, f32[32,128]{1,0:T(8,128)S(1)} %near_part.8.near, ...), custom_call_target="tpu_custom_call" | custom-call | tf_op jit(solution)/shard_map/far_part/pallas_call | solution.py:371
  88.5 3.3 %collective-permute-start.16 = (f32[16,128]{1,0:T(8,128)S(1)}, f32[16,128]{1,0:T(8,128)S(1)}, u32[]{:S(2)}, u32[]{:S(2)}) collective-permute-start(f32[16,128]{1,0:T(8,128)S(1)} %get-tuple-element.65), channel_id=1, source_target_pairs={{2,4},{3,5},{6,8},{7,9},{10,12},{11,13},{14,16},{15,17},{18,20},{1... | collective-permute-start | bytes 24584 | tf_op jit(solution)/shard_map/ppermute | solution.py:346
  91.8 3.5 %collective-permute-start.17 = (f32[16,128]{1,0:T(8,128)S(1)}, f32[16,128]{1,0:T(8,128)S(1)}, u32[]{:S(2)}, u32[]{:S(2)}) collective-permute-start(f32[16,128]{1,0:T(8,128)S(1)} %get-tuple-element.66), channel_id=1, source_target_pairs={{1,2},{3,4},{5,6},{7,8},{9,10},{11,12},{13,14},{15,16},{17,18},{19... | collective-permute-start | bytes 24584 | tf_op jit(solution)/shard_map/ppermute | solution.py:346
  95.3 3.1 %near_part.9.near = f32[32,128]{1,0:T(8,128)S(1)} custom-call(s32[384]{0:T(512)S(4)} %get-tuple-element.42.table, f32[160,128,128]{2,1,0:T(8,128)S(1)} %get-tuple-element.43.blocks, f32[32,128]{1,0:T(8,128)S(1)} %get-tuple-element.64.field.rest_3_, f32[32,128]{1,0:T(8,128)S(1)} %copy-done.7, f32[32,128]{1,0:T(8,128)S(1)} %copy-done.2), custom_call_target="tpu_custom_call" | custom-call | flops 10000000000 | tf_op jit(solution)/shard_map/near_part/pallas_call | solution.py:382
  105.6 3.5 %collective-permute-start.21 = (f32[16,128]{1,0:T(8,128)S(1)}, f32[16,128]{1,0:T(8,128)S(1)}, u32[]{:S(2)}, u32[]{:S(2)}) collective-permute-start(f32[16,128]{1,0:T(8,128)S(1)} %get-tuple-element.71), channel_id=1, source_target_pairs={{1,2},{3,4},{5,6},{7,8},{9,10},{11,12},{13,14},{15,16},{17,18},{19... | collective-permute-start | bytes 24584 | tf_op jit(solution)/shard_map/ppermute | solution.py:346
  109.1 3.1 %near_part.10.near = f32[32,128]{1,0:T(8,128)S(1)} custom-call(s32[384]{0:T(512)S(4)} %get-tuple-element.42.table, f32[160,128,128]{2,1,0:T(8,128)S(1)} %get-tuple-element.43.blocks, f32[32,128]{1,0:T(8,128)S(1)} %get-tuple-element.69.field.rest_4_, f32[32,128]{1,0:T(8,128)S(1)} %copy-done.7, f32[32,128]{1,0:T(8,128)S(1)} %copy-done.2), custom_call_target="tpu_custom_call" | custom-call | flops 10000000000 | tf_op jit(solution)/shard_map/near_part/pallas_call | solution.py:382
  119.3 3.5 %collective-permute-start.25 = (f32[16,128]{1,0:T(8,128)S(1)}, f32[16,128]{1,0:T(8,128)S(1)}, u32[]{:S(2)}, u32[]{:S(2)}) collective-permute-start(f32[16,128]{1,0:T(8,128)S(1)} %get-tuple-element.76), channel_id=1, source_target_pairs={{1,2},{3,4},{5,6},{7,8},{9,10},{11,12},{13,14},{15,16},{17,18},{19... | collective-permute-start | bytes 24584 | tf_op jit(solution)/shard_map/ppermute | solution.py:346
  122.8 3.1 %near_part.11.near = f32[32,128]{1,0:T(8,128)S(1)} custom-call(s32[384]{0:T(512)S(4)} %get-tuple-element.42.table, f32[160,128,128]{2,1,0:T(8,128)S(1)} %get-tuple-element.43.blocks, f32[32,128]{1,0:T(8,128)S(1)} %get-tuple-element.74.field.rest_5_, f32[32,128]{1,0:T(8,128)S(1)} %copy-done.7, f32[32,128]{1,0:T(8,128)S(1)} %copy-done.2), custom_call_target="tpu_custom_call" | custom-call | flops 10000000000 | tf_op jit(solution)/shard_map/near_part/pallas_call | solution.py:382
  127.8 3.9 %last_part.1 = f32[128,128]{1,0:T(8,128)} custom-call(s32[384]{0:T(512)S(4)} %get-tuple-element.42.table, f32[160,128,128]{2,1,0:T(8,128)S(1)} %get-tuple-element.43.blocks, f32[32,128]{1,0:T(8,128)S(1)} %near_part.11.near, f32[16,128]{1,0:T(8,128)S(1)} %collective-permute-done.24.g0, f32[16,128]{1,0:T(8,128)S(1)} %collective-permute-done.25.g1, ...), custom_call_target="tpu_custom_call" | custom-call | tf_op jit(solution)/shard_map/last_part/pallas_call | solution.py:392
  131.7 5.5 %all-to-all-start = ((f32[128,1,128]{2,1,0:T(1,128)}), f32[128,1,128]{2,1,0:T(1,128)S(1)}, u32[]{:S(2)}, u32[]{:S(2)}) async-start(f32[128,1,128]{2,1,0:T(1,128)} %bitcast.1), calls=%async_computation | async-start | bytes 131072 | tf_op jit(solution)/shard_map/all_to_all | solution.py:401
  137.9 8.7 %all-to-all-done = f32[128,1,128]{2,1,0:T(1,128)S(1)} async-done(((f32[128,1,128]{2,1,0:T(1,128)}), f32[128,1,128]{2,1,0:T(1,128)S(1)}, u32[]{:S(2)}, u32[]{:S(2)}) %all-to-all-start) | async-done | bytes 65568 | tf_op jit(solution)/shard_map/all_to_all | solution.py:401
  (69 shorter events, 33.6 us)
Async XLA Ops:
  2.0 37.9 %collective-permute-start = (f32[16,128]{1,0:T(8,128)S(1)}, f32[16,128]{1,0:T(8,128)S(1)}, u32[]{:S(2)}, u32[]{:S(2)}) collective-permute-start(f32[16,128]{1,0:T(8,128)S(1)} %get-tuple-element.45), channel_id=1, source_target_pairs={{2,4},{3,5},{6,8},{7,9},{10,12},{11,13},{14,16},{15,17},{18,20},{1... | collective-permute-start | bytes 24584 | tf_op jit(solution)/shard_map/ppermute | solution.py:346
  10.9 29.0 %collective-permute-start.1 = (f32[16,128]{1,0:T(8,128)S(1)}, f32[16,128]{1,0:T(8,128)S(1)}, u32[]{:S(2)}, u32[]{:S(2)}) collective-permute-start(f32[16,128]{1,0:T(8,128)S(1)} %get-tuple-element.46), channel_id=1, source_target_pairs={{1,2},{3,4},{5,6},{7,8},{9,10},{11,12},{13,14},{15,16},{17,18},{19... | collective-permute-start | bytes 24584 | tf_op jit(solution)/shard_map/ppermute | solution.py:346
  10.9 29.0 %collective-permute-start.2 = (f32[16,128]{1,0:T(8,128)S(1)}, f32[16,128]{1,0:T(8,128)S(1)}, u32[]{:S(2)}, u32[]{:S(2)}) collective-permute-start(f32[16,128]{1,0:T(8,128)S(1)} %get-tuple-element.47), channel_id=1, source_target_pairs={{0,2},{1,3},{4,6},{5,7},{8,10},{9,11},{12,14},{13,15},{16,18},{17,... | collective-permute-start | bytes 24584 | tf_op jit(solution)/shard_map/ppermute | solution.py:346
  12.1 27.8 %collective-permute-start.3 = (f32[16,128]{1,0:T(8,128)S(1)}, f32[16,128]{1,0:T(8,128)S(1)}, u32[]{:S(2)}, u32[]{:S(2)}) collective-permute-start(f32[16,128]{1,0:T(8,128)S(1)} %get-tuple-element.48), channel_id=1, source_target_pairs={{0,1},{2,3},{4,5},{6,7},{8,9},{10,11},{12,13},{14,15},{16,17},{18,... | collective-permute-start | bytes 24584 | tf_op jit(solution)/shard_map/ppermute | solution.py:346
  42.9 11.0 %collective-permute-start.4 = (f32[16,128]{1,0:T(8,128)S(1)}, f32[16,128]{1,0:T(8,128)S(1)}, u32[]{:S(2)}, u32[]{:S(2)}) collective-permute-start(f32[16,128]{1,0:T(8,128)S(1)} %get-tuple-element.50), channel_id=1, source_target_pairs={{2,4},{3,5},{6,8},{7,9},{10,12},{11,13},{14,16},{15,17},{18,20},{1... | collective-permute-start | bytes 24584 | tf_op jit(solution)/shard_map/ppermute | solution.py:346
  49.3 8.5 %collective-permute-start.5 = (f32[16,128]{1,0:T(8,128)S(1)}, f32[16,128]{1,0:T(8,128)S(1)}, u32[]{:S(2)}, u32[]{:S(2)}) collective-permute-start(f32[16,128]{1,0:T(8,128)S(1)} %get-tuple-element.51), channel_id=1, source_target_pairs={{1,2},{3,4},{5,6},{7,8},{9,10},{11,12},{13,14},{15,16},{17,18},{19... | collective-permute-start | bytes 24584 | tf_op jit(solution)/shard_map/ppermute | solution.py:346
  50.5 7.3 %collective-permute-start.6 = (f32[16,128]{1,0:T(8,128)S(1)}, f32[16,128]{1,0:T(8,128)S(1)}, u32[]{:S(2)}, u32[]{:S(2)}) collective-permute-start(f32[16,128]{1,0:T(8,128)S(1)} %get-tuple-element.52), channel_id=1, source_target_pairs={{0,2},{1,3},{4,6},{5,7},{8,10},{9,11},{12,14},{13,15},{16,18},{17,... | collective-permute-start | bytes 24584 | tf_op jit(solution)/shard_map/ppermute | solution.py:346
  50.7 7.1 %collective-permute-start.7 = (f32[16,128]{1,0:T(8,128)S(1)}, f32[16,128]{1,0:T(8,128)S(1)}, u32[]{:S(2)}, u32[]{:S(2)}) collective-permute-start(f32[16,128]{1,0:T(8,128)S(1)} %get-tuple-element.53), channel_id=1, source_target_pairs={{0,1},{2,3},{4,5},{6,7},{8,9},{10,11},{12,13},{14,15},{16,17},{18,... | collective-permute-start | bytes 24584 | tf_op jit(solution)/shard_map/ppermute | solution.py:346
  60.8 10.6 %collective-permute-start.10 = (f32[16,128]{1,0:T(8,128)S(1)}, f32[16,128]{1,0:T(8,128)S(1)}, u32[]{:S(2)}, u32[]{:S(2)}) collective-permute-start(f32[16,128]{1,0:T(8,128)S(1)} %get-tuple-element.57), channel_id=1, source_target_pairs={{0,2},{1,3},{4,6},{5,7},{8,10},{9,11},{12,14},{13,15},{16,18},{17,... | collective-permute-start | bytes 24584 | tf_op jit(solution)/shard_map/ppermute | solution.py:346
  60.9 10.5 %collective-permute-start.11 = (f32[16,128]{1,0:T(8,128)S(1)}, f32[16,128]{1,0:T(8,128)S(1)}, u32[]{:S(2)}, u32[]{:S(2)}) collective-permute-start(f32[16,128]{1,0:T(8,128)S(1)} %get-tuple-element.58), channel_id=1, source_target_pairs={{0,1},{2,3},{4,5},{6,7},{8,9},{10,11},{12,13},{14,15},{16,17},{18,... | collective-permute-start | bytes 24584 | tf_op jit(solution)/shard_map/ppermute | solution.py:346
  60.9 10.4 %collective-permute-start.8 = (f32[16,128]{1,0:T(8,128)S(1)}, f32[16,128]{1,0:T(8,128)S(1)}, u32[]{:S(2)}, u32[]{:S(2)}) collective-permute-start(f32[16,128]{1,0:T(8,128)S(1)} %get-tuple-element.55), channel_id=1, source_target_pairs={{2,4},{3,5},{6,8},{7,9},{10,12},{11,13},{14,16},{15,17},{18,20},{1... | collective-permute-start | bytes 24584 | tf_op jit(solution)/shard_map/ppermute | solution.py:346
  64.8 8.5 %collective-permute-start.9 = (f32[16,128]{1,0:T(8,128)S(1)}, f32[16,128]{1,0:T(8,128)S(1)}, u32[]{:S(2)}, u32[]{:S(2)}) collective-permute-start(f32[16,128]{1,0:T(8,128)S(1)} %get-tuple-element.56), channel_id=1, source_target_pairs={{1,2},{3,4},{5,6},{7,8},{9,10},{11,12},{13,14},{15,16},{17,18},{19... | collective-permute-start | bytes 24584 | tf_op jit(solution)/shard_map/ppermute | solution.py:346
  76.3 9.2 %collective-permute-start.12 = (f32[16,128]{1,0:T(8,128)S(1)}, f32[16,128]{1,0:T(8,128)S(1)}, u32[]{:S(2)}, u32[]{:S(2)}) collective-permute-start(f32[16,128]{1,0:T(8,128)S(1)} %get-tuple-element.60), channel_id=1, source_target_pairs={{2,4},{3,5},{6,8},{7,9},{10,12},{11,13},{14,16},{15,17},{18,20},{1... | collective-permute-start | bytes 24584 | tf_op jit(solution)/shard_map/ppermute | solution.py:346
  76.9 8.6 %collective-permute-start.13 = (f32[16,128]{1,0:T(8,128)S(1)}, f32[16,128]{1,0:T(8,128)S(1)}, u32[]{:S(2)}, u32[]{:S(2)}) collective-permute-start(f32[16,128]{1,0:T(8,128)S(1)} %get-tuple-element.61), channel_id=1, source_target_pairs={{1,2},{3,4},{5,6},{7,8},{9,10},{11,12},{13,14},{15,16},{17,18},{19... | collective-permute-start | bytes 24584 | tf_op jit(solution)/shard_map/ppermute | solution.py:346
  79.9 5.6 %collective-permute-start.14 = (f32[16,128]{1,0:T(8,128)S(1)}, f32[16,128]{1,0:T(8,128)S(1)}, u32[]{:S(2)}, u32[]{:S(2)}) collective-permute-start(f32[16,128]{1,0:T(8,128)S(1)} %get-tuple-element.62), channel_id=1, source_target_pairs={{0,2},{1,3},{4,6},{5,7},{8,10},{9,11},{12,14},{13,15},{16,18},{17,... | collective-permute-start | bytes 24584 | tf_op jit(solution)/shard_map/ppermute | solution.py:346
  88.5 10.0 %collective-permute-start.16 = (f32[16,128]{1,0:T(8,128)S(1)}, f32[16,128]{1,0:T(8,128)S(1)}, u32[]{:S(2)}, u32[]{:S(2)}) collective-permute-start(f32[16,128]{1,0:T(8,128)S(1)} %get-tuple-element.65), channel_id=1, source_target_pairs={{2,4},{3,5},{6,8},{7,9},{10,12},{11,13},{14,16},{15,17},{18,20},{1... | collective-permute-start | bytes 24584 | tf_op jit(solution)/shard_map/ppermute | solution.py:346
  91.8 8.5 %collective-permute-start.17 = (f32[16,128]{1,0:T(8,128)S(1)}, f32[16,128]{1,0:T(8,128)S(1)}, u32[]{:S(2)}, u32[]{:S(2)}) collective-permute-start(f32[16,128]{1,0:T(8,128)S(1)} %get-tuple-element.66), channel_id=1, source_target_pairs={{1,2},{3,4},{5,6},{7,8},{9,10},{11,12},{13,14},{15,16},{17,18},{19... | collective-permute-start | bytes 24584 | tf_op jit(solution)/shard_map/ppermute | solution.py:346
  95.3 5.0 %collective-permute-start.18 = (f32[16,128]{1,0:T(8,128)S(1)}, f32[16,128]{1,0:T(8,128)S(1)}, u32[]{:S(2)}, u32[]{:S(2)}) collective-permute-start(f32[16,128]{1,0:T(8,128)S(1)} %get-tuple-element.67), channel_id=1, source_target_pairs={{0,2},{1,3},{4,6},{5,7},{8,10},{9,11},{12,14},{13,15},{16,18},{17,... | collective-permute-start | bytes 24584 | tf_op jit(solution)/shard_map/ppermute | solution.py:346
  95.3 5.0 %collective-permute-start.19 = (f32[16,128]{1,0:T(8,128)S(1)}, f32[16,128]{1,0:T(8,128)S(1)}, u32[]{:S(2)}, u32[]{:S(2)}) collective-permute-start(f32[16,128]{1,0:T(8,128)S(1)} %get-tuple-element.68), channel_id=1, source_target_pairs={{0,1},{2,3},{4,5},{6,7},{8,9},{10,11},{12,13},{14,15},{16,17},{18,... | collective-permute-start | bytes 24584 | tf_op jit(solution)/shard_map/ppermute | solution.py:346
  103.3 9.2 %collective-permute-start.20 = (f32[16,128]{1,0:T(8,128)S(1)}, f32[16,128]{1,0:T(8,128)S(1)}, u32[]{:S(2)}, u32[]{:S(2)}) collective-permute-start(f32[16,128]{1,0:T(8,128)S(1)} %get-tuple-element.70), channel_id=1, source_target_pairs={{2,4},{3,5},{6,8},{7,9},{10,12},{11,13},{14,16},{15,17},{18,20},{1... | collective-permute-start | bytes 24584 | tf_op jit(solution)/shard_map/ppermute | solution.py:346
  105.6 8.5 %collective-permute-start.21 = (f32[16,128]{1,0:T(8,128)S(1)}, f32[16,128]{1,0:T(8,128)S(1)}, u32[]{:S(2)}, u32[]{:S(2)}) collective-permute-start(f32[16,128]{1,0:T(8,128)S(1)} %get-tuple-element.71), channel_id=1, source_target_pairs={{1,2},{3,4},{5,6},{7,8},{9,10},{11,12},{13,14},{15,16},{17,18},{19... | collective-permute-start | bytes 24584 | tf_op jit(solution)/shard_map/ppermute | solution.py:346
  117.0 9.2 %collective-permute-start.24 = (f32[16,128]{1,0:T(8,128)S(1)}, f32[16,128]{1,0:T(8,128)S(1)}, u32[]{:S(2)}, u32[]{:S(2)}) collective-permute-start(f32[16,128]{1,0:T(8,128)S(1)} %get-tuple-element.75), channel_id=1, source_target_pairs={{2,4},{3,5},{6,8},{7,9},{10,12},{11,13},{14,16},{15,17},{18,20},{1... | collective-permute-start | bytes 24584 | tf_op jit(solution)/shard_map/ppermute | solution.py:346
  119.3 8.5 %collective-permute-start.25 = (f32[16,128]{1,0:T(8,128)S(1)}, f32[16,128]{1,0:T(8,128)S(1)}, u32[]{:S(2)}, u32[]{:S(2)}) collective-permute-start(f32[16,128]{1,0:T(8,128)S(1)} %get-tuple-element.76), channel_id=1, source_target_pairs={{1,2},{3,4},{5,6},{7,8},{9,10},{11,12},{13,14},{15,16},{17,18},{19... | collective-permute-start | bytes 24584 | tf_op jit(solution)/shard_map/ppermute | solution.py:346
  131.7 14.9 %all-to-all-start = ((f32[128,1,128]{2,1,0:T(1,128)}), f32[128,1,128]{2,1,0:T(1,128)S(1)}, u32[]{:S(2)}, u32[]{:S(2)}) async-start(f32[128,1,128]{2,1,0:T(1,128)} %bitcast.1), calls=%async_computation | async-start | bytes 131072 | tf_op jit(solution)/shard_map/all_to_all | solution.py:401
  (14 other events, 53.8 us)

commit v2 on v1

--- a/solution.py
+++ b/solution.py
@@ -17,10 +17,15 @@
 
 FIRST = 0
 LAST = 32
-REMOTE = 64
-COLUMN = 128
-SEND = 288
-TABLE = 384
+LOCAL = 64
+GROUP = 32
+LIST = 128 + GROUP
+FAR = 224
+MID = FAR + 3 * LIST
+SEND = MID + 3 * LIST
+COUNTS = SEND + 64
+TABLE = 1280
+CHUNKS = 8
 
 f32 = jnp.float32
 bf16 = jnp.bfloat16
@@ -60,59 +65,62 @@
             packets[t][g : g + 1, :] = field[pl.ds(row_of(t, g), 1), :]
 
 
-def first_packets(send, field, *packets):
+def first_packets(send, concentration, rate, field, speed, table, p0, p1, p2, p3, done):
+    copies = [
+        pltpu.make_async_copy(send, table, done.at[0]),
+        pltpu.make_async_copy(concentration, field, done.at[1]),
+        pltpu.make_async_copy(rate, speed, done.at[2]),
+    ]
+    for copy in copies:
+        copy.start()
     by = roles()
-    write_packets(field, lambda t, g: send[0, by[t], g], packets)
-
-
-def partial_products(table, begin, end, place, blocks, field, pieces):
+    for copy in copies:
+        copy.wait()
+    write_packets(field, lambda t, g: table[0, by[t], g], (p0, p1, p2, p3))
+
+
+def split(x):
+    high = x.astype(bf16)
+    return high, (x - high.astype(f32)).astype(bf16)
+
+
+def local_rows(table, blocks, field, pieces, begin, end):
     def row(b, carry):
         def entry(e, total):
-            at = place(e)
-            return total + blocks[at] * field[pl.ds(table[COLUMN + at], 1), :]
-
-        total = lax.fori_loop(begin(b), end(b), entry, jnp.zeros((BLK, BLK), f32))
+            word = table[LOCAL + e]
+            return total + blocks[word >> 6] * field[pl.ds(word & 63, 1), :]
+
+        total = lax.fori_loop(table[FIRST + b], table[LAST + b], entry, jnp.zeros((BLK, BLK), f32))
         span = pl.ds(pl.multiple_of(b * BLK, BLK), BLK)
-        high = total.astype(bf16)
-        rest = total - high.astype(f32)
-        middle = rest.astype(bf16)
-        pieces[0, span, :] = high
-        pieces[1, span, :] = middle
-        pieces[2, span, :] = (rest - middle.astype(f32)).astype(bf16)
+        high, low = split(total)
+        pieces[span, 0:BLK] = high
+        pieces[span, BLK : 2 * BLK] = low
         return carry
 
-    lax.fori_loop(0, ROWS, row, 0)
+    lax.fori_loop(begin, end, row, 0)
 
 
 def column_sums(pieces, out):
-    ones = jnp.ones((8, BLK), bf16)
-    for b in range(ROWS):
-        total = sum(
-            lax.dot_general(
-                ones,
-                pieces[k, b * BLK : (b + 1) * BLK, :],
-                (((1,), (1,)), ((), ())),
-                preferred_element_type=f32,
-            )
-            for k in range(3)
+    ones = jnp.ones((8, 2 * BLK), bf16)
+    for b in range(0, ROWS, 2):
+        total = lax.dot_general(
+            ones,
+            pieces[b * BLK : (b + 2) * BLK, :],
+            (((1,), (1,)), ((), ())),
+            preferred_element_type=f32,
         )
-        out[b : b + 1, :] = total[0:1]
-
-
-def local_product(table, blocks, field, pieces, out):
-    partial_products(
-        table,
-        lambda b: table[FIRST + b],
-        lambda b: table[LAST + b],
-        lambda e: e,
-        blocks,
-        field,
-        pieces,
-    )
-    column_sums(pieces, out)
-
-
-def setup(columns, lengths, send, values, field, rate, blocks, table, out, pieces, done):
+        out[b : b + 1, :] = total[0:1, 0:BLK]
+        out[b + 1 : b + 2, :] = total[0:1, BLK : 2 * BLK]
+
+
+def setup(columns, lengths, send, values, field, rate, blocks, turned, table, out, where, length_of, pieces, done, small):
+    step = ROWS // CHUNKS
+    copies = [pltpu.make_async_copy(columns, where, small.at[0]), pltpu.make_async_copy(lengths, length_of, small.at[1])]
+    for copy in copies:
+        copy.start()
+    for k in range(CHUNKS):
+        part = pl.ds(k * step * SLOTS, step * SLOTS)
+        pltpu.make_async_copy(values.at[part], blocks.at[part], done.at[k]).start()
     by = roles()
     place = lax.axis_index("dom")
     even = (place % 2) == 0
@@ -123,74 +131,137 @@
         jnp.where(even, 1, 3),
         jnp.where(low, 0, 2),
     )
+    for t in range(4):
+        for g in range(GHOST):
+            table[SEND + t * GHOST + g] = send[0, by[t], g]
+    for copy in copies:
+        copy.wait()
 
     def row(b, carry):
-        near, far = carry
-        length = lengths[b]
+        near, far, mid = carry
+        length = length_of[b]
         table[FIRST + b] = near
-        table[REMOTE + b] = far
-        last = near
         for s in range(SLOTS):
-            column = columns[b, s]
+            column = where[s, b]
             live = s < length
             ghost = jnp.logical_and(live, column >= ROWS)
             index = jnp.maximum(column - ROWS, 0)
             q = index // GHOST
             spot = jnp.where(q < 2, jnp.where(q == 0, at[0], at[1]), jnp.where(q == 2, at[2], at[3]))
-            target = jnp.where(ghost, ENTRIES - 1 - far, near)
-            table[COLUMN + target] = jnp.where(ghost, spot * GHOST + index % GHOST, column)
-            pltpu.make_async_copy(values.at[b, s], blocks.at[target], done).start()
-            one = ghost.astype(jnp.int32)
-            far = far + one
-            near = near + 1 - one
-            last = jnp.where(live, near, last)
-        table[LAST + b] = last
-        return near, far
-
-    _, far = lax.fori_loop(0, ROWS, row, (jnp.int32(0), jnp.int32(0)))
-    table[REMOTE + ROWS] = far
-    for t in range(4):
-        for g in range(GHOST):
-            table[SEND + t * GHOST + g] = send[0, by[t], g]
-    pltpu.make_async_copy(blocks, blocks, done).wait()
-    local_product(table, blocks, field, pieces, out)
+            first = jnp.logical_and(ghost, spot < 2)
+            second = jnp.logical_and(ghost, spot >= 2)
+            home = jnp.logical_and(live, column < ROWS)
+            slot = b * SLOTS + s
+
+            @pl.when(home)
+            def _(near=near):
+                table[LOCAL + near] = slot * 64 + column
+
+            @pl.when(ghost)
+            def _(far=far, mid=mid):
+                base = jnp.where(first, FAR + far, MID + mid)
+                table[base] = (spot % 2) * GHOST + index % GHOST
+                table[base + LIST] = slot
+                table[base + 2 * LIST] = b
+
+            near = near + home.astype(jnp.int32)
+            far = far + first.astype(jnp.int32)
+            mid = mid + second.astype(jnp.int32)
+        table[LAST + b] = near
+        return near, far, mid
+
+    zero = jnp.int32(0)
+    _, far, mid = lax.fori_loop(0, ROWS, row, (zero, zero, zero))
+    table[COUNTS] = far
+    table[COUNTS + 1] = mid
+    for base, count in ((FAR, far), (MID, mid)):
+
+        def fill(i, carry, base=base, count=count):
+            table[base + count + i] = 2 * GHOST
+            table[base + LIST + count + i] = table[base + LIST]
+            table[base + 2 * LIST + count + i] = 0
+            return carry
+
+        lax.fori_loop(0, GROUP, fill, 0)
+    for k in range(CHUNKS):
+        part = pl.ds(k * step * SLOTS, step * SLOTS)
+        pltpu.make_async_copy(values.at[part], blocks.at[part], done.at[k]).wait()
+        local_rows(table, blocks, field, pieces, k * step, (k + 1) * step)
+    column_sums(pieces, out)
     out[...] = rate[...] * field[...] * (1.0 - field[...]) - out[...]
+    for base, count, start, sign in ((FAR, far, 0, 1), (MID, mid, 127, -1)):
+
+        def turn(c, carry, base=base, count=count, start=start, sign=sign):
+            for u in range(4):
+                i = c * 4 + u
+                slot = table[base + LIST + i]
+                to = jnp.where(i < count, i, 0)
+                high, rest = split(jnp.transpose(blocks[slot]))
+                turned[start + sign * to, :, 0:BLK] = high
+                turned[start + sign * to, :, BLK : 2 * BLK] = rest
+            return carry
+
+        lax.fori_loop(0, (count + 3) // 4, turn, 0)
+
+        def rename(i, carry, base=base, count=count, start=start, sign=sign):
+            table[base + LIST + i] = start + sign * jnp.where(i < count, i, 0)
+            return carry
+
+        lax.fori_loop(0, count + GROUP, rename, 0)
 
 
 def near_part(table, blocks, field, rate, concentration, out, pieces):
-    local_product(table, blocks, field, pieces, out)
+    local_rows(table, blocks, field, pieces, 0, ROWS)
+    column_sums(pieces, out)
     slope = rate[...] * (1.0 - 2.0 * concentration[...]) + SHIFT
     out[...] = slope * field[...] - out[...]
 
 
-def ghost_product(table, blocks, near, arrived, out, ghosts, pieces, scale):
-    for t in range(4):
-        ghosts[t * GHOST : (t + 1) * GHOST, :] = arrived[t][...]
-    partial_products(
-        table,
-        lambda b: table[REMOTE + b],
-        lambda b: table[REMOTE + b + 1],
-        lambda e: ENTRIES - 1 - e,
-        blocks,
-        ghosts,
-        pieces,
-    )
-    column_sums(pieces, out)
-    out[...] = (near[...] - out[...]) * scale
+def ghost_product(table, base, count, turned, arrived, ghosts, stage, sums):
+    ghosts[0:GHOST, :] = arrived[0][...]
+    ghosts[GHOST : 2 * GHOST, :] = arrived[1][...]
+    ghosts[2 * GHOST : 2 * GHOST + 8, :] = jnp.zeros((8, BLK), f32)
+    for ref in sums:
+        ref[...] = jnp.zeros((ROWS, BLK), f32)
+
+    def group(c, carry):
+        first = base + c * GROUP
+        for u in range(GROUP):
+            stage[u : u + 1, :] = ghosts[pl.ds(table[first + u], 1), :]
+        for v in range(0, GROUP, 8):
+            left = jnp.concatenate(split(stage[v : v + 8, :]), axis=0)
+            for u in range(v, v + 8):
+                got = jnp.dot(left, turned[table[first + LIST + u]], preferred_element_type=f32)
+                both = got[:, 0:BLK] + got[:, BLK : 2 * BLK]
+                line = both[0:8] + both[8:16]
+                to = pl.ds(table[first + 2 * LIST + u], 1)
+                ref = sums[u % 4]
+                ref[to, :] = ref[to, :] + line[u - v : u - v + 1, :]
+        return carry
+
+    lax.fori_loop(0, (count + GROUP - 1) // GROUP, group, 0)
+    return (sums[0][...] + sums[1][...]) + (sums[2][...] + sums[3][...])
+
+
+def middle_part(table, turned, near, g2, g3, out, ghosts, stage, *sums):
+    total = ghost_product(table, MID, table[COUNTS + 1], turned, (g2, g3), ghosts, stage, sums)
+    out[...] = near[...] - total
 
 
 def far_part(scale):
-    def kernel(table, blocks, near, g0, g1, g2, g3, out, p0, p1, p2, p3, ghosts, pieces):
-        ghost_product(table, blocks, near, (g0, g1, g2, g3), out, ghosts, pieces, scale)
+    def kernel(table, turned, near, g0, g1, out, p0, p1, p2, p3, ghosts, stage, *sums):
+        total = ghost_product(table, FAR, table[COUNTS], turned, (g0, g1), ghosts, stage, sums)
+        out[...] = (near[...] - total) * scale
         write_packets(out, lambda t, g: table[SEND + t * GHOST + g], (p0, p1, p2, p3))
 
     return kernel
 
 
-def last_part(table, blocks, near, g0, g1, g2, g3, *rest):
+def last_part(table, turned, near, g0, g1, *rest):
     basis = rest[:DEGREE]
-    sums, out, ghosts, pieces, rows = rest[DEGREE:]
-    ghost_product(table, blocks, near, (g0, g1, g2, g3), out, ghosts, pieces, SCALE)
+    sums, out, rows, ghosts, stage, *partial = rest[DEGREE:]
+    total = ghost_product(table, FAR, table[COUNTS], turned, (g0, g1), ghosts, stage, partial)
+    out[...] = (near[...] - total) * SCALE
     basis = basis + (out,)
     rows[...] = jnp.zeros((BLK, BLK), f32)
     for k, (a, b) in enumerate(PAIRS):
@@ -277,7 +348,7 @@
         column = apply(reduced, column)
         column[0] = add(column[0], 1.0 / 64.0)
         column = [None if x is None else x * inverse for x in column]
-    for turn in range(6):
+    for _ in range(6):
         moved = apply(block, column)
         column = [add(x, y) for x, y in zip(moved, column)]
         block = matmul(block, block)
@@ -327,8 +398,11 @@
 LIMIT = 16 << 20
 FIELD = jax.ShapeDtypeStruct((ROWS, BLK), f32)
 PACKETS = [jax.ShapeDtypeStruct((GHOST, BLK), f32)] * 4
-PIECES = pltpu.VMEM((3, ROWS * BLK, BLK), bf16)
-GHOSTS = pltpu.VMEM((4 * GHOST, BLK), f32)
+PIECES = pltpu.VMEM((ROWS * BLK, 2 * BLK), bf16)
+PARTIAL = [
+    pltpu.VMEM((2 * GHOST + 8, BLK), f32),
+    pltpu.VMEM((GROUP, BLK), f32),
+] + [pltpu.VMEM((ROWS, BLK), f32)] * 4
 
 
 def params():
@@ -339,44 +413,83 @@
     return pl.CostEstimate(flops=flops, bytes_accessed=0, transcendentals=0)
 
 
+def hbm(n=1):
+    return [pl.BlockSpec(memory_space=pltpu.HBM)] * n
+
+
 def shards(pairs, concentration, rate, step, values, columns, lengths, send):
     devices = BLK
 
     def exchange(packets):
-        return [lax.ppermute(x, "dom", by) for x, by in zip(packets, pairs)]
-
-    packets = pl.pallas_call(
+        arrived = []
+        for t in range(4):
+            arrived.append(lax.ppermute(packets[t], "dom", pairs[t]))
+        return arrived
+
+    send, concentration, rate, values, columns, lengths = (
+        pltpu.with_memory_space_constraint(x, pltpu.HBM)
+        for x in (send, concentration, rate, values.reshape(ENTRIES, BLK, BLK), columns.T, lengths)
+    )
+    concentration, rate, send, *packets = pl.pallas_call(
         first_packets,
-        out_shape=PACKETS,
-        in_specs=smem() + vmem(),
-        out_specs=vmem(4),
+        out_shape=[FIELD, FIELD, pltpu.SMEM((1, 4, GHOST), jnp.int32)] + PACKETS,
+        in_specs=hbm(3),
+        out_specs=vmem(2) + smem() + vmem(4),
+        scratch_shapes=[pltpu.SemaphoreType.DMA((3,))],
         compiler_params=params(),
         name="first_packets",
-    )(send, concentration)
+    )(send, concentration, rate)
     arrived = exchange(packets)
-    blocks, table, near = pl.pallas_call(
+    send = pltpu.with_memory_space_constraint(send, pltpu.SMEM)
+    blocks, turned, table, near = pl.pallas_call(
         setup,
-        out_shape=[pltpu.VMEM((ENTRIES, BLK, BLK), f32), pltpu.SMEM((TABLE,), jnp.int32), FIELD],
-        in_specs=smem(3) + [pl.BlockSpec(memory_space=pl.ANY)] + vmem(2),
-        out_specs=vmem() + smem() + vmem(),
-        scratch_shapes=[PIECES, pltpu.SemaphoreType.DMA(())],
+        out_shape=[
+            pltpu.VMEM((ENTRIES, BLK, BLK), f32),
+            pltpu.VMEM((BLK, BLK, 2 * BLK), bf16),
+            pltpu.SMEM((TABLE,), jnp.int32),
+            FIELD,
+        ],
+        in_specs=hbm(2) + smem() + hbm() + vmem(2),
+        out_specs=vmem(2) + smem() + vmem(),
+        scratch_shapes=[
+            pltpu.SMEM((SLOTS, ROWS), jnp.int32),
+            pltpu.SMEM((ROWS,), jnp.int32),
+            PIECES,
+            pltpu.SemaphoreType.DMA((CHUNKS,)),
+            pltpu.SemaphoreType.DMA((2,)),
+        ],
         compiler_params=params(),
         cost_estimate=cost(10**10),
         name="setup",
     )(columns, lengths, send, values, concentration, rate)
     blocks = pltpu.with_memory_space_constraint(blocks, pltpu.VMEM)
+    turned = pltpu.with_memory_space_constraint(turned, pltpu.VMEM)
     table = pltpu.with_memory_space_constraint(table, pltpu.SMEM)
     basis = []
+
+    def middle_call(near, arrived):
+        return pl.pallas_call(
+            middle_part,
+            out_shape=FIELD,
+            in_specs=smem() + vmem(4),
+            out_specs=vmem()[0],
+            scratch_shapes=PARTIAL,
+            compiler_params=params(),
+            cost_estimate=cost(10**9),
+            name="middle_part",
+        )(table, turned, near, *arrived[2:])
+
+    near = middle_call(near, arrived)
     for k in range(DEGREE):
         field, *packets = pl.pallas_call(
             far_part(1.0 if k == 0 else SCALE),
             out_shape=[FIELD] + PACKETS,
-            in_specs=smem() + vmem(6),
+            in_specs=smem() + vmem(4),
             out_specs=vmem(5),
-            scratch_shapes=[GHOSTS, PIECES],
+            scratch_shapes=PARTIAL,
             compiler_params=params(),
             name="far_part",
-        )(table, blocks, near, *arrived)
+        )(table, turned, near, *arrived[:2])
         basis.append(field)
         arrived = exchange(packets)
         near = pl.pallas_call(
@@ -389,15 +502,16 @@
             cost_estimate=cost(10**10),
             name="near_part",
         )(table, blocks, field, rate, concentration)
+        near = middle_call(near, arrived)
     sums = pl.pallas_call(
         last_part,
         out_shape=jax.ShapeDtypeStruct((devices, BLK), f32),
-        in_specs=smem() + vmem(6 + DEGREE),
+        in_specs=smem() + vmem(4 + DEGREE),
         out_specs=vmem()[0],
-        scratch_shapes=[pltpu.VMEM((ROWS, BLK), f32), GHOSTS, PIECES, pltpu.VMEM((BLK, BLK), f32)],
+        scratch_shapes=[pltpu.VMEM((ROWS, BLK), f32), pltpu.VMEM((BLK, BLK), f32)] + PARTIAL,
         compiler_params=params(),
         name="last_part",
-    )(table, blocks, near, *arrived, *basis)
+    )(table, turned, near, *arrived[:2], *basis)
     everyone = lax.all_to_all(sums, "dom", split_axis=0, concat_axis=0, tiled=True)
     return pl.pallas_call(
         finish,

time: 149 us -> 130 us (0.87)
  Pallas kernels: 62.6 us -> 30.2 us
  waiting for transfers between devices: 20.9 us -> 34.4 us
  starting transfers between devices: 54.6 us -> 64.3 us
  local copies, waits for them, and re-layouts: 8.93 us -> 0 us
    pallas_call x6, Pallas kernels: 17.7 us -> 2.78 us  [shards(): pl.pallas_call(far_part(1.0 if k == 0 else SCALE), out_shape=[FIELD] + PA...]
    ppermute x28, waiting for transfers between devices: 12.2 us -> 25.7 us  [exchange(): arrived.append(lax.ppermute(packets[t], 'dom', pairs[t]))]
    pallas_call x1, Pallas kernels: 20.2 us -> 8.83 us  [shards(): pl.pallas_call(setup, out_shape=[pltpu.VMEM((ENTRIES, BLK, BLK), f32), pl...]
    unnamed x19 -> x0, local copies, waits for them, and re-layouts: 8.93 us -> none
    ppermute x28, starting transfers between devices: 49 us -> 57.2 us  [exchange(): arrived.append(lax.ppermute(packets[t], 'dom', pairs[t]))]
    pallas_call x6, Pallas kernels: 18.8 us -> 12.3 us  [shards(): pl.pallas_call(near_part, out_shape=FIELD, in_specs=smem() + vmem(4), out...]
    pallas_call x1 -> x8, Pallas kernels: 0.63 us -> 3.73 us  [the longest x7 2.92 us: middle_call(): pl.pallas_call(middle_part, out_shape=FIELD, in_specs=smem() + vmem(4), o...]
    pallas_call x1, Pallas kernels: 3.91 us -> 1.3 us  [shards(): pl.pallas_call(last_part, out_shape=jax.ShapeDtypeStruct((devices, BLK),...]
  transfers between devices with their start and end apart: 29 -> 29, of which waited for: 9 -> 12; matrix products, arithmetic and copies ran while one was open for 1% -> 0% of each run, Pallas kernels for 26% -> 19%
where the time goes in v2:
time: 130 us
  starting transfers between devices  64.3 us (49%)
  waiting for transfers between devices  34.4 us (26%)
  Pallas kernels  30.2 us (23%)
    ppermute x28, starting transfers between devices, exchange(): arrived.append(lax.ppermute(packets[t], 'dom', pairs[t]))  57.2 us
    ppermute x28, waiting for transfers between devices, exchange(): arrived.append(lax.ppermute(packets[t], 'dom', pairs[t]))  25.7 us
    pallas_call x6, Pallas kernels, shards(): pl.pallas_call(near_part, out_shape=FIELD, in_specs=smem() + vmem(4), out...  12.3 us
    pallas_call x1, Pallas kernels, shards(): pl.pallas_call(setup, out_shape=[pltpu.VMEM((ENTRIES, BLK, BLK), f32), pl...  8.83 us
    all_to_all x1, waiting for transfers between devices, shards(): lax.all_to_all(sums, 'dom', split_axis=0, concat_axis=0, tiled=True)  8.67 us
    all_to_all x1, starting transfers between devices, shards(): lax.all_to_all(sums, 'dom', split_axis=0, concat_axis=0, tiled=True)  7.09 us
    pallas_call x7, Pallas kernels, middle_call(): pl.pallas_call(middle_part, out_shape=FIELD, in_specs=smem() + vmem(4), o...  2.92 us
    pallas_call x6, Pallas kernels, shards(): pl.pallas_call(far_part(1.0 if k == 0 else SCALE), out_shape=[FIELD] + PA...  2.78 us
  transfers between devices with their start and end apart: 29, of which 12 were waited for; matrix products, arithmetic and copies ran while one was open for 0% of the time, Pallas kernels for 19%

profile of v2, /device:TPU:0, one launch (start us, length us, event | category | flops | bytes accessed | tf_op | source)
XLA Modules:
  0.0 129.7 jit_solution(16222260097892695914)
XLA Ops:
  2.5 8.0 %collective-permute-start.2 = (f32[16,128]{1,0:T(8,128)S(1)}, f32[16,128]{1,0:T(8,128)S(1)}, u32[]{:S(2)}, u32[]{:S(2)}) collective-permute-start(f32[16,128]{1,0:T(8,128)S(1)} %get-tuple-element.55), channel_id=1, source_target_pairs={{2,4},{3,5},{6,8},{7,9},{10,12},{11,13},{14,16},{15,17},{18,20},{1... | collective-permute-start | bytes 24584 | tf_op jit(solution)/shard_map/ppermute | solution.py:426
  10.6 8.8 %setup.1 = (f32[160,128,128]{2,1,0:T(8,128)S(1)}, bf16[128,128,256]{2,1,0:T(8,128)(2,1)S(1)}, s32[1280]{0:T(1024)S(4)}, f32[32,128]{1,0:T(8,128)S(1)}) custom-call(s32[5,32]{1,0:T(8,128)} %bitcast.8, s32[32]{0:T(128)} %lengths.1, s32[1,4,16]{2,1,0:T(4,128)S(4)} %get-tuple-element.46.send, f32[160,128,128]{2,1,0:T(8,128)} %bitcast.7, ...), custom_call_target="tpu_custom_call" | custom-call | flops 10000000000 | tf_op jit(solution)/shard_map/setup/pallas_call | solution.py:444
  20.4 2.0 %collective-permute-start.4 = (f32[16,128]{1,0:T(8,128)S(1)}, f32[16,128]{1,0:T(8,128)S(1)}, u32[]{:S(2)}, u32[]{:S(2)}) collective-permute-start(f32[16,128]{1,0:T(8,128)S(1)} %get-tuple-element.58), channel_id=1, source_target_pairs={{0,2},{1,3},{4,6},{5,7},{8,10},{9,11},{12,14},{13,15},{16,18},{17,... | collective-permute-start | bytes 24584 | tf_op jit(solution)/shard_map/ppermute | solution.py:426
  22.4 5.5 %collective-permute-start.6 = (f32[16,128]{1,0:T(8,128)S(1)}, f32[16,128]{1,0:T(8,128)S(1)}, u32[]{:S(2)}, u32[]{:S(2)}) collective-permute-start(f32[16,128]{1,0:T(8,128)S(1)} %get-tuple-element.60), channel_id=1, source_target_pairs={{2,4},{3,5},{6,8},{7,9},{10,12},{11,13},{14,16},{15,17},{18,20},{1... | collective-permute-start | bytes 24584 | tf_op jit(solution)/shard_map/ppermute | solution.py:426
  28.0 1.8 %collective-permute-start.7 = (f32[16,128]{1,0:T(8,128)S(1)}, f32[16,128]{1,0:T(8,128)S(1)}, u32[]{:S(2)}, u32[]{:S(2)}) collective-permute-start(f32[16,128]{1,0:T(8,128)S(1)} %get-tuple-element.61), channel_id=1, source_target_pairs={{1,2},{3,4},{5,6},{7,8},{9,10},{11,12},{13,14},{15,16},{17,18},{19... | collective-permute-start | bytes 24584 | tf_op jit(solution)/shard_map/ppermute | solution.py:426
  29.7 2.0 %near_part.6.near = f32[32,128]{1,0:T(8,128)S(1)} custom-call(s32[1280]{0:T(1024)S(4)} %get-tuple-element.49.table, f32[160,128,128]{2,1,0:T(8,128)S(1)} %get-tuple-element.51.blocks, f32[32,128]{1,0:T(8,128)S(1)} %get-tuple-element.57.field.rest_0_, f32[32,128]{1,0:T(8,128)S(1)} %get-tuple-element.48.rate, f32[32,128]{1,0:T(8,128)S(1)} %get-tuple-element.47.field.concentration), custom_call_target="tpu_custom_call" | custom-call | flops 10000000000 | tf_op jit(solution)/shard_map/near_part/pallas_call | solution.py:495
  32.2 4.2 %collective-permute-done.7.g1 = f32[16,128]{1,0:T(8,128)S(1)} collective-permute-done((f32[16,128]{1,0:T(8,128)S(1)}, f32[16,128]{1,0:T(8,128)S(1)}, u32[]{:S(2)}, u32[]{:S(2)}) %collective-permute-start.7) | collective-permute-done | bytes 8224 | tf_op jit(solution)/shard_map/ppermute | solution.py:426
  37.1 2.0 %near_part.7.near = f32[32,128]{1,0:T(8,128)S(1)} custom-call(s32[1280]{0:T(1024)S(4)} %get-tuple-element.49.table, f32[160,128,128]{2,1,0:T(8,128)S(1)} %get-tuple-element.51.blocks, f32[32,128]{1,0:T(8,128)S(1)} %get-tuple-element.62.field.rest_1_, f32[32,128]{1,0:T(8,128)S(1)} %get-tuple-element.48.rate, f32[32,128]{1,0:T(8,128)S(1)} %get-tuple-element.47.field.concentration), custom_call_target="tpu_custom_call" | custom-call | flops 10000000000 | tf_op jit(solution)/shard_map/near_part/pallas_call | solution.py:495
  39.2 2.3 %collective-permute-start.10 = (f32[16,128]{1,0:T(8,128)S(1)}, f32[16,128]{1,0:T(8,128)S(1)}, u32[]{:S(2)}, u32[]{:S(2)}) collective-permute-start(f32[16,128]{1,0:T(8,128)S(1)} %get-tuple-element.65), channel_id=1, source_target_pairs={{2,4},{3,5},{6,8},{7,9},{10,12},{11,13},{14,16},{15,17},{18,20},{1... | collective-permute-start | bytes 24584 | tf_op jit(solution)/shard_map/ppermute | solution.py:426
  41.4 5.2 %collective-permute-start.11 = (f32[16,128]{1,0:T(8,128)S(1)}, f32[16,128]{1,0:T(8,128)S(1)}, u32[]{:S(2)}, u32[]{:S(2)}) collective-permute-start(f32[16,128]{1,0:T(8,128)S(1)} %get-tuple-element.66), channel_id=1, source_target_pairs={{1,2},{3,4},{5,6},{7,8},{9,10},{11,12},{13,14},{15,16},{17,18},{19... | collective-permute-start | bytes 24584 | tf_op jit(solution)/shard_map/ppermute | solution.py:426
  50.6 2.0 %near_part.8.near = f32[32,128]{1,0:T(8,128)S(1)} custom-call(s32[1280]{0:T(1024)S(4)} %get-tuple-element.49.table, f32[160,128,128]{2,1,0:T(8,128)S(1)} %get-tuple-element.51.blocks, f32[32,128]{1,0:T(8,128)S(1)} %get-tuple-element.67.field.rest_2_, f32[32,128]{1,0:T(8,128)S(1)} %get-tuple-element.48.rate, f32[32,128]{1,0:T(8,128)S(1)} %get-tuple-element.47.field.concentration), custom_call_target="tpu_custom_call" | custom-call | flops 10000000000 | tf_op jit(solution)/shard_map/near_part/pallas_call | solution.py:495
  52.6 5.6 %collective-permute-start.14 = (f32[16,128]{1,0:T(8,128)S(1)}, f32[16,128]{1,0:T(8,128)S(1)}, u32[]{:S(2)}, u32[]{:S(2)}) collective-permute-start(f32[16,128]{1,0:T(8,128)S(1)} %get-tuple-element.70), channel_id=1, source_target_pairs={{2,4},{3,5},{6,8},{7,9},{10,12},{11,13},{14,16},{15,17},{18,20},{1... | collective-permute-start | bytes 24584 | tf_op jit(solution)/shard_map/ppermute | solution.py:426
  61.7 5.1 %collective-permute-done.15.g1 = f32[16,128]{1,0:T(8,128)S(1)} collective-permute-done((f32[16,128]{1,0:T(8,128)S(1)}, f32[16,128]{1,0:T(8,128)S(1)}, u32[]{:S(2)}, u32[]{:S(2)}) %collective-permute-start.15) | collective-permute-done | bytes 8224 | tf_op jit(solution)/shard_map/ppermute | solution.py:426
  67.5 2.0 %near_part.9.near = f32[32,128]{1,0:T(8,128)S(1)} custom-call(s32[1280]{0:T(1024)S(4)} %get-tuple-element.49.table, f32[160,128,128]{2,1,0:T(8,128)S(1)} %get-tuple-element.51.blocks, f32[32,128]{1,0:T(8,128)S(1)} %get-tuple-element.72.field.rest_3_, f32[32,128]{1,0:T(8,128)S(1)} %get-tuple-element.48.rate, f32[32,128]{1,0:T(8,128)S(1)} %get-tuple-element.47.field.concentration), custom_call_target="tpu_custom_call" | custom-call | flops 10000000000 | tf_op jit(solution)/shard_map/near_part/pallas_call | solution.py:495
  69.5 2.3 %collective-permute-start.18 = (f32[16,128]{1,0:T(8,128)S(1)}, f32[16,128]{1,0:T(8,128)S(1)}, u32[]{:S(2)}, u32[]{:S(2)}) collective-permute-start(f32[16,128]{1,0:T(8,128)S(1)} %get-tuple-element.75), channel_id=1, source_target_pairs={{2,4},{3,5},{6,8},{7,9},{10,12},{11,13},{14,16},{15,17},{18,20},{1... | collective-permute-start | bytes 24584 | tf_op jit(solution)/shard_map/ppermute | solution.py:426
  71.8 5.2 %collective-permute-start.19 = (f32[16,128]{1,0:T(8,128)S(1)}, f32[16,128]{1,0:T(8,128)S(1)}, u32[]{:S(2)}, u32[]{:S(2)}) collective-permute-start(f32[16,128]{1,0:T(8,128)S(1)} %get-tuple-element.76), channel_id=1, source_target_pairs={{1,2},{3,4},{5,6},{7,8},{9,10},{11,12},{13,14},{15,16},{17,18},{19... | collective-permute-start | bytes 24584 | tf_op jit(solution)/shard_map/ppermute | solution.py:426
  81.1 2.0 %near_part.10.near = f32[32,128]{1,0:T(8,128)S(1)} custom-call(s32[1280]{0:T(1024)S(4)} %get-tuple-element.49.table, f32[160,128,128]{2,1,0:T(8,128)S(1)} %get-tuple-element.51.blocks, f32[32,128]{1,0:T(8,128)S(1)} %get-tuple-element.77.field.rest_4_, f32[32,128]{1,0:T(8,128)S(1)} %get-tuple-element.48.rate, f32[32,128]{1,0:T(8,128)S(1)} %get-tuple-element.47.field.concentration), custom_call_target="tpu_custom_call" | custom-call | flops 10000000000 | tf_op jit(solution)/shard_map/near_part/pallas_call | solution.py:495
  83.1 5.6 %collective-permute-start.22 = (f32[16,128]{1,0:T(8,128)S(1)}, f32[16,128]{1,0:T(8,128)S(1)}, u32[]{:S(2)}, u32[]{:S(2)}) collective-permute-start(f32[16,128]{1,0:T(8,128)S(1)} %get-tuple-element.80), channel_id=1, source_target_pairs={{2,4},{3,5},{6,8},{7,9},{10,12},{11,13},{14,16},{15,17},{18,20},{1... | collective-permute-start | bytes 24584 | tf_op jit(solution)/shard_map/ppermute | solution.py:426
  92.2 5.1 %collective-permute-done.23.g1 = f32[16,128]{1,0:T(8,128)S(1)} collective-permute-done((f32[16,128]{1,0:T(8,128)S(1)}, f32[16,128]{1,0:T(8,128)S(1)}, u32[]{:S(2)}, u32[]{:S(2)}) %collective-permute-start.23) | collective-permute-done | bytes 8224 | tf_op jit(solution)/shard_map/ppermute | solution.py:426
  98.0 2.0 %near_part.11.near = f32[32,128]{1,0:T(8,128)S(1)} custom-call(s32[1280]{0:T(1024)S(4)} %get-tuple-element.49.table, f32[160,128,128]{2,1,0:T(8,128)S(1)} %get-tuple-element.51.blocks, f32[32,128]{1,0:T(8,128)S(1)} %get-tuple-element.82.field.rest_5_, f32[32,128]{1,0:T(8,128)S(1)} %get-tuple-element.48.rate, f32[32,128]{1,0:T(8,128)S(1)} %get-tuple-element.47.field.concentration), custom_call_target="tpu_custom_call" | custom-call | flops 10000000000 | tf_op jit(solution)/shard_map/near_part/pallas_call | solution.py:495
  100.0 2.3 %collective-permute-start.26 = (f32[16,128]{1,0:T(8,128)S(1)}, f32[16,128]{1,0:T(8,128)S(1)}, u32[]{:S(2)}, u32[]{:S(2)}) collective-permute-start(f32[16,128]{1,0:T(8,128)S(1)} %get-tuple-element.85), channel_id=1, source_target_pairs={{2,4},{3,5},{6,8},{7,9},{10,12},{11,13},{14,16},{15,17},{18,20},{1... | collective-permute-start | bytes 24584 | tf_op jit(solution)/shard_map/ppermute | solution.py:426
  102.3 5.2 %collective-permute-start.27 = (f32[16,128]{1,0:T(8,128)S(1)}, f32[16,128]{1,0:T(8,128)S(1)}, u32[]{:S(2)}, u32[]{:S(2)}) collective-permute-start(f32[16,128]{1,0:T(8,128)S(1)} %get-tuple-element.86), channel_id=1, source_target_pairs={{1,2},{3,4},{5,6},{7,8},{9,10},{11,12},{13,14},{15,16},{17,18},{19... | collective-permute-start | bytes 24584 | tf_op jit(solution)/shard_map/ppermute | solution.py:426
  112.1 7.1 %all-to-all-start = ((f32[128,1,128]{2,1,0:T(1,128)}), f32[128,1,128]{2,1,0:T(1,128)S(1)}, u32[]{:S(2)}, u32[]{:S(2)}) async-start(f32[128,1,128]{2,1,0:T(1,128)} %bitcast.3), calls=%async_computation | async-start | bytes 131072 | tf_op jit(solution)/shard_map/all_to_all | solution.py:515
  119.8 8.7 %all-to-all-done = f32[128,1,128]{2,1,0:T(1,128)S(1)} async-done(((f32[128,1,128]{2,1,0:T(1,128)}), f32[128,1,128]{2,1,0:T(1,128)S(1)}, u32[]{:S(2)}, u32[]{:S(2)}) %all-to-all-start) | async-done | bytes 65568 | tf_op jit(solution)/shard_map/all_to_all | solution.py:515
  (57 shorter events, 26.8 us)
Async XLA Ops:
  0.8 18.7 %collective-permute-start = (f32[16,128]{1,0:T(8,128)S(1)}, f32[16,128]{1,0:T(8,128)S(1)}, u32[]{:S(2)}, u32[]{:S(2)}) collective-permute-start(f32[16,128]{1,0:T(8,128)S(1)} %get-tuple-element.53), channel_id=1, source_target_pairs={{0,2},{1,3},{4,6},{5,7},{8,10},{9,11},{12,14},{13,15},{16,18},{17,... | collective-permute-start | bytes 24584 | tf_op jit(solution)/shard_map/ppermute | solution.py:426
  2.5 17.0 %collective-permute-start.1 = (f32[16,128]{1,0:T(8,128)S(1)}, f32[16,128]{1,0:T(8,128)S(1)}, u32[]{:S(2)}, u32[]{:S(2)}) collective-permute-start(f32[16,128]{1,0:T(8,128)S(1)} %get-tuple-element.54), channel_id=1, source_target_pairs={{0,1},{2,3},{4,5},{6,7},{8,9},{10,11},{12,13},{14,15},{16,17},{18,... | collective-permute-start | bytes 24584 | tf_op jit(solution)/shard_map/ppermute | solution.py:426
  2.5 17.4 %collective-permute-start.2 = (f32[16,128]{1,0:T(8,128)S(1)}, f32[16,128]{1,0:T(8,128)S(1)}, u32[]{:S(2)}, u32[]{:S(2)}) collective-permute-start(f32[16,128]{1,0:T(8,128)S(1)} %get-tuple-element.55), channel_id=1, source_target_pairs={{2,4},{3,5},{6,8},{7,9},{10,12},{11,13},{14,16},{15,17},{18,20},{1... | collective-permute-start | bytes 24584 | tf_op jit(solution)/shard_map/ppermute | solution.py:426
  10.5 9.4 %collective-permute-start.3 = (f32[16,128]{1,0:T(8,128)S(1)}, f32[16,128]{1,0:T(8,128)S(1)}, u32[]{:S(2)}, u32[]{:S(2)}) collective-permute-start(f32[16,128]{1,0:T(8,128)S(1)} %get-tuple-element.56), channel_id=1, source_target_pairs={{1,2},{3,4},{5,6},{7,8},{9,10},{11,12},{13,14},{15,16},{17,18},{19... | collective-permute-start | bytes 24584 | tf_op jit(solution)/shard_map/ppermute | solution.py:426
  20.4 11.3 %collective-permute-start.4 = (f32[16,128]{1,0:T(8,128)S(1)}, f32[16,128]{1,0:T(8,128)S(1)}, u32[]{:S(2)}, u32[]{:S(2)}) collective-permute-start(f32[16,128]{1,0:T(8,128)S(1)} %get-tuple-element.58), channel_id=1, source_target_pairs={{0,2},{1,3},{4,6},{5,7},{8,10},{9,11},{12,14},{13,15},{16,18},{17,... | collective-permute-start | bytes 24584 | tf_op jit(solution)/shard_map/ppermute | solution.py:426
  22.4 9.3 %collective-permute-start.5 = (f32[16,128]{1,0:T(8,128)S(1)}, f32[16,128]{1,0:T(8,128)S(1)}, u32[]{:S(2)}, u32[]{:S(2)}) collective-permute-start(f32[16,128]{1,0:T(8,128)S(1)} %get-tuple-element.59), channel_id=1, source_target_pairs={{0,1},{2,3},{4,5},{6,7},{8,9},{10,11},{12,13},{14,15},{16,17},{18,... | collective-permute-start | bytes 24584 | tf_op jit(solution)/shard_map/ppermute | solution.py:426
  22.4 9.8 %collective-permute-start.6 = (f32[16,128]{1,0:T(8,128)S(1)}, f32[16,128]{1,0:T(8,128)S(1)}, u32[]{:S(2)}, u32[]{:S(2)}) collective-permute-start(f32[16,128]{1,0:T(8,128)S(1)} %get-tuple-element.60), channel_id=1, source_target_pairs={{2,4},{3,5},{6,8},{7,9},{10,12},{11,13},{14,16},{15,17},{18,20},{1... | collective-permute-start | bytes 24584 | tf_op jit(solution)/shard_map/ppermute | solution.py:426
  36.9 9.6 %collective-permute-start.8 = (f32[16,128]{1,0:T(8,128)S(1)}, f32[16,128]{1,0:T(8,128)S(1)}, u32[]{:S(2)}, u32[]{:S(2)}) collective-permute-start(f32[16,128]{1,0:T(8,128)S(1)} %get-tuple-element.63), channel_id=1, source_target_pairs={{0,2},{1,3},{4,6},{5,7},{8,10},{9,11},{12,14},{13,15},{16,18},{17,... | collective-permute-start | bytes 24584 | tf_op jit(solution)/shard_map/ppermute | solution.py:426
  37.0 9.6 %collective-permute-start.9 = (f32[16,128]{1,0:T(8,128)S(1)}, f32[16,128]{1,0:T(8,128)S(1)}, u32[]{:S(2)}, u32[]{:S(2)}) collective-permute-start(f32[16,128]{1,0:T(8,128)S(1)} %get-tuple-element.64), channel_id=1, source_target_pairs={{0,1},{2,3},{4,5},{6,7},{8,9},{10,11},{12,13},{14,15},{16,17},{18,... | collective-permute-start | bytes 24584 | tf_op jit(solution)/shard_map/ppermute | solution.py:426
  39.2 9.1 %collective-permute-start.10 = (f32[16,128]{1,0:T(8,128)S(1)}, f32[16,128]{1,0:T(8,128)S(1)}, u32[]{:S(2)}, u32[]{:S(2)}) collective-permute-start(f32[16,128]{1,0:T(8,128)S(1)} %get-tuple-element.65), channel_id=1, source_target_pairs={{2,4},{3,5},{6,8},{7,9},{10,12},{11,13},{14,16},{15,17},{18,20},{1... | collective-permute-start | bytes 24584 | tf_op jit(solution)/shard_map/ppermute | solution.py:426
  50.4 9.6 %collective-permute-start.12 = (f32[16,128]{1,0:T(8,128)S(1)}, f32[16,128]{1,0:T(8,128)S(1)}, u32[]{:S(2)}, u32[]{:S(2)}) collective-permute-start(f32[16,128]{1,0:T(8,128)S(1)} %get-tuple-element.68), channel_id=1, source_target_pairs={{0,2},{1,3},{4,6},{5,7},{8,10},{9,11},{12,14},{13,15},{16,18},{17,... | collective-permute-start | bytes 24584 | tf_op jit(solution)/shard_map/ppermute | solution.py:426
  50.5 9.6 %collective-permute-start.13 = (f32[16,128]{1,0:T(8,128)S(1)}, f32[16,128]{1,0:T(8,128)S(1)}, u32[]{:S(2)}, u32[]{:S(2)}) collective-permute-start(f32[16,128]{1,0:T(8,128)S(1)} %get-tuple-element.69), channel_id=1, source_target_pairs={{0,1},{2,3},{4,5},{6,7},{8,9},{10,11},{12,13},{14,15},{16,17},{18,... | collective-permute-start | bytes 24584 | tf_op jit(solution)/shard_map/ppermute | solution.py:426
  52.6 9.1 %collective-permute-start.14 = (f32[16,128]{1,0:T(8,128)S(1)}, f32[16,128]{1,0:T(8,128)S(1)}, u32[]{:S(2)}, u32[]{:S(2)}) collective-permute-start(f32[16,128]{1,0:T(8,128)S(1)} %get-tuple-element.70), channel_id=1, source_target_pairs={{2,4},{3,5},{6,8},{7,9},{10,12},{11,13},{14,16},{15,17},{18,20},{1... | collective-permute-start | bytes 24584 | tf_op jit(solution)/shard_map/ppermute | solution.py:426
  58.3 8.5 %collective-permute-start.15 = (f32[16,128]{1,0:T(8,128)S(1)}, f32[16,128]{1,0:T(8,128)S(1)}, u32[]{:S(2)}, u32[]{:S(2)}) collective-permute-start(f32[16,128]{1,0:T(8,128)S(1)} %get-tuple-element.71), channel_id=1, source_target_pairs={{1,2},{3,4},{5,6},{7,8},{9,10},{11,12},{13,14},{15,16},{17,18},{19... | collective-permute-start | bytes 24584 | tf_op jit(solution)/shard_map/ppermute | solution.py:426
  67.3 9.6 %collective-permute-start.16 = (f32[16,128]{1,0:T(8,128)S(1)}, f32[16,128]{1,0:T(8,128)S(1)}, u32[]{:S(2)}, u32[]{:S(2)}) collective-permute-start(f32[16,128]{1,0:T(8,128)S(1)} %get-tuple-element.73), channel_id=1, source_target_pairs={{0,2},{1,3},{4,6},{5,7},{8,10},{9,11},{12,14},{13,15},{16,18},{17,... | collective-permute-start | bytes 24584 | tf_op jit(solution)/shard_map/ppermute | solution.py:426
  67.4 9.6 %collective-permute-start.17 = (f32[16,128]{1,0:T(8,128)S(1)}, f32[16,128]{1,0:T(8,128)S(1)}, u32[]{:S(2)}, u32[]{:S(2)}) collective-permute-start(f32[16,128]{1,0:T(8,128)S(1)} %get-tuple-element.74), channel_id=1, source_target_pairs={{0,1},{2,3},{4,5},{6,7},{8,9},{10,11},{12,13},{14,15},{16,17},{18,... | collective-permute-start | bytes 24584 | tf_op jit(solution)/shard_map/ppermute | solution.py:426
  69.5 9.1 %collective-permute-start.18 = (f32[16,128]{1,0:T(8,128)S(1)}, f32[16,128]{1,0:T(8,128)S(1)}, u32[]{:S(2)}, u32[]{:S(2)}) collective-permute-start(f32[16,128]{1,0:T(8,128)S(1)} %get-tuple-element.75), channel_id=1, source_target_pairs={{2,4},{3,5},{6,8},{7,9},{10,12},{11,13},{14,16},{15,17},{18,20},{1... | collective-permute-start | bytes 24584 | tf_op jit(solution)/shard_map/ppermute | solution.py:426
  80.7 9.8 %collective-permute-start.20 = (f32[16,128]{1,0:T(8,128)S(1)}, f32[16,128]{1,0:T(8,128)S(1)}, u32[]{:S(2)}, u32[]{:S(2)}) collective-permute-start(f32[16,128]{1,0:T(8,128)S(1)} %get-tuple-element.78), channel_id=1, source_target_pairs={{0,2},{1,3},{4,6},{5,7},{8,10},{9,11},{12,14},{13,15},{16,18},{17,... | collective-permute-start | bytes 24584 | tf_op jit(solution)/shard_map/ppermute | solution.py:426
  80.8 9.7 %collective-permute-start.21 = (f32[16,128]{1,0:T(8,128)S(1)}, f32[16,128]{1,0:T(8,128)S(1)}, u32[]{:S(2)}, u32[]{:S(2)}) collective-permute-start(f32[16,128]{1,0:T(8,128)S(1)} %get-tuple-element.79), channel_id=1, source_target_pairs={{0,1},{2,3},{4,5},{6,7},{8,9},{10,11},{12,13},{14,15},{16,17},{18,... | collective-permute-start | bytes 24584 | tf_op jit(solution)/shard_map/ppermute | solution.py:426
  83.1 9.1 %collective-permute-start.22 = (f32[16,128]{1,0:T(8,128)S(1)}, f32[16,128]{1,0:T(8,128)S(1)}, u32[]{:S(2)}, u32[]{:S(2)}) collective-permute-start(f32[16,128]{1,0:T(8,128)S(1)} %get-tuple-element.80), channel_id=1, source_target_pairs={{2,4},{3,5},{6,8},{7,9},{10,12},{11,13},{14,16},{15,17},{18,20},{1... | collective-permute-start | bytes 24584 | tf_op jit(solution)/shard_map/ppermute | solution.py:426
  97.8 9.6 %collective-permute-start.24 = (f32[16,128]{1,0:T(8,128)S(1)}, f32[16,128]{1,0:T(8,128)S(1)}, u32[]{:S(2)}, u32[]{:S(2)}) collective-permute-start(f32[16,128]{1,0:T(8,128)S(1)} %get-tuple-element.83), channel_id=1, source_target_pairs={{0,2},{1,3},{4,6},{5,7},{8,10},{9,11},{12,14},{13,15},{16,18},{17,... | collective-permute-start | bytes 24584 | tf_op jit(solution)/shard_map/ppermute | solution.py:426
  97.9 9.6 %collective-permute-start.25 = (f32[16,128]{1,0:T(8,128)S(1)}, f32[16,128]{1,0:T(8,128)S(1)}, u32[]{:S(2)}, u32[]{:S(2)}) collective-permute-start(f32[16,128]{1,0:T(8,128)S(1)} %get-tuple-element.84), channel_id=1, source_target_pairs={{0,1},{2,3},{4,5},{6,7},{8,9},{10,11},{12,13},{14,15},{16,17},{18,... | collective-permute-start | bytes 24584 | tf_op jit(solution)/shard_map/ppermute | solution.py:426
  100.0 9.1 %collective-permute-start.26 = (f32[16,128]{1,0:T(8,128)S(1)}, f32[16,128]{1,0:T(8,128)S(1)}, u32[]{:S(2)}, u32[]{:S(2)}) collective-permute-start(f32[16,128]{1,0:T(8,128)S(1)} %get-tuple-element.85), channel_id=1, source_target_pairs={{2,4},{3,5},{6,8},{7,9},{10,12},{11,13},{14,16},{15,17},{18,20},{1... | collective-permute-start | bytes 24584 | tf_op jit(solution)/shard_map/ppermute | solution.py:426
  112.1 16.4 %all-to-all-start = ((f32[128,1,128]{2,1,0:T(1,128)}), f32[128,1,128]{2,1,0:T(1,128)S(1)}, u32[]{:S(2)}, u32[]{:S(2)}) async-start(f32[128,1,128]{2,1,0:T(1,128)} %bitcast.3), calls=%async_computation | async-start | bytes 131072 | tf_op jit(solution)/shard_map/all_to_all | solution.py:515
  (5 other events, 42.5 us)

commit v3 on v2

--- a/solution.py
+++ b/solution.py
@@ -15,17 +15,16 @@
 SCALE = 0.25
 PAIRS = [(a, b) for b in range(DEGREE + 1) for a in range(min(b, DEGREE - 1) + 1)]
 
-FIRST = 0
-LAST = 32
-LOCAL = 64
-GROUP = 32
-LIST = 128 + GROUP
-FAR = 224
-MID = FAR + 3 * LIST
-SEND = MID + 3 * LIST
+LIST = ENTRIES + 40
+GROUPS = (40, 32, 32)
+NEAR = 0
+FAR = 3 * LIST
+MID = 6 * LIST
+REST = 9 * LIST
+SEND = REST + 3 * LIST
 COUNTS = SEND + 64
-TABLE = 1280
-CHUNKS = 8
+TABLE = COUNTS + 8
+ZERO = ROWS
 
 f32 = jnp.float32
 bf16 = jnp.bfloat16
@@ -84,43 +83,17 @@
     return high, (x - high.astype(f32)).astype(bf16)
 
 
-def local_rows(table, blocks, field, pieces, begin, end):
-    def row(b, carry):
-        def entry(e, total):
-            word = table[LOCAL + e]
-            return total + blocks[word >> 6] * field[pl.ds(word & 63, 1), :]
-
-        total = lax.fori_loop(table[FIRST + b], table[LAST + b], entry, jnp.zeros((BLK, BLK), f32))
-        span = pl.ds(pl.multiple_of(b * BLK, BLK), BLK)
-        high, low = split(total)
-        pieces[span, 0:BLK] = high
-        pieces[span, BLK : 2 * BLK] = low
-        return carry
-
-    lax.fori_loop(begin, end, row, 0)
-
-
-def column_sums(pieces, out):
-    ones = jnp.ones((8, 2 * BLK), bf16)
-    for b in range(0, ROWS, 2):
-        total = lax.dot_general(
-            ones,
-            pieces[b * BLK : (b + 2) * BLK, :],
-            (((1,), (1,)), ((), ())),
-            preferred_element_type=f32,
-        )
-        out[b : b + 1, :] = total[0:1, 0:BLK]
-        out[b + 1 : b + 2, :] = total[0:1, BLK : 2 * BLK]
-
-
-def setup(columns, lengths, send, values, field, rate, blocks, turned, table, out, where, length_of, pieces, done, small):
-    step = ROWS // CHUNKS
+def setup(columns, lengths, send, values, field, rate, turned, table, out, where, length_of, blocks, done, small, *scratch):
     copies = [pltpu.make_async_copy(columns, where, small.at[0]), pltpu.make_async_copy(lengths, length_of, small.at[1])]
     for copy in copies:
         copy.start()
-    for k in range(CHUNKS):
-        part = pl.ds(k * step * SLOTS, step * SLOTS)
-        pltpu.make_async_copy(values.at[part], blocks.at[part], done.at[k]).start()
+
+    def fetch(b):
+        part = pl.ds(b * 2 * SLOTS, 2 * SLOTS)
+        return pltpu.make_async_copy(values.at[part], blocks.at[part], done.at[b])
+
+    for b in range(ROWS // 2):
+        fetch(b).start()
     by = roles()
     place = lax.axis_index("dom")
     even = (place % 2) == 0
@@ -137,98 +110,72 @@
     for copy in copies:
         copy.wait()
 
-    def row(b, carry):
+    def rows(pair, carry):
         near, far, mid = carry
-        length = length_of[b]
-        table[FIRST + b] = near
-        for s in range(SLOTS):
-            column = where[s, b]
-            live = s < length
-            ghost = jnp.logical_and(live, column >= ROWS)
-            index = jnp.maximum(column - ROWS, 0)
-            q = index // GHOST
-            spot = jnp.where(q < 2, jnp.where(q == 0, at[0], at[1]), jnp.where(q == 2, at[2], at[3]))
-            first = jnp.logical_and(ghost, spot < 2)
-            second = jnp.logical_and(ghost, spot >= 2)
-            home = jnp.logical_and(live, column < ROWS)
-            slot = b * SLOTS + s
-
-            @pl.when(home)
-            def _(near=near):
-                table[LOCAL + near] = slot * 64 + column
-
-            @pl.when(ghost)
-            def _(far=far, mid=mid):
-                base = jnp.where(first, FAR + far, MID + mid)
-                table[base] = (spot % 2) * GHOST + index % GHOST
-                table[base + LIST] = slot
+        fetch(pair).wait()
+        for half in range(2):
+            b = pair * 2 + half
+            length = length_of[b]
+            for s in range(SLOTS):
+                column = where[s, b]
+                index = jnp.maximum(column - ROWS, 0)
+                q = index >> 4
+                spot = jnp.where(q < 2, jnp.where(q == 0, at[0], at[1]), jnp.where(q == 2, at[2], at[3]))
+                live = s < length
+                ghost = jnp.logical_and(live, column >= ROWS)
+                home = jnp.logical_and(live, column < ROWS)
+                first = jnp.logical_and(ghost, spot < 2)
+                second = jnp.logical_and(ghost, spot >= 2)
+                base = jnp.where(
+                    home, NEAR + near, jnp.where(first, FAR + far, jnp.where(second, MID + mid, REST))
+                )
+                table[base] = jnp.where(ghost, ((spot & 1) << 4) + (index & 15), column)
+                table[base + LIST] = b * SLOTS + s
                 table[base + 2 * LIST] = b
-
-            near = near + home.astype(jnp.int32)
-            far = far + first.astype(jnp.int32)
-            mid = mid + second.astype(jnp.int32)
-        table[LAST + b] = near
+                near = near + home.astype(jnp.int32)
+                far = far + first.astype(jnp.int32)
+                mid = mid + second.astype(jnp.int32)
+        for s in range(2 * SLOTS):
+            slot = pair * 2 * SLOTS + s
+            high, rest = split(jnp.transpose(blocks[slot]))
+            turned[slot, :, 0:BLK] = high
+            turned[slot, :, BLK : 2 * BLK] = rest
         return near, far, mid
 
     zero = jnp.int32(0)
-    _, far, mid = lax.fori_loop(0, ROWS, row, (zero, zero, zero))
-    table[COUNTS] = far
-    table[COUNTS + 1] = mid
-    for base, count in ((FAR, far), (MID, mid)):
-
-        def fill(i, carry, base=base, count=count):
-            table[base + count + i] = 2 * GHOST
-            table[base + LIST + count + i] = table[base + LIST]
-            table[base + 2 * LIST + count + i] = 0
-            return carry
-
-        lax.fori_loop(0, GROUP, fill, 0)
-    for k in range(CHUNKS):
-        part = pl.ds(k * step * SLOTS, step * SLOTS)
-        pltpu.make_async_copy(values.at[part], blocks.at[part], done.at[k]).wait()
-        local_rows(table, blocks, field, pieces, k * step, (k + 1) * step)
-    column_sums(pieces, out)
-    out[...] = rate[...] * field[...] * (1.0 - field[...]) - out[...]
-    for base, count, start, sign in ((FAR, far, 0, 1), (MID, mid, 127, -1)):
-
-        def turn(c, carry, base=base, count=count, start=start, sign=sign):
-            for u in range(4):
-                i = c * 4 + u
-                slot = table[base + LIST + i]
-                to = jnp.where(i < count, i, 0)
-                high, rest = split(jnp.transpose(blocks[slot]))
-                turned[start + sign * to, :, 0:BLK] = high
-                turned[start + sign * to, :, BLK : 2 * BLK] = rest
-            return carry
-
-        lax.fori_loop(0, (count + 3) // 4, turn, 0)
-
-        def rename(i, carry, base=base, count=count, start=start, sign=sign):
-            table[base + LIST + i] = start + sign * jnp.where(i < count, i, 0)
-            return carry
-
-        lax.fori_loop(0, count + GROUP, rename, 0)
-
-
-def near_part(table, blocks, field, rate, concentration, out, pieces):
-    local_rows(table, blocks, field, pieces, 0, ROWS)
-    column_sums(pieces, out)
+    counts = lax.fori_loop(0, ROWS // 2, rows, (zero, zero, zero))
+    for i, base in enumerate((NEAR, FAR, MID)):
+        table[COUNTS + i] = counts[i]
+        for g in range(GROUPS[i]):
+            table[base + counts[i] + g] = ZERO
+            table[base + LIST + counts[i] + g] = 0
+            table[base + 2 * LIST + counts[i] + g] = 0
+    total = product(table, 0, turned, (field,), *scratch)
+    out[...] = rate[...] * field[...] * (1.0 - field[...]) - total
+
+
+def near_part(table, turned, field, rate, concentration, out, *scratch):
+    total = product(table, 0, turned, (field,), *scratch)
     slope = rate[...] * (1.0 - 2.0 * concentration[...]) + SHIFT
-    out[...] = slope * field[...] - out[...]
-
-
-def ghost_product(table, base, count, turned, arrived, ghosts, stage, sums):
-    ghosts[0:GHOST, :] = arrived[0][...]
-    ghosts[GHOST : 2 * GHOST, :] = arrived[1][...]
-    ghosts[2 * GHOST : 2 * GHOST + 8, :] = jnp.zeros((8, BLK), f32)
+    out[...] = slope * field[...] - total
+
+
+def product(table, which, turned, sources, lines, stage, *sums):
+    base = (NEAR, FAR, MID)[which]
+    size = GROUPS[which]
+    count = table[COUNTS + which]
+    height = ROWS // len(sources)
+    for i, source in enumerate(sources):
+        lines[i * height : (i + 1) * height, :] = source[...]
+    lines[ZERO : ZERO + 8, :] = jnp.zeros((8, BLK), f32)
     for ref in sums:
         ref[...] = jnp.zeros((ROWS, BLK), f32)
 
     def group(c, carry):
-        first = base + c * GROUP
-        for u in range(GROUP):
-            stage[u : u + 1, :] = ghosts[pl.ds(table[first + u], 1), :]
-        for v in range(0, GROUP, 8):
+        first = base + c * size
+        for u in range(size):
+            stage[u : u + 1, :] = lines[pl.ds(table[first + u], 1), :]
+        for v in range(0, size, 8):
             left = jnp.concatenate(split(stage[v : v + 8, :]), axis=0)
             for u in range(v, v + 8):
                 got = jnp.dot(left, turned[table[first + LIST + u]], preferred_element_type=f32)
@@ -239,19 +186,17 @@
                 ref[to, :] = ref[to, :] + line[u - v : u - v + 1, :]
         return carry
 
-    lax.fori_loop(0, (count + GROUP - 1) // GROUP, group, 0)
+    lax.fori_loop(0, (count + size - 1) // size, group, 0)
     return (sums[0][...] + sums[1][...]) + (sums[2][...] + sums[3][...])
 
 
-def middle_part(table, turned, near, g2, g3, out, ghosts, stage, *sums):
-    total = ghost_product(table, MID, table[COUNTS + 1], turned, (g2, g3), ghosts, stage, sums)
-    out[...] = near[...] - total
+def middle_part(table, turned, near, g2, g3, out, *scratch):
+    out[...] = near[...] - product(table, 2, turned, (g2, g3), *scratch)
 
 
 def far_part(scale):
-    def kernel(table, turned, near, g0, g1, out, p0, p1, p2, p3, ghosts, stage, *sums):
-        total = ghost_product(table, FAR, table[COUNTS], turned, (g0, g1), ghosts, stage, sums)
-        out[...] = (near[...] - total) * scale
+    def kernel(table, turned, near, g0, g1, out, p0, p1, p2, p3, *scratch):
+        out[...] = (near[...] - product(table, 1, turned, (g0, g1), *scratch)) * scale
         write_packets(out, lambda t, g: table[SEND + t * GHOST + g], (p0, p1, p2, p3))
 
     return kernel
@@ -259,9 +204,8 @@
 
 def last_part(table, turned, near, g0, g1, *rest):
     basis = rest[:DEGREE]
-    sums, out, rows, ghosts, stage, *partial = rest[DEGREE:]
-    total = ghost_product(table, FAR, table[COUNTS], turned, (g0, g1), ghosts, stage, partial)
-    out[...] = (near[...] - total) * SCALE
+    sums, out, rows, *scratch = rest[DEGREE:]
+    out[...] = (near[...] - product(table, 1, turned, (g0, g1), *scratch)) * SCALE
     basis = basis + (out,)
     rows[...] = jnp.zeros((BLK, BLK), f32)
     for k, (a, b) in enumerate(PAIRS):
@@ -395,13 +339,12 @@
         out[span, :] = line
 
 
-LIMIT = 16 << 20
+LIMIT = 24 << 20
 FIELD = jax.ShapeDtypeStruct((ROWS, BLK), f32)
 PACKETS = [jax.ShapeDtypeStruct((GHOST, BLK), f32)] * 4
-PIECES = pltpu.VMEM((ROWS * BLK, 2 * BLK), bf16)
 PARTIAL = [
-    pltpu.VMEM((2 * GHOST + 8, BLK), f32),
-    pltpu.VMEM((GROUP, BLK), f32),
+    pltpu.VMEM((ROWS + 8, BLK), f32),
+    pltpu.VMEM((max(GROUPS), BLK), f32),
 ] + [pltpu.VMEM((ROWS, BLK), f32)] * 4
 
 
@@ -441,28 +384,27 @@
     )(send, concentration, rate)
     arrived = exchange(packets)
     send = pltpu.with_memory_space_constraint(send, pltpu.SMEM)
-    blocks, turned, table, near = pl.pallas_call(
+    turned, table, near = pl.pallas_call(
         setup,
         out_shape=[
-            pltpu.VMEM((ENTRIES, BLK, BLK), f32),
-            pltpu.VMEM((BLK, BLK, 2 * BLK), bf16),
+            pltpu.VMEM((ENTRIES, BLK, 2 * BLK), bf16),
             pltpu.SMEM((TABLE,), jnp.int32),
             FIELD,
         ],
         in_specs=hbm(2) + smem() + hbm() + vmem(2),
-        out_specs=vmem(2) + smem() + vmem(),
+        out_specs=vmem() + smem() + vmem(),
         scratch_shapes=[
             pltpu.SMEM((SLOTS, ROWS), jnp.int32),
             pltpu.SMEM((ROWS,), jnp.int32),
-            PIECES,
-            pltpu.SemaphoreType.DMA((CHUNKS,)),
+            pltpu.VMEM((ENTRIES, BLK, BLK), f32),
+            pltpu.SemaphoreType.DMA((ROWS // 2,)),
             pltpu.SemaphoreType.DMA((2,)),
-        ],
+        ]
+        + PARTIAL,
         compiler_params=params(),
         cost_estimate=cost(10**10),
         name="setup",
     )(columns, lengths, send, values, concentration, rate)
-    blocks = pltpu.with_memory_space_constraint(blocks, pltpu.VMEM)
     turned = pltpu.with_memory_space_constraint(turned, pltpu.VMEM)
     table = pltpu.with_memory_space_constraint(table, pltpu.SMEM)
     basis = []
@@ -497,11 +439,11 @@
             out_shape=FIELD,
             in_specs=smem() + vmem(4),
             out_specs=vmem()[0],
-            scratch_shapes=[PIECES],
+            scratch_shapes=PARTIAL,
             compiler_params=params(),
             cost_estimate=cost(10**10),
             name="near_part",
-        )(table, blocks, field, rate, concentration)
+        )(table, turned, field, rate, concentration)
         near = middle_call(near, arrived)
     sums = pl.pallas_call(
         last_part,

time: 130 us -> 125 us (0.962)
  Pallas kernels: 30.2 us -> 23 us
  waiting for transfers between devices: 34.4 us -> 36.5 us
    pallas_call x6, Pallas kernels: 12.3 us -> 5.83 us  [shards(): pl.pallas_call(near_part, out_shape=FIELD, in_specs=smem() + vmem(4), out...]
    ppermute x28, waiting for transfers between devices: 25.7 us -> 27.8 us  [exchange(): arrived.append(lax.ppermute(packets[t], 'dom', pairs[t]))]
  transfers between devices with their start and end apart: 29 -> 29, of which waited for: 12 -> 13; matrix products, arithmetic and copies ran while one was open for 0% -> 0% of each run, Pallas kernels for 19% -> 13%
where the time goes in v3:
time: 125 us; the launch traced here: 124 us
  starting transfers between devices  64.1 us (51%)
  waiting for transfers between devices  36.5 us (29%)
  Pallas kernels  23 us (18%)
    ppermute x28, starting transfers between devices, exchange(): arrived.append(lax.ppermute(packets[t], 'dom', pairs[t]))  56.7 us
    ppermute x28, waiting for transfers between devices, exchange(): arrived.append(lax.ppermute(packets[t], 'dom', pairs[t]))  27.8 us
    all_to_all x1, waiting for transfers between devices, shards(): lax.all_to_all(sums, 'dom', split_axis=0, concat_axis=0, tiled=True)  8.67 us
    pallas_call x1, Pallas kernels, shards(): pl.pallas_call(setup, out_shape=[pltpu.VMEM((ENTRIES, BLK, 2 * BLK), bf16...  8.06 us
    all_to_all x1, starting transfers between devices, shards(): lax.all_to_all(sums, 'dom', split_axis=0, concat_axis=0, tiled=True)  7.34 us
    pallas_call x6, Pallas kernels, shards(): pl.pallas_call(near_part, out_shape=FIELD, in_specs=smem() + vmem(4), out...  5.83 us
    pallas_call x7, Pallas kernels, middle_call(): pl.pallas_call(middle_part, out_shape=FIELD, in_specs=smem() + vmem(4), o...  2.91 us
    pallas_call x6, Pallas kernels, shards(): pl.pallas_call(far_part(1.0 if k == 0 else SCALE), out_shape=[FIELD] + PA...  2.79 us
  transfers between devices with their start and end apart: 29, of which 13 were waited for; matrix products, arithmetic and copies ran while one was open for 0% of the time, Pallas kernels for 13%

profile of v3, /device:TPU:0, one launch (start us, length us, event | category | flops | bytes accessed | tf_op | source)
XLA Modules:
  0.0 124.5 jit_solution(2076727360340110808)
XLA Ops:
  0.8 1.7 %collective-permute-start = (f32[16,128]{1,0:T(8,128)S(1)}, f32[16,128]{1,0:T(8,128)S(1)}, u32[]{:S(2)}, u32[]{:S(2)}) collective-permute-start(f32[16,128]{1,0:T(8,128)S(1)} %get-tuple-element.51), channel_id=1, source_target_pairs={{0,2},{1,3},{4,6},{5,7},{8,10},{9,11},{12,14},{13,15},{16,18},{17,... | collective-permute-start | bytes 24584 | tf_op jit(solution)/shard_map/ppermute | solution.py:369
  2.5 8.0 %collective-permute-start.2 = (f32[16,128]{1,0:T(8,128)S(1)}, f32[16,128]{1,0:T(8,128)S(1)}, u32[]{:S(2)}, u32[]{:S(2)}) collective-permute-start(f32[16,128]{1,0:T(8,128)S(1)} %get-tuple-element.53), channel_id=1, source_target_pairs={{2,4},{3,5},{6,8},{7,9},{10,12},{11,13},{14,16},{15,17},{18,20},{1... | collective-permute-start | bytes 24584 | tf_op jit(solution)/shard_map/ppermute | solution.py:369
  10.6 8.1 %setup.1 = (bf16[160,128,256]{2,1,0:T(8,128)(2,1)S(1)}, s32[2472]{0:T(1024)S(4)}, f32[32,128]{1,0:T(8,128)S(1)}) custom-call(s32[5,32]{1,0:T(8,128)} %bitcast.8, s32[32]{0:T(128)} %lengths.1, s32[1,4,16]{2,1,0:T(4,128)S(4)} %get-tuple-element.45.send, f32[160,128,128]{2,1,0:T(8,128)} %bitcast.7, f32[32,128]{1,0:T(8,128)S(1)} %get-tuple-element.46.field.concentration, ...), custom_call_target="tpu_custom_call" | custom-call | flops 10000000000 | tf_op jit(solution)/shard_map/setup/pallas_call | solution.py:387
  19.7 1.8 %collective-permute-start.4 = (f32[16,128]{1,0:T(8,128)S(1)}, f32[16,128]{1,0:T(8,128)S(1)}, u32[]{:S(2)}, u32[]{:S(2)}) collective-permute-start(f32[16,128]{1,0:T(8,128)S(1)} %get-tuple-element.56), channel_id=1, source_target_pairs={{0,2},{1,3},{4,6},{5,7},{8,10},{9,11},{12,14},{13,15},{16,18},{17,... | collective-permute-start | bytes 24584 | tf_op jit(solution)/shard_map/ppermute | solution.py:369
  22.5 5.9 %collective-permute-start.6 = (f32[16,128]{1,0:T(8,128)S(1)}, f32[16,128]{1,0:T(8,128)S(1)}, u32[]{:S(2)}, u32[]{:S(2)}) collective-permute-start(f32[16,128]{1,0:T(8,128)S(1)} %get-tuple-element.58), channel_id=1, source_target_pairs={{2,4},{3,5},{6,8},{7,9},{10,12},{11,13},{14,16},{15,17},{18,20},{1... | collective-permute-start | bytes 24584 | tf_op jit(solution)/shard_map/ppermute | solution.py:369
  28.3 1.5 %collective-permute-start.7 = (f32[16,128]{1,0:T(8,128)S(1)}, f32[16,128]{1,0:T(8,128)S(1)}, u32[]{:S(2)}, u32[]{:S(2)}) collective-permute-start(f32[16,128]{1,0:T(8,128)S(1)} %get-tuple-element.59), channel_id=1, source_target_pairs={{1,2},{3,4},{5,6},{7,8},{9,10},{11,12},{13,14},{15,16},{17,18},{19... | collective-permute-start | bytes 24584 | tf_op jit(solution)/shard_map/ppermute | solution.py:369
  31.6 5.2 %collective-permute-done.7.g1 = f32[16,128]{1,0:T(8,128)S(1)} collective-permute-done((f32[16,128]{1,0:T(8,128)S(1)}, f32[16,128]{1,0:T(8,128)S(1)}, u32[]{:S(2)}, u32[]{:S(2)}) %collective-permute-start.7) | collective-permute-done | bytes 8224 | tf_op jit(solution)/shard_map/ppermute | solution.py:369
  38.5 1.9 %collective-permute-start.10 = (f32[16,128]{1,0:T(8,128)S(1)}, f32[16,128]{1,0:T(8,128)S(1)}, u32[]{:S(2)}, u32[]{:S(2)}) collective-permute-start(f32[16,128]{1,0:T(8,128)S(1)} %get-tuple-element.63), channel_id=1, source_target_pairs={{2,4},{3,5},{6,8},{7,9},{10,12},{11,13},{14,16},{15,17},{18,20},{1... | collective-permute-start | bytes 24584 | tf_op jit(solution)/shard_map/ppermute | solution.py:369
  40.4 5.4 %collective-permute-start.11 = (f32[16,128]{1,0:T(8,128)S(1)}, f32[16,128]{1,0:T(8,128)S(1)}, u32[]{:S(2)}, u32[]{:S(2)}) collective-permute-start(f32[16,128]{1,0:T(8,128)S(1)} %get-tuple-element.64), channel_id=1, source_target_pairs={{1,2},{3,4},{5,6},{7,8},{9,10},{11,12},{13,14},{15,16},{17,18},{19... | collective-permute-start | bytes 24584 | tf_op jit(solution)/shard_map/ppermute | solution.py:369
  46.3 1.4 %collective-permute-done.10.g0 = f32[16,128]{1,0:T(8,128)S(1)} collective-permute-done((f32[16,128]{1,0:T(8,128)S(1)}, f32[16,128]{1,0:T(8,128)S(1)}, u32[]{:S(2)}, u32[]{:S(2)}) %collective-permute-start.10) | collective-permute-done | bytes 8224 | tf_op jit(solution)/shard_map/ppermute | solution.py:369
  50.6 5.9 %collective-permute-start.14 = (f32[16,128]{1,0:T(8,128)S(1)}, f32[16,128]{1,0:T(8,128)S(1)}, u32[]{:S(2)}, u32[]{:S(2)}) collective-permute-start(f32[16,128]{1,0:T(8,128)S(1)} %get-tuple-element.68), channel_id=1, source_target_pairs={{2,4},{3,5},{6,8},{7,9},{10,12},{11,13},{14,16},{15,17},{18,20},{1... | collective-permute-start | bytes 24584 | tf_op jit(solution)/shard_map/ppermute | solution.py:369
  56.4 1.5 %collective-permute-start.15 = (f32[16,128]{1,0:T(8,128)S(1)}, f32[16,128]{1,0:T(8,128)S(1)}, u32[]{:S(2)}, u32[]{:S(2)}) collective-permute-start(f32[16,128]{1,0:T(8,128)S(1)} %get-tuple-element.69), channel_id=1, source_target_pairs={{1,2},{3,4},{5,6},{7,8},{9,10},{11,12},{13,14},{15,16},{17,18},{19... | collective-permute-start | bytes 24584 | tf_op jit(solution)/shard_map/ppermute | solution.py:369
  58.3 1.4 %collective-permute-done.14.g0 = f32[16,128]{1,0:T(8,128)S(1)} collective-permute-done((f32[16,128]{1,0:T(8,128)S(1)}, f32[16,128]{1,0:T(8,128)S(1)}, u32[]{:S(2)}, u32[]{:S(2)}) %collective-permute-start.14) | collective-permute-done | bytes 8224 | tf_op jit(solution)/shard_map/ppermute | solution.py:369
  59.7 5.2 %collective-permute-done.15.g1 = f32[16,128]{1,0:T(8,128)S(1)} collective-permute-done((f32[16,128]{1,0:T(8,128)S(1)}, f32[16,128]{1,0:T(8,128)S(1)}, u32[]{:S(2)}, u32[]{:S(2)}) %collective-permute-start.15) | collective-permute-done | bytes 8224 | tf_op jit(solution)/shard_map/ppermute | solution.py:369
  66.6 1.9 %collective-permute-start.18 = (f32[16,128]{1,0:T(8,128)S(1)}, f32[16,128]{1,0:T(8,128)S(1)}, u32[]{:S(2)}, u32[]{:S(2)}) collective-permute-start(f32[16,128]{1,0:T(8,128)S(1)} %get-tuple-element.73), channel_id=1, source_target_pairs={{2,4},{3,5},{6,8},{7,9},{10,12},{11,13},{14,16},{15,17},{18,20},{1... | collective-permute-start | bytes 24584 | tf_op jit(solution)/shard_map/ppermute | solution.py:369
  68.5 5.4 %collective-permute-start.19 = (f32[16,128]{1,0:T(8,128)S(1)}, f32[16,128]{1,0:T(8,128)S(1)}, u32[]{:S(2)}, u32[]{:S(2)}) collective-permute-start(f32[16,128]{1,0:T(8,128)S(1)} %get-tuple-element.74), channel_id=1, source_target_pairs={{1,2},{3,4},{5,6},{7,8},{9,10},{11,12},{13,14},{15,16},{17,18},{19... | collective-permute-start | bytes 24584 | tf_op jit(solution)/shard_map/ppermute | solution.py:369
  74.3 1.4 %collective-permute-done.18.g0 = f32[16,128]{1,0:T(8,128)S(1)} collective-permute-done((f32[16,128]{1,0:T(8,128)S(1)}, f32[16,128]{1,0:T(8,128)S(1)}, u32[]{:S(2)}, u32[]{:S(2)}) %collective-permute-start.18) | collective-permute-done | bytes 8224 | tf_op jit(solution)/shard_map/ppermute | solution.py:369
  78.8 5.9 %collective-permute-start.22 = (f32[16,128]{1,0:T(8,128)S(1)}, f32[16,128]{1,0:T(8,128)S(1)}, u32[]{:S(2)}, u32[]{:S(2)}) collective-permute-start(f32[16,128]{1,0:T(8,128)S(1)} %get-tuple-element.78), channel_id=1, source_target_pairs={{2,4},{3,5},{6,8},{7,9},{10,12},{11,13},{14,16},{15,17},{18,20},{1... | collective-permute-start | bytes 24584 | tf_op jit(solution)/shard_map/ppermute | solution.py:369
  84.7 1.5 %collective-permute-start.23 = (f32[16,128]{1,0:T(8,128)S(1)}, f32[16,128]{1,0:T(8,128)S(1)}, u32[]{:S(2)}, u32[]{:S(2)}) collective-permute-start(f32[16,128]{1,0:T(8,128)S(1)} %get-tuple-element.79), channel_id=1, source_target_pairs={{1,2},{3,4},{5,6},{7,8},{9,10},{11,12},{13,14},{15,16},{17,18},{19... | collective-permute-start | bytes 24584 | tf_op jit(solution)/shard_map/ppermute | solution.py:369
  88.0 5.2 %collective-permute-done.23.g1 = f32[16,128]{1,0:T(8,128)S(1)} collective-permute-done((f32[16,128]{1,0:T(8,128)S(1)}, f32[16,128]{1,0:T(8,128)S(1)}, u32[]{:S(2)}, u32[]{:S(2)}) %collective-permute-start.23) | collective-permute-done | bytes 8224 | tf_op jit(solution)/shard_map/ppermute | solution.py:369
  94.8 1.9 %collective-permute-start.26 = (f32[16,128]{1,0:T(8,128)S(1)}, f32[16,128]{1,0:T(8,128)S(1)}, u32[]{:S(2)}, u32[]{:S(2)}) collective-permute-start(f32[16,128]{1,0:T(8,128)S(1)} %get-tuple-element.83), channel_id=1, source_target_pairs={{2,4},{3,5},{6,8},{7,9},{10,12},{11,13},{14,16},{15,17},{18,20},{1... | collective-permute-start | bytes 24584 | tf_op jit(solution)/shard_map/ppermute | solution.py:369
  96.7 5.4 %collective-permute-start.27 = (f32[16,128]{1,0:T(8,128)S(1)}, f32[16,128]{1,0:T(8,128)S(1)}, u32[]{:S(2)}, u32[]{:S(2)}) collective-permute-start(f32[16,128]{1,0:T(8,128)S(1)} %get-tuple-element.84), channel_id=1, source_target_pairs={{1,2},{3,4},{5,6},{7,8},{9,10},{11,12},{13,14},{15,16},{17,18},{19... | collective-permute-start | bytes 24584 | tf_op jit(solution)/shard_map/ppermute | solution.py:369
  106.6 7.3 %all-to-all-start = ((f32[128,1,128]{2,1,0:T(1,128)}), f32[128,1,128]{2,1,0:T(1,128)S(1)}, u32[]{:S(2)}, u32[]{:S(2)}) async-start(f32[128,1,128]{2,1,0:T(1,128)} %bitcast.3), calls=%async_computation | async-start | bytes 131072 | tf_op jit(solution)/shard_map/all_to_all | solution.py:457
  114.6 8.7 %all-to-all-done = f32[128,1,128]{2,1,0:T(1,128)S(1)} async-done(((f32[128,1,128]{2,1,0:T(1,128)}), f32[128,1,128]{2,1,0:T(1,128)S(1)}, u32[]{:S(2)}, u32[]{:S(2)}) %all-to-all-start) | async-done | bytes 65568 | tf_op jit(solution)/shard_map/all_to_all | solution.py:457
  (57 shorter events, 24.1 us)
Async XLA Ops:
  0.8 17.9 %collective-permute-start = (f32[16,128]{1,0:T(8,128)S(1)}, f32[16,128]{1,0:T(8,128)S(1)}, u32[]{:S(2)}, u32[]{:S(2)}) collective-permute-start(f32[16,128]{1,0:T(8,128)S(1)} %get-tuple-element.51), channel_id=1, source_target_pairs={{0,2},{1,3},{4,6},{5,7},{8,10},{9,11},{12,14},{13,15},{16,18},{17,... | collective-permute-start | bytes 24584 | tf_op jit(solution)/shard_map/ppermute | solution.py:369
  2.5 16.2 %collective-permute-start.1 = (f32[16,128]{1,0:T(8,128)S(1)}, f32[16,128]{1,0:T(8,128)S(1)}, u32[]{:S(2)}, u32[]{:S(2)}) collective-permute-start(f32[16,128]{1,0:T(8,128)S(1)} %get-tuple-element.52), channel_id=1, source_target_pairs={{0,1},{2,3},{4,5},{6,7},{8,9},{10,11},{12,13},{14,15},{16,17},{18,... | collective-permute-start | bytes 24584 | tf_op jit(solution)/shard_map/ppermute | solution.py:369
  2.5 16.7 %collective-permute-start.2 = (f32[16,128]{1,0:T(8,128)S(1)}, f32[16,128]{1,0:T(8,128)S(1)}, u32[]{:S(2)}, u32[]{:S(2)}) collective-permute-start(f32[16,128]{1,0:T(8,128)S(1)} %get-tuple-element.53), channel_id=1, source_target_pairs={{2,4},{3,5},{6,8},{7,9},{10,12},{11,13},{14,16},{15,17},{18,20},{1... | collective-permute-start | bytes 24584 | tf_op jit(solution)/shard_map/ppermute | solution.py:369
  10.5 8.6 %collective-permute-start.3 = (f32[16,128]{1,0:T(8,128)S(1)}, f32[16,128]{1,0:T(8,128)S(1)}, u32[]{:S(2)}, u32[]{:S(2)}) collective-permute-start(f32[16,128]{1,0:T(8,128)S(1)} %get-tuple-element.54), channel_id=1, source_target_pairs={{1,2},{3,4},{5,6},{7,8},{9,10},{11,12},{13,14},{15,16},{17,18},{19... | collective-permute-start | bytes 24584 | tf_op jit(solution)/shard_map/ppermute | solution.py:369
  19.7 10.2 %collective-permute-start.4 = (f32[16,128]{1,0:T(8,128)S(1)}, f32[16,128]{1,0:T(8,128)S(1)}, u32[]{:S(2)}, u32[]{:S(2)}) collective-permute-start(f32[16,128]{1,0:T(8,128)S(1)} %get-tuple-element.56), channel_id=1, source_target_pairs={{0,2},{1,3},{4,6},{5,7},{8,10},{9,11},{12,14},{13,15},{16,18},{17,... | collective-permute-start | bytes 24584 | tf_op jit(solution)/shard_map/ppermute | solution.py:369
  22.5 9.2 %collective-permute-start.6 = (f32[16,128]{1,0:T(8,128)S(1)}, f32[16,128]{1,0:T(8,128)S(1)}, u32[]{:S(2)}, u32[]{:S(2)}) collective-permute-start(f32[16,128]{1,0:T(8,128)S(1)} %get-tuple-element.58), channel_id=1, source_target_pairs={{2,4},{3,5},{6,8},{7,9},{10,12},{11,13},{14,16},{15,17},{18,20},{1... | collective-permute-start | bytes 24584 | tf_op jit(solution)/shard_map/ppermute | solution.py:369
  28.3 8.5 %collective-permute-start.7 = (f32[16,128]{1,0:T(8,128)S(1)}, f32[16,128]{1,0:T(8,128)S(1)}, u32[]{:S(2)}, u32[]{:S(2)}) collective-permute-start(f32[16,128]{1,0:T(8,128)S(1)} %get-tuple-element.59), channel_id=1, source_target_pairs={{1,2},{3,4},{5,6},{7,8},{9,10},{11,12},{13,14},{15,16},{17,18},{19... | collective-permute-start | bytes 24584 | tf_op jit(solution)/shard_map/ppermute | solution.py:369
  37.3 8.5 %collective-permute-start.8 = (f32[16,128]{1,0:T(8,128)S(1)}, f32[16,128]{1,0:T(8,128)S(1)}, u32[]{:S(2)}, u32[]{:S(2)}) collective-permute-start(f32[16,128]{1,0:T(8,128)S(1)} %get-tuple-element.61), channel_id=1, source_target_pairs={{0,2},{1,3},{4,6},{5,7},{8,10},{9,11},{12,14},{13,15},{16,18},{17,... | collective-permute-start | bytes 24584 | tf_op jit(solution)/shard_map/ppermute | solution.py:369
  37.4 8.4 %collective-permute-start.9 = (f32[16,128]{1,0:T(8,128)S(1)}, f32[16,128]{1,0:T(8,128)S(1)}, u32[]{:S(2)}, u32[]{:S(2)}) collective-permute-start(f32[16,128]{1,0:T(8,128)S(1)} %get-tuple-element.62), channel_id=1, source_target_pairs={{0,1},{2,3},{4,5},{6,7},{8,9},{10,11},{12,13},{14,15},{16,17},{18,... | collective-permute-start | bytes 24584 | tf_op jit(solution)/shard_map/ppermute | solution.py:369
  38.5 9.2 %collective-permute-start.10 = (f32[16,128]{1,0:T(8,128)S(1)}, f32[16,128]{1,0:T(8,128)S(1)}, u32[]{:S(2)}, u32[]{:S(2)}) collective-permute-start(f32[16,128]{1,0:T(8,128)S(1)} %get-tuple-element.63), channel_id=1, source_target_pairs={{2,4},{3,5},{6,8},{7,9},{10,12},{11,13},{14,16},{15,17},{18,20},{1... | collective-permute-start | bytes 24584 | tf_op jit(solution)/shard_map/ppermute | solution.py:369
  40.4 8.5 %collective-permute-start.11 = (f32[16,128]{1,0:T(8,128)S(1)}, f32[16,128]{1,0:T(8,128)S(1)}, u32[]{:S(2)}, u32[]{:S(2)}) collective-permute-start(f32[16,128]{1,0:T(8,128)S(1)} %get-tuple-element.64), channel_id=1, source_target_pairs={{1,2},{3,4},{5,6},{7,8},{9,10},{11,12},{13,14},{15,16},{17,18},{19... | collective-permute-start | bytes 24584 | tf_op jit(solution)/shard_map/ppermute | solution.py:369
  49.4 8.5 %collective-permute-start.12 = (f32[16,128]{1,0:T(8,128)S(1)}, f32[16,128]{1,0:T(8,128)S(1)}, u32[]{:S(2)}, u32[]{:S(2)}) collective-permute-start(f32[16,128]{1,0:T(8,128)S(1)} %get-tuple-element.66), channel_id=1, source_target_pairs={{0,2},{1,3},{4,6},{5,7},{8,10},{9,11},{12,14},{13,15},{16,18},{17,... | collective-permute-start | bytes 24584 | tf_op jit(solution)/shard_map/ppermute | solution.py:369
  50.6 9.2 %collective-permute-start.14 = (f32[16,128]{1,0:T(8,128)S(1)}, f32[16,128]{1,0:T(8,128)S(1)}, u32[]{:S(2)}, u32[]{:S(2)}) collective-permute-start(f32[16,128]{1,0:T(8,128)S(1)} %get-tuple-element.68), channel_id=1, source_target_pairs={{2,4},{3,5},{6,8},{7,9},{10,12},{11,13},{14,16},{15,17},{18,20},{1... | collective-permute-start | bytes 24584 | tf_op jit(solution)/shard_map/ppermute | solution.py:369
  56.4 8.5 %collective-permute-start.15 = (f32[16,128]{1,0:T(8,128)S(1)}, f32[16,128]{1,0:T(8,128)S(1)}, u32[]{:S(2)}, u32[]{:S(2)}) collective-permute-start(f32[16,128]{1,0:T(8,128)S(1)} %get-tuple-element.69), channel_id=1, source_target_pairs={{1,2},{3,4},{5,6},{7,8},{9,10},{11,12},{13,14},{15,16},{17,18},{19... | collective-permute-start | bytes 24584 | tf_op jit(solution)/shard_map/ppermute | solution.py:369
  65.4 8.5 %collective-permute-start.16 = (f32[16,128]{1,0:T(8,128)S(1)}, f32[16,128]{1,0:T(8,128)S(1)}, u32[]{:S(2)}, u32[]{:S(2)}) collective-permute-start(f32[16,128]{1,0:T(8,128)S(1)} %get-tuple-element.71), channel_id=1, source_target_pairs={{0,2},{1,3},{4,6},{5,7},{8,10},{9,11},{12,14},{13,15},{16,18},{17,... | collective-permute-start | bytes 24584 | tf_op jit(solution)/shard_map/ppermute | solution.py:369
  66.6 9.2 %collective-permute-start.18 = (f32[16,128]{1,0:T(8,128)S(1)}, f32[16,128]{1,0:T(8,128)S(1)}, u32[]{:S(2)}, u32[]{:S(2)}) collective-permute-start(f32[16,128]{1,0:T(8,128)S(1)} %get-tuple-element.73), channel_id=1, source_target_pairs={{2,4},{3,5},{6,8},{7,9},{10,12},{11,13},{14,16},{15,17},{18,20},{1... | collective-permute-start | bytes 24584 | tf_op jit(solution)/shard_map/ppermute | solution.py:369
  68.5 8.5 %collective-permute-start.19 = (f32[16,128]{1,0:T(8,128)S(1)}, f32[16,128]{1,0:T(8,128)S(1)}, u32[]{:S(2)}, u32[]{:S(2)}) collective-permute-start(f32[16,128]{1,0:T(8,128)S(1)} %get-tuple-element.74), channel_id=1, source_target_pairs={{1,2},{3,4},{5,6},{7,8},{9,10},{11,12},{13,14},{15,16},{17,18},{19... | collective-permute-start | bytes 24584 | tf_op jit(solution)/shard_map/ppermute | solution.py:369
  77.5 8.7 %collective-permute-start.20 = (f32[16,128]{1,0:T(8,128)S(1)}, f32[16,128]{1,0:T(8,128)S(1)}, u32[]{:S(2)}, u32[]{:S(2)}) collective-permute-start(f32[16,128]{1,0:T(8,128)S(1)} %get-tuple-element.76), channel_id=1, source_target_pairs={{0,2},{1,3},{4,6},{5,7},{8,10},{9,11},{12,14},{13,15},{16,18},{17,... | collective-permute-start | bytes 24584 | tf_op jit(solution)/shard_map/ppermute | solution.py:369
  78.8 9.2 %collective-permute-start.22 = (f32[16,128]{1,0:T(8,128)S(1)}, f32[16,128]{1,0:T(8,128)S(1)}, u32[]{:S(2)}, u32[]{:S(2)}) collective-permute-start(f32[16,128]{1,0:T(8,128)S(1)} %get-tuple-element.78), channel_id=1, source_target_pairs={{2,4},{3,5},{6,8},{7,9},{10,12},{11,13},{14,16},{15,17},{18,20},{1... | collective-permute-start | bytes 24584 | tf_op jit(solution)/shard_map/ppermute | solution.py:369
  84.7 8.5 %collective-permute-start.23 = (f32[16,128]{1,0:T(8,128)S(1)}, f32[16,128]{1,0:T(8,128)S(1)}, u32[]{:S(2)}, u32[]{:S(2)}) collective-permute-start(f32[16,128]{1,0:T(8,128)S(1)} %get-tuple-element.79), channel_id=1, source_target_pairs={{1,2},{3,4},{5,6},{7,8},{9,10},{11,12},{13,14},{15,16},{17,18},{19... | collective-permute-start | bytes 24584 | tf_op jit(solution)/shard_map/ppermute | solution.py:369
  93.6 8.5 %collective-permute-start.24 = (f32[16,128]{1,0:T(8,128)S(1)}, f32[16,128]{1,0:T(8,128)S(1)}, u32[]{:S(2)}, u32[]{:S(2)}) collective-permute-start(f32[16,128]{1,0:T(8,128)S(1)} %get-tuple-element.81), channel_id=1, source_target_pairs={{0,2},{1,3},{4,6},{5,7},{8,10},{9,11},{12,14},{13,15},{16,18},{17,... | collective-permute-start | bytes 24584 | tf_op jit(solution)/shard_map/ppermute | solution.py:369
  94.8 9.2 %collective-permute-start.26 = (f32[16,128]{1,0:T(8,128)S(1)}, f32[16,128]{1,0:T(8,128)S(1)}, u32[]{:S(2)}, u32[]{:S(2)}) collective-permute-start(f32[16,128]{1,0:T(8,128)S(1)} %get-tuple-element.83), channel_id=1, source_target_pairs={{2,4},{3,5},{6,8},{7,9},{10,12},{11,13},{14,16},{15,17},{18,20},{1... | collective-permute-start | bytes 24584 | tf_op jit(solution)/shard_map/ppermute | solution.py:369
  96.7 8.5 %collective-permute-start.27 = (f32[16,128]{1,0:T(8,128)S(1)}, f32[16,128]{1,0:T(8,128)S(1)}, u32[]{:S(2)}, u32[]{:S(2)}) collective-permute-start(f32[16,128]{1,0:T(8,128)S(1)} %get-tuple-element.84), channel_id=1, source_target_pairs={{1,2},{3,4},{5,6},{7,8},{9,10},{11,12},{13,14},{15,16},{17,18},{19... | collective-permute-start | bytes 24584 | tf_op jit(solution)/shard_map/ppermute | solution.py:369
  106.6 16.7 %all-to-all-start = ((f32[128,1,128]{2,1,0:T(1,128)}), f32[128,1,128]{2,1,0:T(1,128)S(1)}, u32[]{:S(2)}, u32[]{:S(2)}) async-start(f32[128,1,128]{2,1,0:T(1,128)} %bitcast.3), calls=%async_computation | async-start | bytes 131072 | tf_op jit(solution)/shard_map/all_to_all | solution.py:457
  (5 other events, 42.0 us)

commit v4 on v3

--- a/solution.py
+++ b/solution.py
@@ -15,16 +15,15 @@
 SCALE = 0.25
 PAIRS = [(a, b) for b in range(DEGREE + 1) for a in range(min(b, DEGREE - 1) + 1)]
 
-LIST = ENTRIES + 40
-GROUPS = (40, 32, 32)
+GROUPS = (80, 56)
+LIST = ENTRIES + max(GROUPS)
 NEAR = 0
 FAR = 3 * LIST
-MID = 6 * LIST
-REST = 9 * LIST
+REST = 6 * LIST
 SEND = REST + 3 * LIST
 COUNTS = SEND + 64
 TABLE = COUNTS + 8
-ZERO = ROWS
+LINES = 4 * GHOST
 
 f32 = jnp.float32
 bf16 = jnp.bfloat16
@@ -111,7 +110,7 @@
         copy.wait()
 
     def rows(pair, carry):
-        near, far, mid = carry
+        near, far = carry
         fetch(pair).wait()
         for half in range(2):
             b = pair * 2 + half
@@ -124,30 +123,25 @@
                 live = s < length
                 ghost = jnp.logical_and(live, column >= ROWS)
                 home = jnp.logical_and(live, column < ROWS)
-                first = jnp.logical_and(ghost, spot < 2)
-                second = jnp.logical_and(ghost, spot >= 2)
-                base = jnp.where(
-                    home, NEAR + near, jnp.where(first, FAR + far, jnp.where(second, MID + mid, REST))
-                )
-                table[base] = jnp.where(ghost, ((spot & 1) << 4) + (index & 15), column)
+                base = jnp.where(home, NEAR + near, jnp.where(ghost, FAR + far, REST))
+                table[base] = jnp.where(ghost, (spot << 4) + (index & 15), column)
                 table[base + LIST] = b * SLOTS + s
                 table[base + 2 * LIST] = b
                 near = near + home.astype(jnp.int32)
-                far = far + first.astype(jnp.int32)
-                mid = mid + second.astype(jnp.int32)
+                far = far + ghost.astype(jnp.int32)
         for s in range(2 * SLOTS):
             slot = pair * 2 * SLOTS + s
             high, rest = split(jnp.transpose(blocks[slot]))
             turned[slot, :, 0:BLK] = high
             turned[slot, :, BLK : 2 * BLK] = rest
-        return near, far, mid
+        return near, far
 
     zero = jnp.int32(0)
-    counts = lax.fori_loop(0, ROWS // 2, rows, (zero, zero, zero))
-    for i, base in enumerate((NEAR, FAR, MID)):
+    counts = lax.fori_loop(0, ROWS // 2, rows, (zero, zero))
+    for i, base in enumerate((NEAR, FAR)):
         table[COUNTS + i] = counts[i]
         for g in range(GROUPS[i]):
-            table[base + counts[i] + g] = ZERO
+            table[base + counts[i] + g] = LINES
             table[base + LIST + counts[i] + g] = 0
             table[base + 2 * LIST + counts[i] + g] = 0
     total = product(table, 0, turned, (field,), *scratch)
@@ -161,13 +155,13 @@
 
 
 def product(table, which, turned, sources, lines, stage, *sums):
-    base = (NEAR, FAR, MID)[which]
+    base = (NEAR, FAR)[which]
     size = GROUPS[which]
     count = table[COUNTS + which]
-    height = ROWS // len(sources)
     for i, source in enumerate(sources):
+        height = source.shape[0]
         lines[i * height : (i + 1) * height, :] = source[...]
-    lines[ZERO : ZERO + 8, :] = jnp.zeros((8, BLK), f32)
+    lines[LINES : LINES + 8, :] = jnp.zeros((8, BLK), f32)
     for ref in sums:
         ref[...] = jnp.zeros((ROWS, BLK), f32)
 
@@ -190,35 +184,25 @@
     return (sums[0][...] + sums[1][...]) + (sums[2][...] + sums[3][...])
 
 
-def middle_part(table, turned, near, g2, g3, out, *scratch):
-    out[...] = near[...] - product(table, 2, turned, (g2, g3), *scratch)
-
-
 def far_part(scale):
-    def kernel(table, turned, near, g0, g1, out, p0, p1, p2, p3, *scratch):
-        out[...] = (near[...] - product(table, 1, turned, (g0, g1), *scratch)) * scale
+    def kernel(table, turned, near, g0, g1, g2, g3, out, p0, p1, p2, p3, *scratch):
+        out[...] = (near[...] - product(table, 1, turned, (g0, g1, g2, g3), *scratch)) * scale
         write_packets(out, lambda t, g: table[SEND + t * GHOST + g], (p0, p1, p2, p3))
 
     return kernel
 
 
-def last_part(table, turned, near, g0, g1, *rest):
+def last_part(table, turned, near, g0, g1, g2, g3, *rest):
     basis = rest[:DEGREE]
     sums, out, rows, *scratch = rest[DEGREE:]
-    out[...] = (near[...] - product(table, 1, turned, (g0, g1), *scratch)) * SCALE
+    out[...] = (near[...] - product(table, 1, turned, (g0, g1, g2, g3), *scratch)) * SCALE
     basis = basis + (out,)
-    rows[...] = jnp.zeros((BLK, BLK), f32)
+    rows[...] = jnp.zeros(rows.shape, f32)
     for k, (a, b) in enumerate(PAIRS):
         both = basis[a][...] * basis[b][...]
         rows[k : k + 1, :] = jnp.sum(both, axis=0, keepdims=True)
-    line = lax.dot_general(
-        jnp.ones((8, BLK), f32),
-        rows[...],
-        (((1,), (1,)), ((), ())),
-        precision=lax.Precision.HIGHEST,
-        preferred_element_type=f32,
-    )
-    sums[...] = jnp.broadcast_to(line[0:1], sums.shape)
+    line = jnp.sum(jnp.transpose(rows[...]), axis=0, keepdims=True)
+    sums[...] = jnp.broadcast_to(line, sums.shape)
 
 
 def add(x, y):
@@ -343,7 +327,7 @@
 FIELD = jax.ShapeDtypeStruct((ROWS, BLK), f32)
 PACKETS = [jax.ShapeDtypeStruct((GHOST, BLK), f32)] * 4
 PARTIAL = [
-    pltpu.VMEM((ROWS + 8, BLK), f32),
+    pltpu.VMEM((LINES + 8, BLK), f32),
     pltpu.VMEM((max(GROUPS), BLK), f32),
 ] + [pltpu.VMEM((ROWS, BLK), f32)] * 4
 
@@ -409,29 +393,16 @@
     table = pltpu.with_memory_space_constraint(table, pltpu.SMEM)
     basis = []
 
-    def middle_call(near, arrived):
-        return pl.pallas_call(
-            middle_part,
-            out_shape=FIELD,
-            in_specs=smem() + vmem(4),
-            out_specs=vmem()[0],
-            scratch_shapes=PARTIAL,
-            compiler_params=params(),
-            cost_estimate=cost(10**9),
-            name="middle_part",
-        )(table, turned, near, *arrived[2:])
-
-    near = middle_call(near, arrived)
     for k in range(DEGREE):
         field, *packets = pl.pallas_call(
             far_part(1.0 if k == 0 else SCALE),
             out_shape=[FIELD] + PACKETS,
-            in_specs=smem() + vmem(4),
+            in_specs=smem() + vmem(6),
             out_specs=vmem(5),
             scratch_shapes=PARTIAL,
             compiler_params=params(),
             name="far_part",
-        )(table, turned, near, *arrived[:2])
+        )(table, turned, near, *arrived)
         basis.append(field)
         arrived = exchange(packets)
         near = pl.pallas_call(
@@ -444,16 +415,15 @@
             cost_estimate=cost(10**10),
             name="near_part",
         )(table, turned, field, rate, concentration)
-        near = middle_call(near, arrived)
     sums = pl.pallas_call(
         last_part,
-        out_shape=jax.ShapeDtypeStruct((devices, BLK), f32),
-        in_specs=smem() + vmem(4 + DEGREE),
+        out_shape=jax.ShapeDtypeStruct((devices, ROWS), f32),
+        in_specs=smem() + vmem(6 + DEGREE),
         out_specs=vmem()[0],
-        scratch_shapes=[pltpu.VMEM((ROWS, BLK), f32), pltpu.VMEM((BLK, BLK), f32)] + PARTIAL,
+        scratch_shapes=[pltpu.VMEM((ROWS, BLK), f32), pltpu.VMEM((ROWS, BLK), f32)] + PARTIAL,
         compiler_params=params(),
         name="last_part",
-    )(table, turned, near, *arrived[:2], *basis)
+    )(table, turned, near, *arrived, *basis)
     everyone = lax.all_to_all(sums, "dom", split_axis=0, concat_axis=0, tiled=True)
     return pl.pallas_call(
         finish,

time: 125 us -> 106 us (0.85)
  waiting for transfers between devices: 36.5 us -> 26.2 us
  starting transfers between devices: 64.1 us -> 58 us
  Pallas kernels: 23 us -> 20.4 us
    ppermute x28, waiting for transfers between devices: 27.8 us -> 17.6 us  [exchange(): arrived.append(lax.ppermute(packets[t], 'dom', pairs[t]))]
    ppermute x28, starting transfers between devices: 56.7 us -> 52.1 us  [exchange(): arrived.append(lax.ppermute(packets[t], 'dom', pairs[t]))]
    pallas_call x8 -> x1, Pallas kernels: 4.21 us -> 1.41 us  [shards(): pl.pallas_call(last_part, out_shape=jax.ShapeDtypeStruct((devices, ROWS),...]
    all_to_all x1, starting transfers between devices: 7.34 us -> 5.93 us  [shards(): lax.all_to_all(sums, 'dom', split_axis=0, concat_axis=0, tiled=True)]
    pallas_call x6, Pallas kernels: 2.79 us -> 4.1 us  [shards(): pl.pallas_call(far_part(1.0 if k == 0 else SCALE), out_shape=[FIELD] + PA...]
  transfers between devices with their start and end apart: 29 -> 29, of which waited for: 13 -> 13; matrix products, arithmetic and copies ran while one was open for 0% -> 0% of each run, Pallas kernels for 13% -> 12%
where the time goes in v4:
time: 106 us; the launch traced here: 105 us
  starting transfers between devices  58 us (55%)
  waiting for transfers between devices  26.2 us (25%)
  Pallas kernels  20.4 us (19%)
    ppermute x28, starting transfers between devices, exchange(): arrived.append(lax.ppermute(packets[t], 'dom', pairs[t]))  52.1 us
    ppermute x28, waiting for transfers between devices, exchange(): arrived.append(lax.ppermute(packets[t], 'dom', pairs[t]))  17.6 us
    all_to_all x1, waiting for transfers between devices, shards(): lax.all_to_all(sums, 'dom', split_axis=0, concat_axis=0, tiled=True)  8.67 us
    pallas_call x1, Pallas kernels, shards(): pl.pallas_call(setup, out_shape=[pltpu.VMEM((ENTRIES, BLK, 2 * BLK), bf16...  7.6 us
    all_to_all x1, starting transfers between devices, shards(): lax.all_to_all(sums, 'dom', split_axis=0, concat_axis=0, tiled=True)  5.93 us
    pallas_call x6, Pallas kernels, shards(): pl.pallas_call(near_part, out_shape=FIELD, in_specs=smem() + vmem(4), out...  5.2 us
    pallas_call x6, Pallas kernels, shards(): pl.pallas_call(far_part(1.0 if k == 0 else SCALE), out_shape=[FIELD] + PA...  4.1 us
  transfers between devices with their start and end apart: 29, of which 13 were waited for; matrix products, arithmetic and copies ran while one was open for 0% of the time, Pallas kernels for 12%

profile of v4, /device:TPU:0, one launch (start us, length us, event | category | flops | bytes accessed | tf_op | source)
XLA Modules:
  0.0 105.4 jit_solution(6855936279498431295)
XLA Ops:
  0.8 8.9 %collective-permute-start = (f32[16,128]{1,0:T(8,128)S(1)}, f32[16,128]{1,0:T(8,128)S(1)}, u32[]{:S(2)}, u32[]{:S(2)}) collective-permute-start(f32[16,128]{1,0:T(8,128)S(1)} %get-tuple-element.51), channel_id=1, source_target_pairs={{2,4},{3,5},{6,8},{7,9},{10,12},{11,13},{14,16},{15,17},{18,20},{1... | collective-permute-start | bytes 24584 | tf_op jit(solution)/shard_map/ppermute | solution.py:353
  9.7 1.2 %collective-permute-start.2 = (f32[16,128]{1,0:T(8,128)S(1)}, f32[16,128]{1,0:T(8,128)S(1)}, u32[]{:S(2)}, u32[]{:S(2)}) collective-permute-start(f32[16,128]{1,0:T(8,128)S(1)} %get-tuple-element.53), channel_id=1, source_target_pairs={{0,2},{1,3},{4,6},{5,7},{8,10},{9,11},{12,14},{13,15},{16,18},{17,... | collective-permute-start | bytes 24584 | tf_op jit(solution)/shard_map/ppermute | solution.py:353
  10.9 7.6 %setup.1 = (bf16[160,128,256]{2,1,0:T(8,128)(2,1)S(1)}, s32[2232]{0:T(1024)S(4)}, f32[32,128]{1,0:T(8,128)S(1)}) custom-call(s32[5,32]{1,0:T(8,128)} %bitcast.8, s32[32]{0:T(128)} %lengths.1, s32[1,4,16]{2,1,0:T(4,128)S(4)} %get-tuple-element.45.send, f32[160,128,128]{2,1,0:T(8,128)} %bitcast.7, f32[32,128]{1,0:T(8,128)S(1)} %get-tuple-element.46.field.concentration, ...), custom_call_target="tpu_custom_call" | custom-call | flops 10000000000 | tf_op jit(solution)/shard_map/setup/pallas_call | solution.py:371
  19.2 6.5 %collective-permute-start.4 = (f32[16,128]{1,0:T(8,128)S(1)}, f32[16,128]{1,0:T(8,128)S(1)}, u32[]{:S(2)}, u32[]{:S(2)}) collective-permute-start(f32[16,128]{1,0:T(8,128)S(1)} %get-tuple-element.56), channel_id=1, source_target_pairs={{2,4},{3,5},{6,8},{7,9},{10,12},{11,13},{14,16},{15,17},{18,20},{1... | collective-permute-start | bytes 24584 | tf_op jit(solution)/shard_map/ppermute | solution.py:353
  28.4 5.8 %collective-permute-done.5.g1 = f32[16,128]{1,0:T(8,128)S(1)} collective-permute-done((f32[16,128]{1,0:T(8,128)S(1)}, f32[16,128]{1,0:T(8,128)S(1)}, u32[]{:S(2)}, u32[]{:S(2)}) %collective-permute-start.5) | collective-permute-done | bytes 8224 | tf_op jit(solution)/shard_map/ppermute | solution.py:353
  35.1 1.6 %collective-permute-start.8 = (f32[16,128]{1,0:T(8,128)S(1)}, f32[16,128]{1,0:T(8,128)S(1)}, u32[]{:S(2)}, u32[]{:S(2)}) collective-permute-start(f32[16,128]{1,0:T(8,128)S(1)} %get-tuple-element.61), channel_id=1, source_target_pairs={{2,4},{3,5},{6,8},{7,9},{10,12},{11,13},{14,16},{15,17},{18,20},{1... | collective-permute-start | bytes 24584 | tf_op jit(solution)/shard_map/ppermute | solution.py:353
  36.7 5.7 %collective-permute-start.9 = (f32[16,128]{1,0:T(8,128)S(1)}, f32[16,128]{1,0:T(8,128)S(1)}, u32[]{:S(2)}, u32[]{:S(2)}) collective-permute-start(f32[16,128]{1,0:T(8,128)S(1)} %get-tuple-element.62), channel_id=1, source_target_pairs={{1,2},{3,4},{5,6},{7,8},{9,10},{11,12},{13,14},{15,16},{17,18},{19... | collective-permute-start | bytes 24584 | tf_op jit(solution)/shard_map/ppermute | solution.py:353
  46.5 5.2 %collective-permute-start.13 = (f32[16,128]{1,0:T(8,128)S(1)}, f32[16,128]{1,0:T(8,128)S(1)}, u32[]{:S(2)}, u32[]{:S(2)}) collective-permute-start(f32[16,128]{1,0:T(8,128)S(1)} %get-tuple-element.67), channel_id=1, source_target_pairs={{1,2},{3,4},{5,6},{7,8},{9,10},{11,12},{13,14},{15,16},{17,18},{19... | collective-permute-start | bytes 24584 | tf_op jit(solution)/shard_map/ppermute | solution.py:353
  51.7 1.7 %collective-permute-start.14 = (f32[16,128]{1,0:T(8,128)S(1)}, f32[16,128]{1,0:T(8,128)S(1)}, u32[]{:S(2)}, u32[]{:S(2)}) collective-permute-start(f32[16,128]{1,0:T(8,128)S(1)} %get-tuple-element.68), channel_id=1, source_target_pairs={{0,2},{1,3},{4,6},{5,7},{8,10},{9,11},{12,14},{13,15},{16,18},{17,... | collective-permute-start | bytes 24584 | tf_op jit(solution)/shard_map/ppermute | solution.py:353
  56.1 1.8 %collective-permute-start.16 = (f32[16,128]{1,0:T(8,128)S(1)}, f32[16,128]{1,0:T(8,128)S(1)}, u32[]{:S(2)}, u32[]{:S(2)}) collective-permute-start(f32[16,128]{1,0:T(8,128)S(1)} %get-tuple-element.71), channel_id=1, source_target_pairs={{2,4},{3,5},{6,8},{7,9},{10,12},{11,13},{14,16},{15,17},{18,20},{1... | collective-permute-start | bytes 24584 | tf_op jit(solution)/shard_map/ppermute | solution.py:353
  57.8 4.9 %collective-permute-start.17 = (f32[16,128]{1,0:T(8,128)S(1)}, f32[16,128]{1,0:T(8,128)S(1)}, u32[]{:S(2)}, u32[]{:S(2)}) collective-permute-start(f32[16,128]{1,0:T(8,128)S(1)} %get-tuple-element.72), channel_id=1, source_target_pairs={{1,2},{3,4},{5,6},{7,8},{9,10},{11,12},{13,14},{15,16},{17,18},{19... | collective-permute-start | bytes 24584 | tf_op jit(solution)/shard_map/ppermute | solution.py:353
  63.8 1.4 %collective-permute-done.16.g0 = f32[16,128]{1,0:T(8,128)S(1)} collective-permute-done((f32[16,128]{1,0:T(8,128)S(1)}, f32[16,128]{1,0:T(8,128)S(1)}, u32[]{:S(2)}, u32[]{:S(2)}) %collective-permute-start.16) | collective-permute-done | bytes 8224 | tf_op jit(solution)/shard_map/ppermute | solution.py:353
  65.2 1.1 %collective-permute-done.17.g1 = f32[16,128]{1,0:T(8,128)S(1)} collective-permute-done((f32[16,128]{1,0:T(8,128)S(1)}, f32[16,128]{1,0:T(8,128)S(1)}, u32[]{:S(2)}, u32[]{:S(2)}) %collective-permute-start.17) | collective-permute-done | bytes 8224 | tf_op jit(solution)/shard_map/ppermute | solution.py:353
  68.0 4.0 %collective-permute-start.21 = (f32[16,128]{1,0:T(8,128)S(1)}, f32[16,128]{1,0:T(8,128)S(1)}, u32[]{:S(2)}, u32[]{:S(2)}) collective-permute-start(f32[16,128]{1,0:T(8,128)S(1)} %get-tuple-element.77), channel_id=1, source_target_pairs={{1,2},{3,4},{5,6},{7,8},{9,10},{11,12},{13,14},{15,16},{17,18},{19... | collective-permute-start | bytes 24584 | tf_op jit(solution)/shard_map/ppermute | solution.py:353
  72.1 1.7 %collective-permute-start.22 = (f32[16,128]{1,0:T(8,128)S(1)}, f32[16,128]{1,0:T(8,128)S(1)}, u32[]{:S(2)}, u32[]{:S(2)}) collective-permute-start(f32[16,128]{1,0:T(8,128)S(1)} %get-tuple-element.78), channel_id=1, source_target_pairs={{0,2},{1,3},{4,6},{5,7},{8,10},{9,11},{12,14},{13,15},{16,18},{17,... | collective-permute-start | bytes 24584 | tf_op jit(solution)/shard_map/ppermute | solution.py:353
  74.6 1.6 %collective-permute-done.20.g0 = f32[16,128]{1,0:T(8,128)S(1)} collective-permute-done((f32[16,128]{1,0:T(8,128)S(1)}, f32[16,128]{1,0:T(8,128)S(1)}, u32[]{:S(2)}, u32[]{:S(2)}) %collective-permute-start.20) | collective-permute-done | bytes 8224 | tf_op jit(solution)/shard_map/ppermute | solution.py:353
  77.2 1.8 %collective-permute-start.24 = (f32[16,128]{1,0:T(8,128)S(1)}, f32[16,128]{1,0:T(8,128)S(1)}, u32[]{:S(2)}, u32[]{:S(2)}) collective-permute-start(f32[16,128]{1,0:T(8,128)S(1)} %get-tuple-element.81), channel_id=1, source_target_pairs={{2,4},{3,5},{6,8},{7,9},{10,12},{11,13},{14,16},{15,17},{18,20},{1... | collective-permute-start | bytes 24584 | tf_op jit(solution)/shard_map/ppermute | solution.py:353
  79.0 4.0 %collective-permute-start.25 = (f32[16,128]{1,0:T(8,128)S(1)}, f32[16,128]{1,0:T(8,128)S(1)}, u32[]{:S(2)}, u32[]{:S(2)}) collective-permute-start(f32[16,128]{1,0:T(8,128)S(1)} %get-tuple-element.82), channel_id=1, source_target_pairs={{1,2},{3,4},{5,6},{7,8},{9,10},{11,12},{13,14},{15,16},{17,18},{19... | collective-permute-start | bytes 24584 | tf_op jit(solution)/shard_map/ppermute | solution.py:353
  83.9 2.5 %collective-permute-done.24.g0 = f32[16,128]{1,0:T(8,128)S(1)} collective-permute-done((f32[16,128]{1,0:T(8,128)S(1)}, f32[16,128]{1,0:T(8,128)S(1)}, u32[]{:S(2)}, u32[]{:S(2)}) %collective-permute-start.24) | collective-permute-done | bytes 8224 | tf_op jit(solution)/shard_map/ppermute | solution.py:353
  86.4 1.1 %collective-permute-done.25.g1 = f32[16,128]{1,0:T(8,128)S(1)} collective-permute-done((f32[16,128]{1,0:T(8,128)S(1)}, f32[16,128]{1,0:T(8,128)S(1)}, u32[]{:S(2)}, u32[]{:S(2)}) %collective-permute-start.25) | collective-permute-done | bytes 8224 | tf_op jit(solution)/shard_map/ppermute | solution.py:353
  87.5 1.4 %last_part.1 = f32[128,32]{1,0:T(8,128)} custom-call(s32[2232]{0:T(1024)S(4)} %get-tuple-element.48.table, bf16[160,128,256]{2,1,0:T(8,128)(2,1)S(1)} %get-tuple-element.49.turned, f32[32,128]{1,0:T(8,128)S(1)} %near_part.11.near, f32[16,128]{1,0:T(8,128)S(1)} %collective-permute-done.24.g0, f32[16,128]{1,0:T(8,128)S(1)} %collective-permute-done.25.g1, ...), custom_call_target="tpu_custom_call" | custom-call | tf_op jit(solution)/shard_map/last_part/pallas_call | solution.py:418
  88.9 5.9 %all-to-all-start = ((f32[128,1,32]{2,1,0:T(1,128)}), f32[128,1,32]{2,1,0:T(1,128)S(1)}, u32[]{:S(2)}, u32[]{:S(2)}) async-start(f32[128,1,32]{2,1,0:T(1,128)} %bitcast.3), calls=%async_computation | async-start | bytes 131072 | tf_op jit(solution)/shard_map/all_to_all | solution.py:427
  95.5 8.7 %all-to-all-done = f32[128,1,32]{2,1,0:T(1,128)S(1)} async-done(((f32[128,1,32]{2,1,0:T(1,128)}), f32[128,1,32]{2,1,0:T(1,128)S(1)}, u32[]{:S(2)}, u32[]{:S(2)}) %all-to-all-start) | async-done | bytes 16416 | tf_op jit(solution)/shard_map/all_to_all | solution.py:427
  104.2 1.3 %finish.1 = f32[32,128]{1,0:T(8,128)} custom-call(f32[1]{0:T(128)S(6)} %copy.9.step, f32[128,32]{1,0:T(8,128)S(1)} %bitcast.6, f32[32,128]{1,0:T(8,128)S(1)} %get-tuple-element.46.field.concentration, f32[32,128]{1,0:T(8,128)S(1)} %get-tuple-element.55.field.rest_0_, f32[32,128]{1,0:T(8,128)S(1)} %get-tuple-element.60.field.rest_1_, ...), custom_call_target="tpu_custom_call" | custom-call | tf_op jit(solution)/shard_map/finish/pallas_call | solution.py:428
  (50 shorter events, 17.5 us)
Async XLA Ops:
  0.8 17.7 %collective-permute-start = (f32[16,128]{1,0:T(8,128)S(1)}, f32[16,128]{1,0:T(8,128)S(1)}, u32[]{:S(2)}, u32[]{:S(2)}) collective-permute-start(f32[16,128]{1,0:T(8,128)S(1)} %get-tuple-element.51), channel_id=1, source_target_pairs={{2,4},{3,5},{6,8},{7,9},{10,12},{11,13},{14,16},{15,17},{18,20},{1... | collective-permute-start | bytes 24584 | tf_op jit(solution)/shard_map/ppermute | solution.py:353
  9.7 8.8 %collective-permute-start.1 = (f32[16,128]{1,0:T(8,128)S(1)}, f32[16,128]{1,0:T(8,128)S(1)}, u32[]{:S(2)}, u32[]{:S(2)}) collective-permute-start(f32[16,128]{1,0:T(8,128)S(1)} %get-tuple-element.52), channel_id=1, source_target_pairs={{1,2},{3,4},{5,6},{7,8},{9,10},{11,12},{13,14},{15,16},{17,18},{19... | collective-permute-start | bytes 24584 | tf_op jit(solution)/shard_map/ppermute | solution.py:353
  9.7 8.8 %collective-permute-start.2 = (f32[16,128]{1,0:T(8,128)S(1)}, f32[16,128]{1,0:T(8,128)S(1)}, u32[]{:S(2)}, u32[]{:S(2)}) collective-permute-start(f32[16,128]{1,0:T(8,128)S(1)} %get-tuple-element.53), channel_id=1, source_target_pairs={{0,2},{1,3},{4,6},{5,7},{8,10},{9,11},{12,14},{13,15},{16,18},{17,... | collective-permute-start | bytes 24584 | tf_op jit(solution)/shard_map/ppermute | solution.py:353
  10.9 7.6 %collective-permute-start.3 = (f32[16,128]{1,0:T(8,128)S(1)}, f32[16,128]{1,0:T(8,128)S(1)}, u32[]{:S(2)}, u32[]{:S(2)}) collective-permute-start(f32[16,128]{1,0:T(8,128)S(1)} %get-tuple-element.54), channel_id=1, source_target_pairs={{0,1},{2,3},{4,5},{6,7},{8,9},{10,11},{12,13},{14,15},{16,17},{18,... | collective-permute-start | bytes 24584 | tf_op jit(solution)/shard_map/ppermute | solution.py:353
  19.2 9.2 %collective-permute-start.4 = (f32[16,128]{1,0:T(8,128)S(1)}, f32[16,128]{1,0:T(8,128)S(1)}, u32[]{:S(2)}, u32[]{:S(2)}) collective-permute-start(f32[16,128]{1,0:T(8,128)S(1)} %get-tuple-element.56), channel_id=1, source_target_pairs={{2,4},{3,5},{6,8},{7,9},{10,12},{11,13},{14,16},{15,17},{18,20},{1... | collective-permute-start | bytes 24584 | tf_op jit(solution)/shard_map/ppermute | solution.py:353
  25.7 8.5 %collective-permute-start.5 = (f32[16,128]{1,0:T(8,128)S(1)}, f32[16,128]{1,0:T(8,128)S(1)}, u32[]{:S(2)}, u32[]{:S(2)}) collective-permute-start(f32[16,128]{1,0:T(8,128)S(1)} %get-tuple-element.57), channel_id=1, source_target_pairs={{1,2},{3,4},{5,6},{7,8},{9,10},{11,12},{13,14},{15,16},{17,18},{19... | collective-permute-start | bytes 24584 | tf_op jit(solution)/shard_map/ppermute | solution.py:353
  26.6 7.6 %collective-permute-start.6 = (f32[16,128]{1,0:T(8,128)S(1)}, f32[16,128]{1,0:T(8,128)S(1)}, u32[]{:S(2)}, u32[]{:S(2)}) collective-permute-start(f32[16,128]{1,0:T(8,128)S(1)} %get-tuple-element.58), channel_id=1, source_target_pairs={{0,2},{1,3},{4,6},{5,7},{8,10},{9,11},{12,14},{13,15},{16,18},{17,... | collective-permute-start | bytes 24584 | tf_op jit(solution)/shard_map/ppermute | solution.py:353
  27.1 7.2 %collective-permute-start.7 = (f32[16,128]{1,0:T(8,128)S(1)}, f32[16,128]{1,0:T(8,128)S(1)}, u32[]{:S(2)}, u32[]{:S(2)}) collective-permute-start(f32[16,128]{1,0:T(8,128)S(1)} %get-tuple-element.59), channel_id=1, source_target_pairs={{0,1},{2,3},{4,5},{6,7},{8,9},{10,11},{12,13},{14,15},{16,17},{18,... | collective-permute-start | bytes 24584 | tf_op jit(solution)/shard_map/ppermute | solution.py:353
  34.9 8.3 %collective-permute-start.10 = (f32[16,128]{1,0:T(8,128)S(1)}, f32[16,128]{1,0:T(8,128)S(1)}, u32[]{:S(2)}, u32[]{:S(2)}) collective-permute-start(f32[16,128]{1,0:T(8,128)S(1)} %get-tuple-element.63), channel_id=1, source_target_pairs={{0,2},{1,3},{4,6},{5,7},{8,10},{9,11},{12,14},{13,15},{16,18},{17,... | collective-permute-start | bytes 24584 | tf_op jit(solution)/shard_map/ppermute | solution.py:353
  35.0 8.2 %collective-permute-start.11 = (f32[16,128]{1,0:T(8,128)S(1)}, f32[16,128]{1,0:T(8,128)S(1)}, u32[]{:S(2)}, u32[]{:S(2)}) collective-permute-start(f32[16,128]{1,0:T(8,128)S(1)} %get-tuple-element.64), channel_id=1, source_target_pairs={{0,1},{2,3},{4,5},{6,7},{8,9},{10,11},{12,13},{14,15},{16,17},{18,... | collective-permute-start | bytes 24584 | tf_op jit(solution)/shard_map/ppermute | solution.py:353
  35.1 9.2 %collective-permute-start.8 = (f32[16,128]{1,0:T(8,128)S(1)}, f32[16,128]{1,0:T(8,128)S(1)}, u32[]{:S(2)}, u32[]{:S(2)}) collective-permute-start(f32[16,128]{1,0:T(8,128)S(1)} %get-tuple-element.61), channel_id=1, source_target_pairs={{2,4},{3,5},{6,8},{7,9},{10,12},{11,13},{14,16},{15,17},{18,20},{1... | collective-permute-start | bytes 24584 | tf_op jit(solution)/shard_map/ppermute | solution.py:353
  36.7 8.5 %collective-permute-start.9 = (f32[16,128]{1,0:T(8,128)S(1)}, f32[16,128]{1,0:T(8,128)S(1)}, u32[]{:S(2)}, u32[]{:S(2)}) collective-permute-start(f32[16,128]{1,0:T(8,128)S(1)} %get-tuple-element.62), channel_id=1, source_target_pairs={{1,2},{3,4},{5,6},{7,8},{9,10},{11,12},{13,14},{15,16},{17,18},{19... | collective-permute-start | bytes 24584 | tf_op jit(solution)/shard_map/ppermute | solution.py:353
  45.9 9.2 %collective-permute-start.12 = (f32[16,128]{1,0:T(8,128)S(1)}, f32[16,128]{1,0:T(8,128)S(1)}, u32[]{:S(2)}, u32[]{:S(2)}) collective-permute-start(f32[16,128]{1,0:T(8,128)S(1)} %get-tuple-element.66), channel_id=1, source_target_pairs={{2,4},{3,5},{6,8},{7,9},{10,12},{11,13},{14,16},{15,17},{18,20},{1... | collective-permute-start | bytes 24584 | tf_op jit(solution)/shard_map/ppermute | solution.py:353
  46.5 8.6 %collective-permute-start.13 = (f32[16,128]{1,0:T(8,128)S(1)}, f32[16,128]{1,0:T(8,128)S(1)}, u32[]{:S(2)}, u32[]{:S(2)}) collective-permute-start(f32[16,128]{1,0:T(8,128)S(1)} %get-tuple-element.67), channel_id=1, source_target_pairs={{1,2},{3,4},{5,6},{7,8},{9,10},{11,12},{13,14},{15,16},{17,18},{19... | collective-permute-start | bytes 24584 | tf_op jit(solution)/shard_map/ppermute | solution.py:353
  56.1 9.2 %collective-permute-start.16 = (f32[16,128]{1,0:T(8,128)S(1)}, f32[16,128]{1,0:T(8,128)S(1)}, u32[]{:S(2)}, u32[]{:S(2)}) collective-permute-start(f32[16,128]{1,0:T(8,128)S(1)} %get-tuple-element.71), channel_id=1, source_target_pairs={{2,4},{3,5},{6,8},{7,9},{10,12},{11,13},{14,16},{15,17},{18,20},{1... | collective-permute-start | bytes 24584 | tf_op jit(solution)/shard_map/ppermute | solution.py:353
  57.8 8.5 %collective-permute-start.17 = (f32[16,128]{1,0:T(8,128)S(1)}, f32[16,128]{1,0:T(8,128)S(1)}, u32[]{:S(2)}, u32[]{:S(2)}) collective-permute-start(f32[16,128]{1,0:T(8,128)S(1)} %get-tuple-element.72), channel_id=1, source_target_pairs={{1,2},{3,4},{5,6},{7,8},{9,10},{11,12},{13,14},{15,16},{17,18},{19... | collective-permute-start | bytes 24584 | tf_op jit(solution)/shard_map/ppermute | solution.py:353
  67.0 9.2 %collective-permute-start.20 = (f32[16,128]{1,0:T(8,128)S(1)}, f32[16,128]{1,0:T(8,128)S(1)}, u32[]{:S(2)}, u32[]{:S(2)}) collective-permute-start(f32[16,128]{1,0:T(8,128)S(1)} %get-tuple-element.76), channel_id=1, source_target_pairs={{2,4},{3,5},{6,8},{7,9},{10,12},{11,13},{14,16},{15,17},{18,20},{1... | collective-permute-start | bytes 24584 | tf_op jit(solution)/shard_map/ppermute | solution.py:353
  68.0 8.5 %collective-permute-start.21 = (f32[16,128]{1,0:T(8,128)S(1)}, f32[16,128]{1,0:T(8,128)S(1)}, u32[]{:S(2)}, u32[]{:S(2)}) collective-permute-start(f32[16,128]{1,0:T(8,128)S(1)} %get-tuple-element.77), channel_id=1, source_target_pairs={{1,2},{3,4},{5,6},{7,8},{9,10},{11,12},{13,14},{15,16},{17,18},{19... | collective-permute-start | bytes 24584 | tf_op jit(solution)/shard_map/ppermute | solution.py:353
  72.1 4.5 %collective-permute-start.22 = (f32[16,128]{1,0:T(8,128)S(1)}, f32[16,128]{1,0:T(8,128)S(1)}, u32[]{:S(2)}, u32[]{:S(2)}) collective-permute-start(f32[16,128]{1,0:T(8,128)S(1)} %get-tuple-element.78), channel_id=1, source_target_pairs={{0,2},{1,3},{4,6},{5,7},{8,10},{9,11},{12,14},{13,15},{16,18},{17,... | collective-permute-start | bytes 24584 | tf_op jit(solution)/shard_map/ppermute | solution.py:353
  77.2 9.2 %collective-permute-start.24 = (f32[16,128]{1,0:T(8,128)S(1)}, f32[16,128]{1,0:T(8,128)S(1)}, u32[]{:S(2)}, u32[]{:S(2)}) collective-permute-start(f32[16,128]{1,0:T(8,128)S(1)} %get-tuple-element.81), channel_id=1, source_target_pairs={{2,4},{3,5},{6,8},{7,9},{10,12},{11,13},{14,16},{15,17},{18,20},{1... | collective-permute-start | bytes 24584 | tf_op jit(solution)/shard_map/ppermute | solution.py:353
  79.0 8.5 %collective-permute-start.25 = (f32[16,128]{1,0:T(8,128)S(1)}, f32[16,128]{1,0:T(8,128)S(1)}, u32[]{:S(2)}, u32[]{:S(2)}) collective-permute-start(f32[16,128]{1,0:T(8,128)S(1)} %get-tuple-element.82), channel_id=1, source_target_pairs={{1,2},{3,4},{5,6},{7,8},{9,10},{11,12},{13,14},{15,16},{17,18},{19... | collective-permute-start | bytes 24584 | tf_op jit(solution)/shard_map/ppermute | solution.py:353
  83.0 4.5 %collective-permute-start.26 = (f32[16,128]{1,0:T(8,128)S(1)}, f32[16,128]{1,0:T(8,128)S(1)}, u32[]{:S(2)}, u32[]{:S(2)}) collective-permute-start(f32[16,128]{1,0:T(8,128)S(1)} %get-tuple-element.83), channel_id=1, source_target_pairs={{0,2},{1,3},{4,6},{5,7},{8,10},{9,11},{12,14},{13,15},{16,18},{17,... | collective-permute-start | bytes 24584 | tf_op jit(solution)/shard_map/ppermute | solution.py:353
  83.1 4.4 %collective-permute-start.27 = (f32[16,128]{1,0:T(8,128)S(1)}, f32[16,128]{1,0:T(8,128)S(1)}, u32[]{:S(2)}, u32[]{:S(2)}) collective-permute-start(f32[16,128]{1,0:T(8,128)S(1)} %get-tuple-element.84), channel_id=1, source_target_pairs={{0,1},{2,3},{4,5},{6,7},{8,9},{10,11},{12,13},{14,15},{16,17},{18,... | collective-permute-start | bytes 24584 | tf_op jit(solution)/shard_map/ppermute | solution.py:353
  88.9 15.3 %all-to-all-start = ((f32[128,1,32]{2,1,0:T(1,128)}), f32[128,1,32]{2,1,0:T(1,128)S(1)}, u32[]{:S(2)}, u32[]{:S(2)}) async-start(f32[128,1,32]{2,1,0:T(1,128)} %bitcast.3), calls=%async_computation | async-start | bytes 131072 | tf_op jit(solution)/shard_map/all_to_all | solution.py:427
  (5 other events, 15.7 us)

commit v5 on v4

--- a/solution.py
+++ b/solution.py
@@ -25,6 +25,9 @@
 TABLE = COUNTS + 8
 LINES = 4 * GHOST
 
+FIRST_OFFSETS = (1, 2, -2, -1)
+FIRST_INDICES = (2, 3, 0, 1)
+
 f32 = jnp.float32
 bf16 = jnp.bfloat16
 
@@ -46,7 +49,16 @@
         [e for e in two if e[0] % 4 < 2],
         [e for e in one if e[0] % 2 == 0],
     )
-    return [[(a, b) for a, b in es] + [(b, a) for a, b in es] for es in picked]
+    both = [es + [(b, a) for a, b in es] for es in picked]
+    shifts = [[(p, (p + o) % devices) for p in range(devices)] for o in FIRST_OFFSETS]
+    return shifts, both
+
+
+def places():
+    place = lax.axis_index("dom")
+    even = (place % 2) == 0
+    low = (place % 4) < 2
+    return jnp.where(low, 2, 0), jnp.where(even, 3, 1), jnp.where(even, 1, 3), jnp.where(low, 0, 2)
 
 
 def roles():
@@ -71,10 +83,9 @@
     ]
     for copy in copies:
         copy.start()
-    by = roles()
     for copy in copies:
         copy.wait()
-    write_packets(field, lambda t, g: table[0, by[t], g], (p0, p1, p2, p3))
+    write_packets(field, lambda t, g: table[0, FIRST_INDICES[t], g], (p0, p1, p2, p3))
 
 
 def split(x):
@@ -94,15 +105,7 @@
     for b in range(ROWS // 2):
         fetch(b).start()
     by = roles()
-    place = lax.axis_index("dom")
-    even = (place % 2) == 0
-    low = (place % 4) < 2
-    at = (
-        jnp.where(low, 2, 0),
-        jnp.where(even, 3, 1),
-        jnp.where(even, 1, 3),
-        jnp.where(low, 0, 2),
-    )
+    at = places()
     for t in range(4):
         for g in range(GHOST):
             table[SEND + t * GHOST + g] = send[0, by[t], g]
@@ -154,13 +157,14 @@
     out[...] = slope * field[...] - total
 
 
-def product(table, which, turned, sources, lines, stage, *sums):
+def product(table, which, turned, sources, lines, stage, *sums, order=None):
     base = (NEAR, FAR)[which]
     size = GROUPS[which]
     count = table[COUNTS + which]
     for i, source in enumerate(sources):
         height = source.shape[0]
-        lines[i * height : (i + 1) * height, :] = source[...]
+        start = i * height if order is None else pl.multiple_of(order[i] * height, height)
+        lines[pl.ds(start, height), :] = source[...]
     lines[LINES : LINES + 8, :] = jnp.zeros((8, BLK), f32)
     for ref in sums:
         ref[...] = jnp.zeros((ROWS, BLK), f32)
@@ -184,9 +188,12 @@
     return (sums[0][...] + sums[1][...]) + (sums[2][...] + sums[3][...])
 
 
-def far_part(scale):
+def far_part(first):
     def kernel(table, turned, near, g0, g1, g2, g3, out, p0, p1, p2, p3, *scratch):
-        out[...] = (near[...] - product(table, 1, turned, (g0, g1, g2, g3), *scratch)) * scale
+        at = places()
+        order = [at[q] for q in FIRST_INDICES] if first else None
+        total = product(table, 1, turned, (g0, g1, g2, g3), *scratch, order=order)
+        out[...] = (near[...] - total) * (1.0 if first else SCALE)
         write_packets(out, lambda t, g: table[SEND + t * GHOST + g], (p0, p1, p2, p3))
 
     return kernel
@@ -344,13 +351,13 @@
     return [pl.BlockSpec(memory_space=pltpu.HBM)] * n
 
 
-def shards(pairs, concentration, rate, step, values, columns, lengths, send):
+def shards(shifts, swaps, concentration, rate, step, values, columns, lengths, send):
     devices = BLK
 
-    def exchange(packets):
+    def exchange(packets, k):
         arrived = []
         for t in range(4):
-            arrived.append(lax.ppermute(packets[t], "dom", pairs[t]))
+            arrived.append(lax.ppermute(packets[t], "dom", (swaps if k else shifts)[t]))
         return arrived
 
     send, concentration, rate, values, columns, lengths = (
@@ -366,7 +373,7 @@
         compiler_params=params(),
         name="first_packets",
     )(send, concentration, rate)
-    arrived = exchange(packets)
+    arrived = exchange(packets, 0)
     send = pltpu.with_memory_space_constraint(send, pltpu.SMEM)
     turned, table, near = pl.pallas_call(
         setup,
@@ -395,7 +402,7 @@
 
     for k in range(DEGREE):
         field, *packets = pl.pallas_call(
-            far_part(1.0 if k == 0 else SCALE),
+            far_part(k == 0),
             out_shape=[FIELD] + PACKETS,
             in_specs=smem() + vmem(6),
             out_specs=vmem(5),
@@ -404,7 +411,7 @@
             name="far_part",
         )(table, turned, near, *arrived)
         basis.append(field)
-        arrived = exchange(packets)
+        arrived = exchange(packets, k + 1)
         near = pl.pallas_call(
             near_part,
             out_shape=FIELD,
@@ -436,10 +443,10 @@
 
 
 def solution(mesh):
-    pairs = exchanges(mesh.shape["dom"])
+    shifts, swaps = exchanges(mesh.shape["dom"])
 
     def run(*arrays):
-        return shards(pairs, *arrays)
+        return shards(shifts, swaps, *arrays)
 
     split = P("dom")
     return jax.shard_map(

time: 106 us -> 104 us (0.981)
  starting transfers between devices: 58 us -> 43.2 us
  waiting for transfers between devices: 26.2 us -> 38.4 us
    ppermute x28, starting transfers between devices: 52.1 us -> 38.6 us  [exchange(): arrived.append(lax.ppermute(packets[t], 'dom', (swaps if k else shifts)[t]))]
    ppermute x28, waiting for transfers between devices: 17.6 us -> 29.7 us  [exchange(): arrived.append(lax.ppermute(packets[t], 'dom', (swaps if k else shifts)[t]))]
    all_to_all x1, starting transfers between devices: 5.93 us -> 4.59 us  [shards(): lax.all_to_all(sums, 'dom', split_axis=0, concat_axis=0, tiled=True)]
  transfers between devices with their start and end apart: 29 -> 29, of which waited for: 13 -> 12; matrix products, arithmetic and copies ran while one was open for 0% -> 0% of each run, Pallas kernels for 12% -> 12%
where the time goes in v5:
time: 104 us; the launch traced here: 103 us
  starting transfers between devices  43.2 us (42%)
  waiting for transfers between devices  38.4 us (37%)
  Pallas kernels  20.4 us (20%)
    ppermute x28, starting transfers between devices, exchange(): arrived.append(lax.ppermute(packets[t], 'dom', (swaps if k else shifts)[t]))  38.6 us
    ppermute x28, waiting for transfers between devices, exchange(): arrived.append(lax.ppermute(packets[t], 'dom', (swaps if k else shifts)[t]))  29.7 us
    all_to_all x1, waiting for transfers between devices, shards(): lax.all_to_all(sums, 'dom', split_axis=0, concat_axis=0, tiled=True)  8.67 us
    pallas_call x1, Pallas kernels, shards(): pl.pallas_call(setup, out_shape=[pltpu.VMEM((ENTRIES, BLK, 2 * BLK), bf16...  7.6 us
    pallas_call x6, Pallas kernels, shards(): pl.pallas_call(near_part, out_shape=FIELD, in_specs=smem() + vmem(4), out...  5.2 us
    all_to_all x1, starting transfers between devices, shards(): lax.all_to_all(sums, 'dom', split_axis=0, concat_axis=0, tiled=True)  4.59 us
    pallas_call x6, Pallas kernels, shards(): pl.pallas_call(far_part(k == 0), out_shape=[FIELD] + PACKETS, in_specs=sm...  4.12 us
  transfers between devices with their start and end apart: 29, of which 12 were waited for; matrix products, arithmetic and copies ran while one was open for 0% of the time, Pallas kernels for 12%

profile of v5, /device:TPU:0, one launch (start us, length us, event | category | flops | bytes accessed | tf_op | source)
XLA Modules:
  0.0 102.8 jit_solution(11540153597814738284)
XLA Ops:
  0.9 1.7 %collective-permute-start.1 = (f32[16,128]{1,0:T(8,128)S(1)}, f32[16,128]{1,0:T(8,128)S(1)}, u32[]{:S(2)}, u32[]{:S(2)}) collective-permute-start(f32[16,128]{1,0:T(8,128)S(1)} %get-tuple-element.52), channel_id=1, source_target_pairs={{0,2},{1,3},{2,4},{3,5},{4,6},{5,7},{6,8},{7,9},{8,10},{9,11},{10,... | collective-permute-start | bytes 24584 | tf_op jit(solution)/shard_map/ppermute | solution.py:360
  2.6 7.3 %collective-permute-start.2 = (f32[16,128]{1,0:T(8,128)S(1)}, f32[16,128]{1,0:T(8,128)S(1)}, u32[]{:S(2)}, u32[]{:S(2)}) collective-permute-start(f32[16,128]{1,0:T(8,128)S(1)} %get-tuple-element.53), channel_id=1, source_target_pairs={{0,126},{1,127},{2,0},{3,1},{4,2},{5,3},{6,4},{7,5},{8,6},{9,7},{1... | collective-permute-start | bytes 24584 | tf_op jit(solution)/shard_map/ppermute | solution.py:360
  11.2 7.6 %setup.1 = (bf16[160,128,256]{2,1,0:T(8,128)(2,1)S(1)}, s32[2232]{0:T(1024)S(4)}, f32[32,128]{1,0:T(8,128)S(1)}) custom-call(s32[5,32]{1,0:T(8,128)} %bitcast.8, s32[32]{0:T(128)} %lengths.1, s32[1,4,16]{2,1,0:T(4,128)S(4)} %get-tuple-element.45.send, f32[160,128,128]{2,1,0:T(8,128)} %bitcast.7, f32[32,128]{1,0:T(8,128)S(1)} %get-tuple-element.46.field.concentration, ...), custom_call_target="tpu_custom_call" | custom-call | flops 10000000000 | tf_op jit(solution)/shard_map/setup/pallas_call | solution.py:378
  19.5 1.8 %collective-permute-start.4 = (f32[16,128]{1,0:T(8,128)S(1)}, f32[16,128]{1,0:T(8,128)S(1)}, u32[]{:S(2)}, u32[]{:S(2)}) collective-permute-start(f32[16,128]{1,0:T(8,128)S(1)} %get-tuple-element.56), channel_id=1, source_target_pairs={{2,4},{3,5},{6,8},{7,9},{10,12},{11,13},{14,16},{15,17},{18,20},{1... | collective-permute-start | bytes 24584 | tf_op jit(solution)/shard_map/ppermute | solution.py:360
  21.3 4.2 %collective-permute-start.5 = (f32[16,128]{1,0:T(8,128)S(1)}, f32[16,128]{1,0:T(8,128)S(1)}, u32[]{:S(2)}, u32[]{:S(2)}) collective-permute-start(f32[16,128]{1,0:T(8,128)S(1)} %get-tuple-element.57), channel_id=1, source_target_pairs={{1,2},{3,4},{5,6},{7,8},{9,10},{11,12},{13,14},{15,16},{17,18},{19... | collective-permute-start | bytes 24584 | tf_op jit(solution)/shard_map/ppermute | solution.py:360
  26.4 2.2 %collective-permute-done.4.g0 = f32[16,128]{1,0:T(8,128)S(1)} collective-permute-done((f32[16,128]{1,0:T(8,128)S(1)}, f32[16,128]{1,0:T(8,128)S(1)}, u32[]{:S(2)}, u32[]{:S(2)}) %collective-permute-start.4) | collective-permute-done | bytes 8224 | tf_op jit(solution)/shard_map/ppermute | solution.py:360
  30.7 4.6 %collective-permute-start.8 = (f32[16,128]{1,0:T(8,128)S(1)}, f32[16,128]{1,0:T(8,128)S(1)}, u32[]{:S(2)}, u32[]{:S(2)}) collective-permute-start(f32[16,128]{1,0:T(8,128)S(1)} %get-tuple-element.61), channel_id=1, source_target_pairs={{2,4},{3,5},{6,8},{7,9},{10,12},{11,13},{14,16},{15,17},{18,20},{1... | collective-permute-start | bytes 24584 | tf_op jit(solution)/shard_map/ppermute | solution.py:360
  35.3 2.7 %collective-permute-start.9 = (f32[16,128]{1,0:T(8,128)S(1)}, f32[16,128]{1,0:T(8,128)S(1)}, u32[]{:S(2)}, u32[]{:S(2)}) collective-permute-start(f32[16,128]{1,0:T(8,128)S(1)} %get-tuple-element.62), channel_id=1, source_target_pairs={{1,2},{3,4},{5,6},{7,8},{9,10},{11,12},{13,14},{15,16},{17,18},{19... | collective-permute-start | bytes 24584 | tf_op jit(solution)/shard_map/ppermute | solution.py:360
  39.9 4.0 %collective-permute-done.9.g1 = f32[16,128]{1,0:T(8,128)S(1)} collective-permute-done((f32[16,128]{1,0:T(8,128)S(1)}, f32[16,128]{1,0:T(8,128)S(1)}, u32[]{:S(2)}, u32[]{:S(2)}) %collective-permute-start.9) | collective-permute-done | bytes 8224 | tf_op jit(solution)/shard_map/ppermute | solution.py:360
  45.2 2.2 %collective-permute-start.13 = (f32[16,128]{1,0:T(8,128)S(1)}, f32[16,128]{1,0:T(8,128)S(1)}, u32[]{:S(2)}, u32[]{:S(2)}) collective-permute-start(f32[16,128]{1,0:T(8,128)S(1)} %get-tuple-element.67), channel_id=1, source_target_pairs={{1,2},{3,4},{5,6},{7,8},{9,10},{11,12},{13,14},{15,16},{17,18},{19... | collective-permute-start | bytes 24584 | tf_op jit(solution)/shard_map/ppermute | solution.py:360
  47.4 1.7 %collective-permute-start.14 = (f32[16,128]{1,0:T(8,128)S(1)}, f32[16,128]{1,0:T(8,128)S(1)}, u32[]{:S(2)}, u32[]{:S(2)}) collective-permute-start(f32[16,128]{1,0:T(8,128)S(1)} %get-tuple-element.68), channel_id=1, source_target_pairs={{0,2},{1,3},{4,6},{5,7},{8,10},{9,11},{12,14},{13,15},{16,18},{17,... | collective-permute-start | bytes 24584 | tf_op jit(solution)/shard_map/ppermute | solution.py:360
  49.9 3.9 %collective-permute-done.12.g0 = f32[16,128]{1,0:T(8,128)S(1)} collective-permute-done((f32[16,128]{1,0:T(8,128)S(1)}, f32[16,128]{1,0:T(8,128)S(1)}, u32[]{:S(2)}, u32[]{:S(2)}) %collective-permute-start.12) | collective-permute-done | bytes 8224 | tf_op jit(solution)/shard_map/ppermute | solution.py:360
  54.5 2.0 %collective-permute-start.16 = (f32[16,128]{1,0:T(8,128)S(1)}, f32[16,128]{1,0:T(8,128)S(1)}, u32[]{:S(2)}, u32[]{:S(2)}) collective-permute-start(f32[16,128]{1,0:T(8,128)S(1)} %get-tuple-element.71), channel_id=1, source_target_pairs={{2,4},{3,5},{6,8},{7,9},{10,12},{11,13},{14,16},{15,17},{18,20},{1... | collective-permute-start | bytes 24584 | tf_op jit(solution)/shard_map/ppermute | solution.py:360
  56.5 1.5 %collective-permute-start.17 = (f32[16,128]{1,0:T(8,128)S(1)}, f32[16,128]{1,0:T(8,128)S(1)}, u32[]{:S(2)}, u32[]{:S(2)}) collective-permute-start(f32[16,128]{1,0:T(8,128)S(1)} %get-tuple-element.72), channel_id=1, source_target_pairs={{1,2},{3,4},{5,6},{7,8},{9,10},{11,12},{13,14},{15,16},{17,18},{19... | collective-permute-start | bytes 24584 | tf_op jit(solution)/shard_map/ppermute | solution.py:360
  59.4 4.2 %collective-permute-done.16.g0 = f32[16,128]{1,0:T(8,128)S(1)} collective-permute-done((f32[16,128]{1,0:T(8,128)S(1)}, f32[16,128]{1,0:T(8,128)S(1)}, u32[]{:S(2)}, u32[]{:S(2)}) %collective-permute-start.16) | collective-permute-done | bytes 8224 | tf_op jit(solution)/shard_map/ppermute | solution.py:360
  63.7 1.4 %collective-permute-done.17.g1 = f32[16,128]{1,0:T(8,128)S(1)} collective-permute-done((f32[16,128]{1,0:T(8,128)S(1)}, f32[16,128]{1,0:T(8,128)S(1)}, u32[]{:S(2)}, u32[]{:S(2)}) %collective-permute-start.17) | collective-permute-done | bytes 8224 | tf_op jit(solution)/shard_map/ppermute | solution.py:360
  67.4 1.7 %collective-permute-start.22 = (f32[16,128]{1,0:T(8,128)S(1)}, f32[16,128]{1,0:T(8,128)S(1)}, u32[]{:S(2)}, u32[]{:S(2)}) collective-permute-start(f32[16,128]{1,0:T(8,128)S(1)} %get-tuple-element.78), channel_id=1, source_target_pairs={{0,2},{1,3},{4,6},{5,7},{8,10},{9,11},{12,14},{13,15},{16,18},{17,... | collective-permute-start | bytes 24584 | tf_op jit(solution)/shard_map/ppermute | solution.py:360
  69.9 5.0 %collective-permute-done.20.g0 = f32[16,128]{1,0:T(8,128)S(1)} collective-permute-done((f32[16,128]{1,0:T(8,128)S(1)}, f32[16,128]{1,0:T(8,128)S(1)}, u32[]{:S(2)}, u32[]{:S(2)}) %collective-permute-start.20) | collective-permute-done | bytes 8224 | tf_op jit(solution)/shard_map/ppermute | solution.py:360
  75.7 2.0 %collective-permute-start.24 = (f32[16,128]{1,0:T(8,128)S(1)}, f32[16,128]{1,0:T(8,128)S(1)}, u32[]{:S(2)}, u32[]{:S(2)}) collective-permute-start(f32[16,128]{1,0:T(8,128)S(1)} %get-tuple-element.81), channel_id=1, source_target_pairs={{2,4},{3,5},{6,8},{7,9},{10,12},{11,13},{14,16},{15,17},{18,20},{1... | collective-permute-start | bytes 24584 | tf_op jit(solution)/shard_map/ppermute | solution.py:360
  79.5 5.3 %collective-permute-done.24.g0 = f32[16,128]{1,0:T(8,128)S(1)} collective-permute-done((f32[16,128]{1,0:T(8,128)S(1)}, f32[16,128]{1,0:T(8,128)S(1)}, u32[]{:S(2)}, u32[]{:S(2)}) %collective-permute-start.24) | collective-permute-done | bytes 8224 | tf_op jit(solution)/shard_map/ppermute | solution.py:360
  84.8 1.4 %collective-permute-done.25.g1 = f32[16,128]{1,0:T(8,128)S(1)} collective-permute-done((f32[16,128]{1,0:T(8,128)S(1)}, f32[16,128]{1,0:T(8,128)S(1)}, u32[]{:S(2)}, u32[]{:S(2)}) %collective-permute-start.25) | collective-permute-done | bytes 8224 | tf_op jit(solution)/shard_map/ppermute | solution.py:360
  86.2 1.4 %last_part.1 = f32[128,32]{1,0:T(8,128)} custom-call(s32[2232]{0:T(1024)S(4)} %get-tuple-element.48.table, bf16[160,128,256]{2,1,0:T(8,128)(2,1)S(1)} %get-tuple-element.49.turned, f32[32,128]{1,0:T(8,128)S(1)} %near_part.11.near, f32[16,128]{1,0:T(8,128)S(1)} %collective-permute-done.24.g0, f32[16,128]{1,0:T(8,128)S(1)} %collective-permute-done.25.g1, ...), custom_call_target="tpu_custom_call" | custom-call | tf_op jit(solution)/shard_map/last_part/pallas_call | solution.py:425
  87.6 4.6 %all-to-all-start = ((f32[128,1,32]{2,1,0:T(1,128)}), f32[128,1,32]{2,1,0:T(1,128)S(1)}, u32[]{:S(2)}, u32[]{:S(2)}) async-start(f32[128,1,32]{2,1,0:T(1,128)} %bitcast.3), calls=%async_computation | async-start | bytes 131072 | tf_op jit(solution)/shard_map/all_to_all | solution.py:434
  92.8 8.7 %all-to-all-done = f32[128,1,32]{2,1,0:T(1,128)S(1)} async-done(((f32[128,1,32]{2,1,0:T(1,128)}), f32[128,1,32]{2,1,0:T(1,128)S(1)}, u32[]{:S(2)}, u32[]{:S(2)}) %all-to-all-start) | async-done | bytes 16416 | tf_op jit(solution)/shard_map/all_to_all | solution.py:434
  (50 shorter events, 19.0 us)
Async XLA Ops:
  0.8 17.9 %collective-permute-start = (f32[16,128]{1,0:T(8,128)S(1)}, f32[16,128]{1,0:T(8,128)S(1)}, u32[]{:S(2)}, u32[]{:S(2)}) collective-permute-start(f32[16,128]{1,0:T(8,128)S(1)} %get-tuple-element.51), channel_id=1, source_target_pairs={{0,1},{1,2},{2,3},{3,4},{4,5},{5,6},{6,7},{7,8},{8,9},{9,10},{10,1... | collective-permute-start | bytes 24584 | tf_op jit(solution)/shard_map/ppermute | solution.py:360
  0.9 17.9 %collective-permute-start.1 = (f32[16,128]{1,0:T(8,128)S(1)}, f32[16,128]{1,0:T(8,128)S(1)}, u32[]{:S(2)}, u32[]{:S(2)}) collective-permute-start(f32[16,128]{1,0:T(8,128)S(1)} %get-tuple-element.52), channel_id=1, source_target_pairs={{0,2},{1,3},{2,4},{3,5},{4,6},{5,7},{6,8},{7,9},{8,10},{9,11},{10,... | collective-permute-start | bytes 24584 | tf_op jit(solution)/shard_map/ppermute | solution.py:360
  2.6 16.2 %collective-permute-start.2 = (f32[16,128]{1,0:T(8,128)S(1)}, f32[16,128]{1,0:T(8,128)S(1)}, u32[]{:S(2)}, u32[]{:S(2)}) collective-permute-start(f32[16,128]{1,0:T(8,128)S(1)} %get-tuple-element.53), channel_id=1, source_target_pairs={{0,126},{1,127},{2,0},{3,1},{4,2},{5,3},{6,4},{7,5},{8,6},{9,7},{1... | collective-permute-start | bytes 24584 | tf_op jit(solution)/shard_map/ppermute | solution.py:360
  9.8 9.0 %collective-permute-start.3 = (f32[16,128]{1,0:T(8,128)S(1)}, f32[16,128]{1,0:T(8,128)S(1)}, u32[]{:S(2)}, u32[]{:S(2)}) collective-permute-start(f32[16,128]{1,0:T(8,128)S(1)} %get-tuple-element.54), channel_id=1, source_target_pairs={{0,127},{1,0},{2,1},{3,2},{4,3},{5,4},{6,5},{7,6},{8,7},{9,8},{10,... | collective-permute-start | bytes 24584 | tf_op jit(solution)/shard_map/ppermute | solution.py:360
  19.5 9.2 %collective-permute-start.4 = (f32[16,128]{1,0:T(8,128)S(1)}, f32[16,128]{1,0:T(8,128)S(1)}, u32[]{:S(2)}, u32[]{:S(2)}) collective-permute-start(f32[16,128]{1,0:T(8,128)S(1)} %get-tuple-element.56), channel_id=1, source_target_pairs={{2,4},{3,5},{6,8},{7,9},{10,12},{11,13},{14,16},{15,17},{18,20},{1... | collective-permute-start | bytes 24584 | tf_op jit(solution)/shard_map/ppermute | solution.py:360
  21.3 8.5 %collective-permute-start.5 = (f32[16,128]{1,0:T(8,128)S(1)}, f32[16,128]{1,0:T(8,128)S(1)}, u32[]{:S(2)}, u32[]{:S(2)}) collective-permute-start(f32[16,128]{1,0:T(8,128)S(1)} %get-tuple-element.57), channel_id=1, source_target_pairs={{1,2},{3,4},{5,6},{7,8},{9,10},{11,12},{13,14},{15,16},{17,18},{19... | collective-permute-start | bytes 24584 | tf_op jit(solution)/shard_map/ppermute | solution.py:360
  30.5 8.3 %collective-permute-start.10 = (f32[16,128]{1,0:T(8,128)S(1)}, f32[16,128]{1,0:T(8,128)S(1)}, u32[]{:S(2)}, u32[]{:S(2)}) collective-permute-start(f32[16,128]{1,0:T(8,128)S(1)} %get-tuple-element.63), channel_id=1, source_target_pairs={{0,2},{1,3},{4,6},{5,7},{8,10},{9,11},{12,14},{13,15},{16,18},{17,... | collective-permute-start | bytes 24584 | tf_op jit(solution)/shard_map/ppermute | solution.py:360
  30.6 8.2 %collective-permute-start.11 = (f32[16,128]{1,0:T(8,128)S(1)}, f32[16,128]{1,0:T(8,128)S(1)}, u32[]{:S(2)}, u32[]{:S(2)}) collective-permute-start(f32[16,128]{1,0:T(8,128)S(1)} %get-tuple-element.64), channel_id=1, source_target_pairs={{0,1},{2,3},{4,5},{6,7},{8,9},{10,11},{12,13},{14,15},{16,17},{18,... | collective-permute-start | bytes 24584 | tf_op jit(solution)/shard_map/ppermute | solution.py:360
  30.7 9.2 %collective-permute-start.8 = (f32[16,128]{1,0:T(8,128)S(1)}, f32[16,128]{1,0:T(8,128)S(1)}, u32[]{:S(2)}, u32[]{:S(2)}) collective-permute-start(f32[16,128]{1,0:T(8,128)S(1)} %get-tuple-element.61), channel_id=1, source_target_pairs={{2,4},{3,5},{6,8},{7,9},{10,12},{11,13},{14,16},{15,17},{18,20},{1... | collective-permute-start | bytes 24584 | tf_op jit(solution)/shard_map/ppermute | solution.py:360
  35.3 8.5 %collective-permute-start.9 = (f32[16,128]{1,0:T(8,128)S(1)}, f32[16,128]{1,0:T(8,128)S(1)}, u32[]{:S(2)}, u32[]{:S(2)}) collective-permute-start(f32[16,128]{1,0:T(8,128)S(1)} %get-tuple-element.62), channel_id=1, source_target_pairs={{1,2},{3,4},{5,6},{7,8},{9,10},{11,12},{13,14},{15,16},{17,18},{19... | collective-permute-start | bytes 24584 | tf_op jit(solution)/shard_map/ppermute | solution.py:360
  44.5 9.2 %collective-permute-start.12 = (f32[16,128]{1,0:T(8,128)S(1)}, f32[16,128]{1,0:T(8,128)S(1)}, u32[]{:S(2)}, u32[]{:S(2)}) collective-permute-start(f32[16,128]{1,0:T(8,128)S(1)} %get-tuple-element.66), channel_id=1, source_target_pairs={{2,4},{3,5},{6,8},{7,9},{10,12},{11,13},{14,16},{15,17},{18,20},{1... | collective-permute-start | bytes 24584 | tf_op jit(solution)/shard_map/ppermute | solution.py:360
  45.2 8.6 %collective-permute-start.13 = (f32[16,128]{1,0:T(8,128)S(1)}, f32[16,128]{1,0:T(8,128)S(1)}, u32[]{:S(2)}, u32[]{:S(2)}) collective-permute-start(f32[16,128]{1,0:T(8,128)S(1)} %get-tuple-element.67), channel_id=1, source_target_pairs={{1,2},{3,4},{5,6},{7,8},{9,10},{11,12},{13,14},{15,16},{17,18},{19... | collective-permute-start | bytes 24584 | tf_op jit(solution)/shard_map/ppermute | solution.py:360
  54.5 9.2 %collective-permute-start.16 = (f32[16,128]{1,0:T(8,128)S(1)}, f32[16,128]{1,0:T(8,128)S(1)}, u32[]{:S(2)}, u32[]{:S(2)}) collective-permute-start(f32[16,128]{1,0:T(8,128)S(1)} %get-tuple-element.71), channel_id=1, source_target_pairs={{2,4},{3,5},{6,8},{7,9},{10,12},{11,13},{14,16},{15,17},{18,20},{1... | collective-permute-start | bytes 24584 | tf_op jit(solution)/shard_map/ppermute | solution.py:360
  56.5 8.5 %collective-permute-start.17 = (f32[16,128]{1,0:T(8,128)S(1)}, f32[16,128]{1,0:T(8,128)S(1)}, u32[]{:S(2)}, u32[]{:S(2)}) collective-permute-start(f32[16,128]{1,0:T(8,128)S(1)} %get-tuple-element.72), channel_id=1, source_target_pairs={{1,2},{3,4},{5,6},{7,8},{9,10},{11,12},{13,14},{15,16},{17,18},{19... | collective-permute-start | bytes 24584 | tf_op jit(solution)/shard_map/ppermute | solution.py:360
  58.0 7.0 %collective-permute-start.18 = (f32[16,128]{1,0:T(8,128)S(1)}, f32[16,128]{1,0:T(8,128)S(1)}, u32[]{:S(2)}, u32[]{:S(2)}) collective-permute-start(f32[16,128]{1,0:T(8,128)S(1)} %get-tuple-element.73), channel_id=1, source_target_pairs={{0,2},{1,3},{4,6},{5,7},{8,10},{9,11},{12,14},{13,15},{16,18},{17,... | collective-permute-start | bytes 24584 | tf_op jit(solution)/shard_map/ppermute | solution.py:360
  58.4 6.6 %collective-permute-start.19 = (f32[16,128]{1,0:T(8,128)S(1)}, f32[16,128]{1,0:T(8,128)S(1)}, u32[]{:S(2)}, u32[]{:S(2)}) collective-permute-start(f32[16,128]{1,0:T(8,128)S(1)} %get-tuple-element.74), channel_id=1, source_target_pairs={{0,1},{2,3},{4,5},{6,7},{8,9},{10,11},{12,13},{14,15},{16,17},{18,... | collective-permute-start | bytes 24584 | tf_op jit(solution)/shard_map/ppermute | solution.py:360
  65.7 9.2 %collective-permute-start.20 = (f32[16,128]{1,0:T(8,128)S(1)}, f32[16,128]{1,0:T(8,128)S(1)}, u32[]{:S(2)}, u32[]{:S(2)}) collective-permute-start(f32[16,128]{1,0:T(8,128)S(1)} %get-tuple-element.76), channel_id=1, source_target_pairs={{2,4},{3,5},{6,8},{7,9},{10,12},{11,13},{14,16},{15,17},{18,20},{1... | collective-permute-start | bytes 24584 | tf_op jit(solution)/shard_map/ppermute | solution.py:360
  66.5 8.5 %collective-permute-start.21 = (f32[16,128]{1,0:T(8,128)S(1)}, f32[16,128]{1,0:T(8,128)S(1)}, u32[]{:S(2)}, u32[]{:S(2)}) collective-permute-start(f32[16,128]{1,0:T(8,128)S(1)} %get-tuple-element.77), channel_id=1, source_target_pairs={{1,2},{3,4},{5,6},{7,8},{9,10},{11,12},{13,14},{15,16},{17,18},{19... | collective-permute-start | bytes 24584 | tf_op jit(solution)/shard_map/ppermute | solution.py:360
  67.4 7.6 %collective-permute-start.22 = (f32[16,128]{1,0:T(8,128)S(1)}, f32[16,128]{1,0:T(8,128)S(1)}, u32[]{:S(2)}, u32[]{:S(2)}) collective-permute-start(f32[16,128]{1,0:T(8,128)S(1)} %get-tuple-element.78), channel_id=1, source_target_pairs={{0,2},{1,3},{4,6},{5,7},{8,10},{9,11},{12,14},{13,15},{16,18},{17,... | collective-permute-start | bytes 24584 | tf_op jit(solution)/shard_map/ppermute | solution.py:360
  75.7 9.2 %collective-permute-start.24 = (f32[16,128]{1,0:T(8,128)S(1)}, f32[16,128]{1,0:T(8,128)S(1)}, u32[]{:S(2)}, u32[]{:S(2)}) collective-permute-start(f32[16,128]{1,0:T(8,128)S(1)} %get-tuple-element.81), channel_id=1, source_target_pairs={{2,4},{3,5},{6,8},{7,9},{10,12},{11,13},{14,16},{15,17},{18,20},{1... | collective-permute-start | bytes 24584 | tf_op jit(solution)/shard_map/ppermute | solution.py:360
  77.7 8.5 %collective-permute-start.25 = (f32[16,128]{1,0:T(8,128)S(1)}, f32[16,128]{1,0:T(8,128)S(1)}, u32[]{:S(2)}, u32[]{:S(2)}) collective-permute-start(f32[16,128]{1,0:T(8,128)S(1)} %get-tuple-element.82), channel_id=1, source_target_pairs={{1,2},{3,4},{5,6},{7,8},{9,10},{11,12},{13,14},{15,16},{17,18},{19... | collective-permute-start | bytes 24584 | tf_op jit(solution)/shard_map/ppermute | solution.py:360
  78.1 8.1 %collective-permute-start.26 = (f32[16,128]{1,0:T(8,128)S(1)}, f32[16,128]{1,0:T(8,128)S(1)}, u32[]{:S(2)}, u32[]{:S(2)}) collective-permute-start(f32[16,128]{1,0:T(8,128)S(1)} %get-tuple-element.83), channel_id=1, source_target_pairs={{0,2},{1,3},{4,6},{5,7},{8,10},{9,11},{12,14},{13,15},{16,18},{17,... | collective-permute-start | bytes 24584 | tf_op jit(solution)/shard_map/ppermute | solution.py:360
  78.7 7.5 %collective-permute-start.27 = (f32[16,128]{1,0:T(8,128)S(1)}, f32[16,128]{1,0:T(8,128)S(1)}, u32[]{:S(2)}, u32[]{:S(2)}) collective-permute-start(f32[16,128]{1,0:T(8,128)S(1)} %get-tuple-element.84), channel_id=1, source_target_pairs={{0,1},{2,3},{4,5},{6,7},{8,9},{10,11},{12,13},{14,15},{16,17},{18,... | collective-permute-start | bytes 24584 | tf_op jit(solution)/shard_map/ppermute | solution.py:360
  87.6 13.9 %all-to-all-start = ((f32[128,1,32]{2,1,0:T(1,128)}), f32[128,1,32]{2,1,0:T(1,128)S(1)}, u32[]{:S(2)}, u32[]{:S(2)}) async-start(f32[128,1,32]{2,1,0:T(1,128)} %bitcast.3), calls=%async_computation | async-start | bytes 131072 | tf_op jit(solution)/shard_map/all_to_all | solution.py:434
  (5 other events, 25.7 us)

commit v6 on v4

--- a/solution.py
+++ b/solution.py
@@ -15,15 +15,33 @@
 SCALE = 0.25
 PAIRS = [(a, b) for b in range(DEGREE + 1) for a in range(min(b, DEGREE - 1) + 1)]
 
-GROUPS = (80, 56)
+OFFSETS = (-2, -1, 1, 2)
+FIRST_INDICES = (2, 3, 0, 1)
+EIGHT = 8
+EXCHANGES = (
+    ((2, 1), (5, 6)),
+    ((2, 0), (3, 1), (4, 6), (5, 7)),
+    ((6, 8), (8, 6), (7, 9), (9, 7), (2, 4), (4, 2), (3, 5), (5, 3)),
+    ((7, 8), (8, 7), (3, 4), (4, 3), (1, 2), (6, 5)),
+    ((0, 1), (1, 0), (2, 3), (3, 2), (4, 5), (5, 4), (6, 7), (7, 6)),
+    ((0, 2), (1, 3), (6, 4), (7, 5)),
+)
+TURNS = len(EXCHANGES)
+FAR_BY = (2, 3)
+MID_BY = (0, 1, 4, 5)
+
+GROUPS = (80, 32, 40)
 LIST = ENTRIES + max(GROUPS)
 NEAR = 0
 FAR = 3 * LIST
-REST = 6 * LIST
+MID = 6 * LIST
+REST = 9 * LIST
 SEND = REST + 3 * LIST
-COUNTS = SEND + 64
-TABLE = COUNTS + 8
-LINES = 4 * GHOST
+COUNTS = SEND + TURNS * GHOST
+BY = COUNTS + 4
+TABLE = BY + 4
+LINES = TURNS * GHOST
+
 
 f32 = jnp.float32
 bf16 = jnp.bfloat16
@@ -38,27 +56,38 @@
 
 
 def exchanges(devices):
-    two = [(p, (p + 2) % devices) for p in range(devices)]
-    one = [(p, (p + 1) % devices) for p in range(devices)]
-    picked = (
-        [e for e in two if e[0] % 4 >= 2],
-        [e for e in one if e[0] % 2 == 1],
-        [e for e in two if e[0] % 4 < 2],
-        [e for e in one if e[0] % 2 == 0],
-    )
-    return [[(a, b) for a, b in es] + [(b, a) for a, b in es] for es in picked]
-
-
-def roles():
-    place = lax.axis_index("dom")
-    even = (place % 2) == 0
-    low = (place % 4) < 2
-    pick = lambda c, a, b: jnp.where(c, jnp.int32(a), jnp.int32(b))
-    return pick(low, 0, 3), pick(even, 1, 2), pick(low, 3, 0), pick(even, 2, 1)
+    shifts = [[(p, (p + OFFSETS[q]) % devices) for p in range(devices)] for q in FIRST_INDICES]
+    turns = [
+        [((m + a) % devices, (m + b) % devices) for m in range(0, devices, EIGHT) for a, b in edges]
+        for edges in EXCHANGES
+    ]
+    return shifts, turns
+
+
+def looked_up(values):
+    place = lax.axis_index("dom") % EIGHT
+    found = jnp.int32(values[0])
+    for i in range(1, EIGHT):
+        found = jnp.where(place == i, jnp.int32(values[i]), found)
+    return found
+
+
+def arrivals():
+    by = {
+        (b % EIGHT, OFFSETS.index(b - a)): t for t, edges in enumerate(EXCHANGES) for a, b in edges
+    }
+    return [looked_up([by[r, q] for r in range(EIGHT)]) for q in range(4)]
+
+
+def departures():
+    by = {
+        (a % EIGHT, t): OFFSETS.index(b - a) for t, edges in enumerate(EXCHANGES) for a, b in edges
+    }
+    return [looked_up([by.get((r, t), 0) for r in range(EIGHT)]) for t in range(TURNS)]
 
 
 def write_packets(field, row_of, packets):
-    for t in range(4):
+    for t in range(len(packets)):
         for g in range(GHOST):
             packets[t][g : g + 1, :] = field[pl.ds(row_of(t, g), 1), :]
 
@@ -71,10 +100,9 @@
     ]
     for copy in copies:
         copy.start()
-    by = roles()
     for copy in copies:
         copy.wait()
-    write_packets(field, lambda t, g: table[0, by[t], g], (p0, p1, p2, p3))
+    write_packets(field, lambda t, g: table[0, FIRST_INDICES[t], g], (p0, p1, p2, p3))
 
 
 def split(x):
@@ -93,24 +121,18 @@
 
     for b in range(ROWS // 2):
         fetch(b).start()
-    by = roles()
-    place = lax.axis_index("dom")
-    even = (place % 2) == 0
-    low = (place % 4) < 2
-    at = (
-        jnp.where(low, 2, 0),
-        jnp.where(even, 3, 1),
-        jnp.where(even, 1, 3),
-        jnp.where(low, 0, 2),
-    )
-    for t in range(4):
+    by = departures()
+    at = arrivals()
+    for q in range(4):
+        table[BY + q] = at[q]
+    for t in range(TURNS):
         for g in range(GHOST):
             table[SEND + t * GHOST + g] = send[0, by[t], g]
     for copy in copies:
         copy.wait()
 
     def rows(pair, carry):
-        near, far = carry
+        near, far, mid = carry
         fetch(pair).wait()
         for half in range(2):
             b = pair * 2 + half
@@ -123,45 +145,56 @@
                 live = s < length
                 ghost = jnp.logical_and(live, column >= ROWS)
                 home = jnp.logical_and(live, column < ROWS)
-                base = jnp.where(home, NEAR + near, jnp.where(ghost, FAR + far, REST))
+                slow = jnp.logical_or(spot == FAR_BY[0], spot == FAR_BY[1])
+                first = jnp.logical_and(ghost, slow)
+                second = jnp.logical_and(ghost, jnp.logical_not(slow))
+                base = jnp.where(
+                    home, NEAR + near, jnp.where(first, FAR + far, jnp.where(second, MID + mid, REST))
+                )
                 table[base] = jnp.where(ghost, (spot << 4) + (index & 15), column)
                 table[base + LIST] = b * SLOTS + s
                 table[base + 2 * LIST] = b
                 near = near + home.astype(jnp.int32)
-                far = far + ghost.astype(jnp.int32)
+                far = far + first.astype(jnp.int32)
+                mid = mid + second.astype(jnp.int32)
         for s in range(2 * SLOTS):
             slot = pair * 2 * SLOTS + s
             high, rest = split(jnp.transpose(blocks[slot]))
             turned[slot, :, 0:BLK] = high
             turned[slot, :, BLK : 2 * BLK] = rest
-        return near, far
+        return near, far, mid
 
     zero = jnp.int32(0)
-    counts = lax.fori_loop(0, ROWS // 2, rows, (zero, zero))
-    for i, base in enumerate((NEAR, FAR)):
+    counts = lax.fori_loop(0, ROWS // 2, rows, (zero, zero, zero))
+    for i, base in enumerate((NEAR, FAR, MID)):
         table[COUNTS + i] = counts[i]
         for g in range(GROUPS[i]):
             table[base + counts[i] + g] = LINES
             table[base + LIST + counts[i] + g] = 0
             table[base + 2 * LIST + counts[i] + g] = 0
-    total = product(table, 0, turned, (field,), *scratch)
+    fill((field,), (0,), *scratch)
+    total = product(table, 0, turned, *scratch)
     out[...] = rate[...] * field[...] * (1.0 - field[...]) - total
 
 
 def near_part(table, turned, field, rate, concentration, out, *scratch):
-    total = product(table, 0, turned, (field,), *scratch)
+    fill((field,), (0,), *scratch)
+    total = product(table, 0, turned, *scratch)
     slope = rate[...] * (1.0 - 2.0 * concentration[...]) + SHIFT
     out[...] = slope * field[...] - total
 
 
-def product(table, which, turned, sources, lines, stage, *sums):
-    base = (NEAR, FAR)[which]
+def fill(sources, turns, lines, *rest):
+    for source, t in zip(sources, turns):
+        start = pl.multiple_of(t * GHOST, GHOST)
+        lines[pl.ds(start, source.shape[0]), :] = source[...]
+    lines[LINES : LINES + 8, :] = jnp.zeros((8, BLK), f32)
+
+
+def product(table, which, turned, lines, stage, *sums):
+    base = (NEAR, FAR, MID)[which]
     size = GROUPS[which]
     count = table[COUNTS + which]
-    for i, source in enumerate(sources):
-        height = source.shape[0]
-        lines[i * height : (i + 1) * height, :] = source[...]
-    lines[LINES : LINES + 8, :] = jnp.zeros((8, BLK), f32)
     for ref in sums:
         ref[...] = jnp.zeros((ROWS, BLK), f32)
 
@@ -184,18 +217,35 @@
     return (sums[0][...] + sums[1][...]) + (sums[2][...] + sums[3][...])
 
 
-def far_part(scale):
-    def kernel(table, turned, near, g0, g1, g2, g3, out, p0, p1, p2, p3, *scratch):
-        out[...] = (near[...] - product(table, 1, turned, (g0, g1, g2, g3), *scratch)) * scale
-        write_packets(out, lambda t, g: table[SEND + t * GHOST + g], (p0, p1, p2, p3))
-
-    return kernel
-
-
-def last_part(table, turned, near, g0, g1, g2, g3, *rest):
+def middle_part(table, turned, near, g0, g1, g4, g5, out, *scratch):
+    fill((g0, g1, g4, g5), MID_BY, *scratch)
+    out[...] = near[...] - product(table, 2, turned, *scratch)
+
+
+def send_out(table, out, packets):
+    write_packets(out, lambda t, g: table[SEND + t * GHOST + g], packets)
+
+
+def first_far_part(table, turned, near, g0, g1, g2, g3, out, *rest):
+    packets, scratch = rest[:TURNS], rest[TURNS:]
+    fill((g0, g1, g2, g3), [table[BY + q] for q in FIRST_INDICES], *scratch)
+    out[...] = near[...] - product(table, 1, turned, *scratch)
+    out[...] = out[...] - product(table, 2, turned, *scratch)
+    send_out(table, out, packets)
+
+
+def far_part(table, turned, near, g2, g3, out, *rest):
+    packets, scratch = rest[:TURNS], rest[TURNS:]
+    fill((g2, g3), FAR_BY, *scratch)
+    out[...] = (near[...] - product(table, 1, turned, *scratch)) * SCALE
+    send_out(table, out, packets)
+
+
+def last_part(table, turned, near, g2, g3, *rest):
     basis = rest[:DEGREE]
     sums, out, rows, *scratch = rest[DEGREE:]
-    out[...] = (near[...] - product(table, 1, turned, (g0, g1, g2, g3), *scratch)) * SCALE
+    fill((g2, g3), FAR_BY, *scratch)
+    out[...] = (near[...] - product(table, 1, turned, *scratch)) * SCALE
     basis = basis + (out,)
     rows[...] = jnp.zeros(rows.shape, f32)
     for k, (a, b) in enumerate(PAIRS):
@@ -325,7 +375,7 @@
 
 LIMIT = 24 << 20
 FIELD = jax.ShapeDtypeStruct((ROWS, BLK), f32)
-PACKETS = [jax.ShapeDtypeStruct((GHOST, BLK), f32)] * 4
+PACKET = jax.ShapeDtypeStruct((GHOST, BLK), f32)
 PARTIAL = [
     pltpu.VMEM((LINES + 8, BLK), f32),
     pltpu.VMEM((max(GROUPS), BLK), f32),
@@ -344,14 +394,26 @@
     return [pl.BlockSpec(memory_space=pltpu.HBM)] * n
 
 
-def shards(pairs, concentration, rate, step, values, columns, lengths, send):
+def shards(shifts, turns, concentration, rate, step, values, columns, lengths, send):
     devices = BLK
 
-    def exchange(packets):
+    def exchange(packets, by):
         arrived = []
-        for t in range(4):
-            arrived.append(lax.ppermute(packets[t], "dom", pairs[t]))
+        for t in range(len(by)):
+            arrived.append(lax.ppermute(packets[t], "dom", by[t]))
         return arrived
+
+    def middle(near, arrived):
+        return pl.pallas_call(
+            middle_part,
+            out_shape=FIELD,
+            in_specs=smem() + vmem(6),
+            out_specs=vmem()[0],
+            scratch_shapes=PARTIAL,
+            compiler_params=params(),
+            cost_estimate=cost(10**9),
+            name="middle_part",
+        )(table, turned, near, *[arrived[t] for t in MID_BY])
 
     send, concentration, rate, values, columns, lengths = (
         pltpu.with_memory_space_constraint(x, pltpu.HBM)
@@ -359,14 +421,14 @@
     )
     concentration, rate, send, *packets = pl.pallas_call(
         first_packets,
-        out_shape=[FIELD, FIELD, pltpu.SMEM((1, 4, GHOST), jnp.int32)] + PACKETS,
+        out_shape=[FIELD, FIELD, pltpu.SMEM((1, 4, GHOST), jnp.int32)] + [PACKET] * 4,
         in_specs=hbm(3),
         out_specs=vmem(2) + smem() + vmem(4),
         scratch_shapes=[pltpu.SemaphoreType.DMA((3,))],
         compiler_params=params(),
         name="first_packets",
     )(send, concentration, rate)
-    arrived = exchange(packets)
+    arrived = exchange(packets, shifts)
     send = pltpu.with_memory_space_constraint(send, pltpu.SMEM)
     turned, table, near = pl.pallas_call(
         setup,
@@ -394,17 +456,18 @@
     basis = []
 
     for k in range(DEGREE):
+        ghosts = arrived if k == 0 else [arrived[t] for t in FAR_BY]
         field, *packets = pl.pallas_call(
-            far_part(1.0 if k == 0 else SCALE),
-            out_shape=[FIELD] + PACKETS,
-            in_specs=smem() + vmem(6),
-            out_specs=vmem(5),
+            far_part if k else first_far_part,
+            out_shape=[FIELD] + [PACKET] * TURNS,
+            in_specs=smem() + vmem(2 + len(ghosts)),
+            out_specs=vmem(1 + TURNS),
             scratch_shapes=PARTIAL,
             compiler_params=params(),
             name="far_part",
-        )(table, turned, near, *arrived)
+        )(table, turned, near, *ghosts)
         basis.append(field)
-        arrived = exchange(packets)
+        arrived = exchange(packets, turns)
         near = pl.pallas_call(
             near_part,
             out_shape=FIELD,
@@ -415,15 +478,16 @@
             cost_estimate=cost(10**10),
             name="near_part",
         )(table, turned, field, rate, concentration)
+        near = middle(near, arrived)
     sums = pl.pallas_call(
         last_part,
         out_shape=jax.ShapeDtypeStruct((devices, ROWS), f32),
-        in_specs=smem() + vmem(6 + DEGREE),
+        in_specs=smem() + vmem(4 + DEGREE),
         out_specs=vmem()[0],
         scratch_shapes=[pltpu.VMEM((ROWS, BLK), f32), pltpu.VMEM((ROWS, BLK), f32)] + PARTIAL,
         compiler_params=params(),
         name="last_part",
-    )(table, turned, near, *arrived, *basis)
+    )(table, turned, near, *[arrived[t] for t in FAR_BY], *basis)
     everyone = lax.all_to_all(sums, "dom", split_axis=0, concat_axis=0, tiled=True)
     return pl.pallas_call(
         finish,
@@ -436,10 +500,10 @@
 
 
 def solution(mesh):
-    pairs = exchanges(mesh.shape["dom"])
+    shifts, turns = exchanges(mesh.shape["dom"])
 
     def run(*arrays):
-        return shards(pairs, *arrays)
+        return shards(shifts, turns, *arrays)
 
     split = P("dom")
     return jax.shard_map(

time: 106 us -> 169 us (1.59)
  starting transfers between devices: 58 us -> 108 us
  waiting for transfers between devices: 26.2 us -> 35.7 us
  Pallas kernels: 20.4 us -> 23 us
    ppermute x28 -> x40, starting transfers between devices: 52.1 us -> 104 us  [exchange(): arrived.append(lax.ppermute(packets[t], 'dom', by[t]))]
    ppermute x28 -> x40, waiting for transfers between devices: 17.6 us -> 27 us  [exchange(): arrived.append(lax.ppermute(packets[t], 'dom', by[t]))]
    pallas_call x6 -> x12, Pallas kernels: 4.1 us -> 6.4 us  [the longest x6 3.43 us: shards(): pl.pallas_call(far_part if k else first_far_part, out_shape=[FIELD] + [PA...]
  transfers between devices with their start and end apart: 29 -> 41, of which waited for: 13 -> 7; matrix products, arithmetic and copies ran while one was open for 0% -> 0% of each run, Pallas kernels for 12% -> 10%
where the time goes in v6:
time: 169 us; the launch traced here: 168 us
  starting transfers between devices  108 us (64%)
  waiting for transfers between devices  35.7 us (21%)
  Pallas kernels  23 us (14%)
    ppermute x40, starting transfers between devices, exchange(): arrived.append(lax.ppermute(packets[t], 'dom', by[t]))  104 us
    ppermute x40, waiting for transfers between devices, exchange(): arrived.append(lax.ppermute(packets[t], 'dom', by[t]))  27 us
    all_to_all x1, waiting for transfers between devices, shards(): lax.all_to_all(sums, 'dom', split_axis=0, concat_axis=0, tiled=True)  8.68 us
    pallas_call x1, Pallas kernels, shards(): pl.pallas_call(setup, out_shape=[pltpu.VMEM((ENTRIES, BLK, 2 * BLK), bf16...  8.09 us
    pallas_call x6, Pallas kernels, shards(): pl.pallas_call(near_part, out_shape=FIELD, in_specs=smem() + vmem(4), out...  5.25 us
    all_to_all x1, starting transfers between devices, shards(): lax.all_to_all(sums, 'dom', split_axis=0, concat_axis=0, tiled=True)  4.55 us
    pallas_call x6, Pallas kernels, shards(): pl.pallas_call(far_part if k else first_far_part, out_shape=[FIELD] + [PA...  3.43 us
  transfers between devices with their start and end apart: 41, of which 7 were waited for; matrix products, arithmetic and copies ran while one was open for 0% of the time, Pallas kernels for 10%

profile of v6, /device:TPU:0, one launch (start us, length us, event | category | flops | bytes accessed | tf_op | source)
XLA Modules:
  0.0 168.1 jit_solution(8587192169415139920)
XLA Ops:
  2.6 7.3 %collective-permute-start.2 = (f32[16,128]{1,0:T(8,128)S(1)}, f32[16,128]{1,0:T(8,128)S(1)}, u32[]{:S(2)}, u32[]{:S(2)}) collective-permute-start(f32[16,128]{1,0:T(8,128)S(1)} %get-tuple-element.65), channel_id=1, source_target_pairs={{0,126},{1,127},{2,0},{3,1},{4,2},{5,3},{6,4},{7,5},{8,6},{9,7},{1... | collective-permute-start | bytes 24584 | tf_op jit(solution)/shard_map/ppermute | solution.py:403
  11.2 8.1 %setup.1 = (bf16[160,128,256]{2,1,0:T(8,128)(2,1)S(1)}, s32[2984]{0:T(1024)S(4)}, f32[32,128]{1,0:T(8,128)S(1)}) custom-call(s32[5,32]{1,0:T(8,128)} %bitcast.8, s32[32]{0:T(128)} %lengths.1, s32[1,4,16]{2,1,0:T(4,128)S(4)} %get-tuple-element.57.send, f32[160,128,128]{2,1,0:T(8,128)} %bitcast.7, f32[32,128]{1,0:T(8,128)S(1)} %get-tuple-element.58.field.concentration, ...), custom_call_target="tpu_custom_call" | custom-call | flops 10000000000 | tf_op jit(solution)/shard_map/setup/pallas_call | solution.py:433
  22.4 4.5 %collective-permute-start.7 = (f32[16,128]{1,0:T(8,128)S(1)}, f32[16,128]{1,0:T(8,128)S(1)}, u32[]{:S(2)}, u32[]{:S(2)}) collective-permute-start(f32[16,128]{1,0:T(8,128)S(1)} %get-tuple-element.71), channel_id=1, source_target_pairs={{0,2},{1,3},{6,4},{7,5},{8,10},{9,11},{14,12},{15,13},{16,18},{17,... | collective-permute-start | bytes 24584 | tf_op jit(solution)/shard_map/ppermute | solution.py:403
  30.3 6.4 %collective-permute-start.9 = (f32[16,128]{1,0:T(8,128)S(1)}, f32[16,128]{1,0:T(8,128)S(1)}, u32[]{:S(2)}, u32[]{:S(2)}) collective-permute-start(f32[16,128]{1,0:T(8,128)S(1)} %get-tuple-element.73), channel_id=1, source_target_pairs={{7,8},{8,7},{3,4},{4,3},{1,2},{6,5},{15,16},{16,15},{11,12},{12,11... | collective-permute-start | bytes 24584 | tf_op jit(solution)/shard_map/ppermute | solution.py:403
  37.3 3.4 %collective-permute-done.9.g3 = f32[16,128]{1,0:T(8,128)S(1)} collective-permute-done((f32[16,128]{1,0:T(8,128)S(1)}, f32[16,128]{1,0:T(8,128)S(1)}, u32[]{:S(2)}, u32[]{:S(2)}) %collective-permute-start.9) | collective-permute-done | bytes 8224 | tf_op jit(solution)/shard_map/ppermute | solution.py:403
  43.2 4.5 %collective-permute-start.13 = (f32[16,128]{1,0:T(8,128)S(1)}, f32[16,128]{1,0:T(8,128)S(1)}, u32[]{:S(2)}, u32[]{:S(2)}) collective-permute-start(f32[16,128]{1,0:T(8,128)S(1)} %get-tuple-element.78), channel_id=1, source_target_pairs={{0,2},{1,3},{6,4},{7,5},{8,10},{9,11},{14,12},{15,13},{16,18},{17,... | collective-permute-start | bytes 24584 | tf_op jit(solution)/shard_map/ppermute | solution.py:403
  48.7 4.7 %collective-permute-start.14 = (f32[16,128]{1,0:T(8,128)S(1)}, f32[16,128]{1,0:T(8,128)S(1)}, u32[]{:S(2)}, u32[]{:S(2)}) collective-permute-start(f32[16,128]{1,0:T(8,128)S(1)} %get-tuple-element.79), channel_id=1, source_target_pairs={{6,8},{8,6},{7,9},{9,7},{2,4},{4,2},{3,5},{5,3},{14,16},{16,14},{1... | collective-permute-start | bytes 24584 | tf_op jit(solution)/shard_map/ppermute | solution.py:403
  53.4 4.3 %collective-permute-start.15 = (f32[16,128]{1,0:T(8,128)S(1)}, f32[16,128]{1,0:T(8,128)S(1)}, u32[]{:S(2)}, u32[]{:S(2)}) collective-permute-start(f32[16,128]{1,0:T(8,128)S(1)} %get-tuple-element.80), channel_id=1, source_target_pairs={{7,8},{8,7},{3,4},{4,3},{1,2},{6,5},{15,16},{16,15},{11,12},{12,11... | collective-permute-start | bytes 24584 | tf_op jit(solution)/shard_map/ppermute | solution.py:403
  58.2 5.6 %collective-permute-done.15.g3 = f32[16,128]{1,0:T(8,128)S(1)} collective-permute-done((f32[16,128]{1,0:T(8,128)S(1)}, f32[16,128]{1,0:T(8,128)S(1)}, u32[]{:S(2)}, u32[]{:S(2)}) %collective-permute-start.15) | collective-permute-done | bytes 8224 | tf_op jit(solution)/shard_map/ppermute | solution.py:403
  66.3 4.5 %collective-permute-start.19 = (f32[16,128]{1,0:T(8,128)S(1)}, f32[16,128]{1,0:T(8,128)S(1)}, u32[]{:S(2)}, u32[]{:S(2)}) collective-permute-start(f32[16,128]{1,0:T(8,128)S(1)} %get-tuple-element.85), channel_id=1, source_target_pairs={{0,2},{1,3},{6,4},{7,5},{8,10},{9,11},{14,12},{15,13},{16,18},{17,... | collective-permute-start | bytes 24584 | tf_op jit(solution)/shard_map/ppermute | solution.py:403
  74.2 6.4 %collective-permute-start.21 = (f32[16,128]{1,0:T(8,128)S(1)}, f32[16,128]{1,0:T(8,128)S(1)}, u32[]{:S(2)}, u32[]{:S(2)}) collective-permute-start(f32[16,128]{1,0:T(8,128)S(1)} %get-tuple-element.87), channel_id=1, source_target_pairs={{7,8},{8,7},{3,4},{4,3},{1,2},{6,5},{15,16},{16,15},{11,12},{12,11... | collective-permute-start | bytes 24584 | tf_op jit(solution)/shard_map/ppermute | solution.py:403
  87.2 4.5 %collective-permute-start.25 = (f32[16,128]{1,0:T(8,128)S(1)}, f32[16,128]{1,0:T(8,128)S(1)}, u32[]{:S(2)}, u32[]{:S(2)}) collective-permute-start(f32[16,128]{1,0:T(8,128)S(1)} %get-tuple-element.92), channel_id=1, source_target_pairs={{0,2},{1,3},{6,4},{7,5},{8,10},{9,11},{14,12},{15,13},{16,18},{17,... | collective-permute-start | bytes 24584 | tf_op jit(solution)/shard_map/ppermute | solution.py:403
  92.8 4.7 %collective-permute-start.26 = (f32[16,128]{1,0:T(8,128)S(1)}, f32[16,128]{1,0:T(8,128)S(1)}, u32[]{:S(2)}, u32[]{:S(2)}) collective-permute-start(f32[16,128]{1,0:T(8,128)S(1)} %get-tuple-element.93), channel_id=1, source_target_pairs={{6,8},{8,6},{7,9},{9,7},{2,4},{4,2},{3,5},{5,3},{14,16},{16,14},{1... | collective-permute-start | bytes 24584 | tf_op jit(solution)/shard_map/ppermute | solution.py:403
  97.5 4.3 %collective-permute-start.27 = (f32[16,128]{1,0:T(8,128)S(1)}, f32[16,128]{1,0:T(8,128)S(1)}, u32[]{:S(2)}, u32[]{:S(2)}) collective-permute-start(f32[16,128]{1,0:T(8,128)S(1)} %get-tuple-element.94), channel_id=1, source_target_pairs={{7,8},{8,7},{3,4},{4,3},{1,2},{6,5},{15,16},{16,15},{11,12},{12,11... | collective-permute-start | bytes 24584 | tf_op jit(solution)/shard_map/ppermute | solution.py:403
  102.3 5.6 %collective-permute-done.27.g3 = f32[16,128]{1,0:T(8,128)S(1)} collective-permute-done((f32[16,128]{1,0:T(8,128)S(1)}, f32[16,128]{1,0:T(8,128)S(1)}, u32[]{:S(2)}, u32[]{:S(2)}) %collective-permute-start.27) | collective-permute-done | bytes 8224 | tf_op jit(solution)/shard_map/ppermute | solution.py:403
  110.4 4.5 %collective-permute-start.31 = (f32[16,128]{1,0:T(8,128)S(1)}, f32[16,128]{1,0:T(8,128)S(1)}, u32[]{:S(2)}, u32[]{:S(2)}) collective-permute-start(f32[16,128]{1,0:T(8,128)S(1)} %get-tuple-element.99), channel_id=1, source_target_pairs={{0,2},{1,3},{6,4},{7,5},{8,10},{9,11},{14,12},{15,13},{16,18},{17,... | collective-permute-start | bytes 24584 | tf_op jit(solution)/shard_map/ppermute | solution.py:403
  118.4 6.4 %collective-permute-start.33 = (f32[16,128]{1,0:T(8,128)S(1)}, f32[16,128]{1,0:T(8,128)S(1)}, u32[]{:S(2)}, u32[]{:S(2)}) collective-permute-start(f32[16,128]{1,0:T(8,128)S(1)} %get-tuple-element.101), channel_id=1, source_target_pairs={{7,8},{8,7},{3,4},{4,3},{1,2},{6,5},{15,16},{16,15},{11,12},{12,11... | collective-permute-start | bytes 24584 | tf_op jit(solution)/shard_map/ppermute | solution.py:403
  125.3 3.4 %collective-permute-done.33.g3 = f32[16,128]{1,0:T(8,128)S(1)} collective-permute-done((f32[16,128]{1,0:T(8,128)S(1)}, f32[16,128]{1,0:T(8,128)S(1)}, u32[]{:S(2)}, u32[]{:S(2)}) %collective-permute-start.33) | collective-permute-done | bytes 8224 | tf_op jit(solution)/shard_map/ppermute | solution.py:403
  131.3 4.5 %collective-permute-start.37 = (f32[16,128]{1,0:T(8,128)S(1)}, f32[16,128]{1,0:T(8,128)S(1)}, u32[]{:S(2)}, u32[]{:S(2)}) collective-permute-start(f32[16,128]{1,0:T(8,128)S(1)} %get-tuple-element.106), channel_id=1, source_target_pairs={{0,2},{1,3},{6,4},{7,5},{8,10},{9,11},{14,12},{15,13},{16,18},{17,... | collective-permute-start | bytes 24584 | tf_op jit(solution)/shard_map/ppermute | solution.py:403
  136.7 4.7 %collective-permute-start.38 = (f32[16,128]{1,0:T(8,128)S(1)}, f32[16,128]{1,0:T(8,128)S(1)}, u32[]{:S(2)}, u32[]{:S(2)}) collective-permute-start(f32[16,128]{1,0:T(8,128)S(1)} %get-tuple-element.107), channel_id=1, source_target_pairs={{6,8},{8,6},{7,9},{9,7},{2,4},{4,2},{3,5},{5,3},{14,16},{16,14},{1... | collective-permute-start | bytes 24584 | tf_op jit(solution)/shard_map/ppermute | solution.py:403
  141.4 4.3 %collective-permute-start.39 = (f32[16,128]{1,0:T(8,128)S(1)}, f32[16,128]{1,0:T(8,128)S(1)}, u32[]{:S(2)}, u32[]{:S(2)}) collective-permute-start(f32[16,128]{1,0:T(8,128)S(1)} %get-tuple-element.108), channel_id=1, source_target_pairs={{7,8},{8,7},{3,4},{4,3},{1,2},{6,5},{15,16},{16,15},{11,12},{12,11... | collective-permute-start | bytes 24584 | tf_op jit(solution)/shard_map/ppermute | solution.py:403
  146.2 5.6 %collective-permute-done.39.g3 = f32[16,128]{1,0:T(8,128)S(1)} collective-permute-done((f32[16,128]{1,0:T(8,128)S(1)}, f32[16,128]{1,0:T(8,128)S(1)}, u32[]{:S(2)}, u32[]{:S(2)}) %collective-permute-start.39) | collective-permute-done | bytes 8224 | tf_op jit(solution)/shard_map/ppermute | solution.py:403
  153.0 4.5 %all-to-all-start = ((f32[128,1,32]{2,1,0:T(1,128)}), f32[128,1,32]{2,1,0:T(1,128)S(1)}, u32[]{:S(2)}, u32[]{:S(2)}) async-start(f32[128,1,32]{2,1,0:T(1,128)} %bitcast.3), calls=%async_computation | async-start | bytes 131072 | tf_op jit(solution)/shard_map/all_to_all | solution.py:491
  158.2 8.7 %all-to-all-done = f32[128,1,32]{2,1,0:T(1,128)S(1)} async-done(((f32[128,1,32]{2,1,0:T(1,128)}), f32[128,1,32]{2,1,0:T(1,128)S(1)}, u32[]{:S(2)}, u32[]{:S(2)}) %all-to-all-start) | async-done | bytes 16416 | tf_op jit(solution)/shard_map/all_to_all | solution.py:491
  (80 shorter events, 41.3 us)
Async XLA Ops:
  0.8 18.4 %collective-permute-start = (f32[16,128]{1,0:T(8,128)S(1)}, f32[16,128]{1,0:T(8,128)S(1)}, u32[]{:S(2)}, u32[]{:S(2)}) collective-permute-start(f32[16,128]{1,0:T(8,128)S(1)} %get-tuple-element.63), channel_id=1, source_target_pairs={{0,1},{1,2},{2,3},{3,4},{4,5},{5,6},{6,7},{7,8},{8,9},{9,10},{10,1... | collective-permute-start | bytes 24584 | tf_op jit(solution)/shard_map/ppermute | solution.py:403
  0.9 18.4 %collective-permute-start.1 = (f32[16,128]{1,0:T(8,128)S(1)}, f32[16,128]{1,0:T(8,128)S(1)}, u32[]{:S(2)}, u32[]{:S(2)}) collective-permute-start(f32[16,128]{1,0:T(8,128)S(1)} %get-tuple-element.64), channel_id=1, source_target_pairs={{0,2},{1,3},{2,4},{3,5},{4,6},{5,7},{6,8},{7,9},{8,10},{9,11},{10,... | collective-permute-start | bytes 24584 | tf_op jit(solution)/shard_map/ppermute | solution.py:403
  2.6 16.7 %collective-permute-start.2 = (f32[16,128]{1,0:T(8,128)S(1)}, f32[16,128]{1,0:T(8,128)S(1)}, u32[]{:S(2)}, u32[]{:S(2)}) collective-permute-start(f32[16,128]{1,0:T(8,128)S(1)} %get-tuple-element.65), channel_id=1, source_target_pairs={{0,126},{1,127},{2,0},{3,1},{4,2},{5,3},{6,4},{7,5},{8,6},{9,7},{1... | collective-permute-start | bytes 24584 | tf_op jit(solution)/shard_map/ppermute | solution.py:403
  21.0 15.8 %collective-permute-start.5 = (f32[16,128]{1,0:T(8,128)S(1)}, f32[16,128]{1,0:T(8,128)S(1)}, u32[]{:S(2)}, u32[]{:S(2)}) collective-permute-start(f32[16,128]{1,0:T(8,128)S(1)} %get-tuple-element.69), channel_id=1, source_target_pairs={{2,0},{3,1},{4,6},{5,7},{10,8},{11,9},{12,14},{13,15},{18,16},{19,... | collective-permute-start | bytes 24584 | tf_op jit(solution)/shard_map/ppermute | solution.py:403
  22.3 14.5 %collective-permute-start.6 = (f32[16,128]{1,0:T(8,128)S(1)}, f32[16,128]{1,0:T(8,128)S(1)}, u32[]{:S(2)}, u32[]{:S(2)}) collective-permute-start(f32[16,128]{1,0:T(8,128)S(1)} %get-tuple-element.70), channel_id=1, source_target_pairs={{0,1},{1,0},{2,3},{3,2},{4,5},{5,4},{6,7},{7,6},{8,9},{9,8},{10,11... | collective-permute-start | bytes 24584 | tf_op jit(solution)/shard_map/ppermute | solution.py:403
  22.4 14.4 %collective-permute-start.7 = (f32[16,128]{1,0:T(8,128)S(1)}, f32[16,128]{1,0:T(8,128)S(1)}, u32[]{:S(2)}, u32[]{:S(2)}) collective-permute-start(f32[16,128]{1,0:T(8,128)S(1)} %get-tuple-element.71), channel_id=1, source_target_pairs={{0,2},{1,3},{6,4},{7,5},{8,10},{9,11},{14,12},{15,13},{16,18},{17,... | collective-permute-start | bytes 24584 | tf_op jit(solution)/shard_map/ppermute | solution.py:403
  41.2 12.2 %collective-permute-start.10 = (f32[16,128]{1,0:T(8,128)S(1)}, f32[16,128]{1,0:T(8,128)S(1)}, u32[]{:S(2)}, u32[]{:S(2)}) collective-permute-start(f32[16,128]{1,0:T(8,128)S(1)} %get-tuple-element.75), channel_id=1, source_target_pairs={{2,1},{5,6},{10,9},{13,14},{18,17},{21,22},{26,25},{29,30},{34,33}... | collective-permute-start | bytes 24584 | tf_op jit(solution)/shard_map/ppermute | solution.py:403
  41.9 15.8 %collective-permute-start.11 = (f32[16,128]{1,0:T(8,128)S(1)}, f32[16,128]{1,0:T(8,128)S(1)}, u32[]{:S(2)}, u32[]{:S(2)}) collective-permute-start(f32[16,128]{1,0:T(8,128)S(1)} %get-tuple-element.76), channel_id=1, source_target_pairs={{2,0},{3,1},{4,6},{5,7},{10,8},{11,9},{12,14},{13,15},{18,16},{19,... | collective-permute-start | bytes 24584 | tf_op jit(solution)/shard_map/ppermute | solution.py:403
  43.2 14.5 %collective-permute-start.12 = (f32[16,128]{1,0:T(8,128)S(1)}, f32[16,128]{1,0:T(8,128)S(1)}, u32[]{:S(2)}, u32[]{:S(2)}) collective-permute-start(f32[16,128]{1,0:T(8,128)S(1)} %get-tuple-element.77), channel_id=1, source_target_pairs={{0,1},{1,0},{2,3},{3,2},{4,5},{5,4},{6,7},{7,6},{8,9},{9,8},{10,11... | collective-permute-start | bytes 24584 | tf_op jit(solution)/shard_map/ppermute | solution.py:403
  43.2 14.4 %collective-permute-start.13 = (f32[16,128]{1,0:T(8,128)S(1)}, f32[16,128]{1,0:T(8,128)S(1)}, u32[]{:S(2)}, u32[]{:S(2)}) collective-permute-start(f32[16,128]{1,0:T(8,128)S(1)} %get-tuple-element.78), channel_id=1, source_target_pairs={{0,2},{1,3},{6,4},{7,5},{8,10},{9,11},{14,12},{15,13},{16,18},{17,... | collective-permute-start | bytes 24584 | tf_op jit(solution)/shard_map/ppermute | solution.py:403
  64.9 15.8 %collective-permute-start.17 = (f32[16,128]{1,0:T(8,128)S(1)}, f32[16,128]{1,0:T(8,128)S(1)}, u32[]{:S(2)}, u32[]{:S(2)}) collective-permute-start(f32[16,128]{1,0:T(8,128)S(1)} %get-tuple-element.83), channel_id=1, source_target_pairs={{2,0},{3,1},{4,6},{5,7},{10,8},{11,9},{12,14},{13,15},{18,16},{19,... | collective-permute-start | bytes 24584 | tf_op jit(solution)/shard_map/ppermute | solution.py:403
  66.2 14.5 %collective-permute-start.18 = (f32[16,128]{1,0:T(8,128)S(1)}, f32[16,128]{1,0:T(8,128)S(1)}, u32[]{:S(2)}, u32[]{:S(2)}) collective-permute-start(f32[16,128]{1,0:T(8,128)S(1)} %get-tuple-element.84), channel_id=1, source_target_pairs={{0,1},{1,0},{2,3},{3,2},{4,5},{5,4},{6,7},{7,6},{8,9},{9,8},{10,11... | collective-permute-start | bytes 24584 | tf_op jit(solution)/shard_map/ppermute | solution.py:403
  66.3 14.4 %collective-permute-start.19 = (f32[16,128]{1,0:T(8,128)S(1)}, f32[16,128]{1,0:T(8,128)S(1)}, u32[]{:S(2)}, u32[]{:S(2)}) collective-permute-start(f32[16,128]{1,0:T(8,128)S(1)} %get-tuple-element.85), channel_id=1, source_target_pairs={{0,2},{1,3},{6,4},{7,5},{8,10},{9,11},{14,12},{15,13},{16,18},{17,... | collective-permute-start | bytes 24584 | tf_op jit(solution)/shard_map/ppermute | solution.py:403
  85.1 12.3 %collective-permute-start.22 = (f32[16,128]{1,0:T(8,128)S(1)}, f32[16,128]{1,0:T(8,128)S(1)}, u32[]{:S(2)}, u32[]{:S(2)}) collective-permute-start(f32[16,128]{1,0:T(8,128)S(1)} %get-tuple-element.89), channel_id=1, source_target_pairs={{2,1},{5,6},{10,9},{13,14},{18,17},{21,22},{26,25},{29,30},{34,33}... | collective-permute-start | bytes 24584 | tf_op jit(solution)/shard_map/ppermute | solution.py:403
  85.8 16.0 %collective-permute-start.23 = (f32[16,128]{1,0:T(8,128)S(1)}, f32[16,128]{1,0:T(8,128)S(1)}, u32[]{:S(2)}, u32[]{:S(2)}) collective-permute-start(f32[16,128]{1,0:T(8,128)S(1)} %get-tuple-element.90), channel_id=1, source_target_pairs={{2,0},{3,1},{4,6},{5,7},{10,8},{11,9},{12,14},{13,15},{18,16},{19,... | collective-permute-start | bytes 24584 | tf_op jit(solution)/shard_map/ppermute | solution.py:403
  87.1 14.7 %collective-permute-start.24 = (f32[16,128]{1,0:T(8,128)S(1)}, f32[16,128]{1,0:T(8,128)S(1)}, u32[]{:S(2)}, u32[]{:S(2)}) collective-permute-start(f32[16,128]{1,0:T(8,128)S(1)} %get-tuple-element.91), channel_id=1, source_target_pairs={{0,1},{1,0},{2,3},{3,2},{4,5},{5,4},{6,7},{7,6},{8,9},{9,8},{10,11... | collective-permute-start | bytes 24584 | tf_op jit(solution)/shard_map/ppermute | solution.py:403
  87.2 14.6 %collective-permute-start.25 = (f32[16,128]{1,0:T(8,128)S(1)}, f32[16,128]{1,0:T(8,128)S(1)}, u32[]{:S(2)}, u32[]{:S(2)}) collective-permute-start(f32[16,128]{1,0:T(8,128)S(1)} %get-tuple-element.92), channel_id=1, source_target_pairs={{0,2},{1,3},{6,4},{7,5},{8,10},{9,11},{14,12},{15,13},{16,18},{17,... | collective-permute-start | bytes 24584 | tf_op jit(solution)/shard_map/ppermute | solution.py:403
  109.0 15.8 %collective-permute-start.29 = (f32[16,128]{1,0:T(8,128)S(1)}, f32[16,128]{1,0:T(8,128)S(1)}, u32[]{:S(2)}, u32[]{:S(2)}) collective-permute-start(f32[16,128]{1,0:T(8,128)S(1)} %get-tuple-element.97), channel_id=1, source_target_pairs={{2,0},{3,1},{4,6},{5,7},{10,8},{11,9},{12,14},{13,15},{18,16},{19,... | collective-permute-start | bytes 24584 | tf_op jit(solution)/shard_map/ppermute | solution.py:403
  110.3 14.5 %collective-permute-start.30 = (f32[16,128]{1,0:T(8,128)S(1)}, f32[16,128]{1,0:T(8,128)S(1)}, u32[]{:S(2)}, u32[]{:S(2)}) collective-permute-start(f32[16,128]{1,0:T(8,128)S(1)} %get-tuple-element.98), channel_id=1, source_target_pairs={{0,1},{1,0},{2,3},{3,2},{4,5},{5,4},{6,7},{7,6},{8,9},{9,8},{10,11... | collective-permute-start | bytes 24584 | tf_op jit(solution)/shard_map/ppermute | solution.py:403
  110.4 14.4 %collective-permute-start.31 = (f32[16,128]{1,0:T(8,128)S(1)}, f32[16,128]{1,0:T(8,128)S(1)}, u32[]{:S(2)}, u32[]{:S(2)}) collective-permute-start(f32[16,128]{1,0:T(8,128)S(1)} %get-tuple-element.99), channel_id=1, source_target_pairs={{0,2},{1,3},{6,4},{7,5},{8,10},{9,11},{14,12},{15,13},{16,18},{17,... | collective-permute-start | bytes 24584 | tf_op jit(solution)/shard_map/ppermute | solution.py:403
  129.9 15.8 %collective-permute-start.35 = (f32[16,128]{1,0:T(8,128)S(1)}, f32[16,128]{1,0:T(8,128)S(1)}, u32[]{:S(2)}, u32[]{:S(2)}) collective-permute-start(f32[16,128]{1,0:T(8,128)S(1)} %get-tuple-element.104), channel_id=1, source_target_pairs={{2,0},{3,1},{4,6},{5,7},{10,8},{11,9},{12,14},{13,15},{18,16},{19,... | collective-permute-start | bytes 24584 | tf_op jit(solution)/shard_map/ppermute | solution.py:403
  131.2 14.5 %collective-permute-start.36 = (f32[16,128]{1,0:T(8,128)S(1)}, f32[16,128]{1,0:T(8,128)S(1)}, u32[]{:S(2)}, u32[]{:S(2)}) collective-permute-start(f32[16,128]{1,0:T(8,128)S(1)} %get-tuple-element.105), channel_id=1, source_target_pairs={{0,1},{1,0},{2,3},{3,2},{4,5},{5,4},{6,7},{7,6},{8,9},{9,8},{10,11... | collective-permute-start | bytes 24584 | tf_op jit(solution)/shard_map/ppermute | solution.py:403
  131.3 14.4 %collective-permute-start.37 = (f32[16,128]{1,0:T(8,128)S(1)}, f32[16,128]{1,0:T(8,128)S(1)}, u32[]{:S(2)}, u32[]{:S(2)}) collective-permute-start(f32[16,128]{1,0:T(8,128)S(1)} %get-tuple-element.106), channel_id=1, source_target_pairs={{0,2},{1,3},{6,4},{7,5},{8,10},{9,11},{14,12},{15,13},{16,18},{17,... | collective-permute-start | bytes 24584 | tf_op jit(solution)/shard_map/ppermute | solution.py:403
  153.0 13.9 %all-to-all-start = ((f32[128,1,32]{2,1,0:T(1,128)}), f32[128,1,32]{2,1,0:T(1,128)S(1)}, u32[]{:S(2)}, u32[]{:S(2)}) async-start(f32[128,1,32]{2,1,0:T(1,128)} %bitcast.3), calls=%async_computation | async-start | bytes 131072 | tf_op jit(solution)/shard_map/all_to_all | solution.py:491
  (17 other events, 171.0 us)

commit v7 on v6

--- a/solution.py
+++ b/solution.py
@@ -18,19 +18,18 @@
 OFFSETS = (-2, -1, 1, 2)
 FIRST_INDICES = (2, 3, 0, 1)
 EIGHT = 8
-EXCHANGES = (
-    ((2, 1), (5, 6)),
-    ((2, 0), (3, 1), (4, 6), (5, 7)),
-    ((6, 8), (8, 6), (7, 9), (9, 7), (2, 4), (4, 2), (3, 5), (5, 3)),
-    ((7, 8), (8, 7), (3, 4), (4, 3), (1, 2), (6, 5)),
-    ((0, 1), (1, 0), (2, 3), (3, 2), (4, 5), (5, 4), (6, 7), (7, 6)),
-    ((0, 2), (1, 3), (6, 4), (7, 5)),
+HOPS = (
+    (1, -2, -2, -1, 2, -2, -2, -2),
+    (-1, 2, -1, 1, -2, 1, -1, 1),
+    (-2, 1, 2, 2, -1, 2, 2, 2),
+    (2, -1, 1, -2, 1, -1, 1, -1),
 )
+EXCHANGES = tuple(tuple((r, r + hop) for r, hop in enumerate(hops)) for hops in HOPS)
 TURNS = len(EXCHANGES)
 FAR_BY = (2, 3)
-MID_BY = (0, 1, 4, 5)
-
-GROUPS = (80, 32, 40)
+MID_BY = (0, 1)
+
+GROUPS = (80, 32, 32)
 LIST = ENTRIES + max(GROUPS)
 NEAR = 0
 FAR = 3 * LIST
@@ -41,7 +40,6 @@
 BY = COUNTS + 4
 TABLE = BY + 4
 LINES = TURNS * GHOST
-
 
 f32 = jnp.float32
 bf16 = jnp.bfloat16
@@ -131,41 +129,43 @@
     for copy in copies:
         copy.wait()
 
-    def rows(pair, carry):
+    spots = (at[0] | (at[1] << 8)) | ((at[2] << 16) | (at[3] << 24))
+
+    def listed(b, carry):
         near, far, mid = carry
+        length = length_of[b]
+        for s in range(SLOTS):
+            column = where[s, b]
+            index = jnp.maximum(column - ROWS, 0)
+            spot = (spots >> ((index >> 4) << 3)) & 7
+            live = s < length
+            ghost = jnp.logical_and(live, column >= ROWS)
+            home = jnp.logical_and(live, column < ROWS)
+            first = jnp.logical_and(ghost, spot >= FAR_BY[0])
+            second = jnp.logical_and(ghost, spot < FAR_BY[0])
+            base = jnp.where(
+                home, NEAR + near, jnp.where(first, FAR + far, jnp.where(second, MID + mid, REST))
+            )
+            table[base] = jnp.where(ghost, (spot << 4) + (index & 15), column)
+            table[base + LIST] = b * SLOTS + s
+            table[base + 2 * LIST] = b
+            near = near + home.astype(jnp.int32)
+            far = far + first.astype(jnp.int32)
+            mid = mid + second.astype(jnp.int32)
+        return near, far, mid
+
+    def turn(pair, carry):
         fetch(pair).wait()
-        for half in range(2):
-            b = pair * 2 + half
-            length = length_of[b]
-            for s in range(SLOTS):
-                column = where[s, b]
-                index = jnp.maximum(column - ROWS, 0)
-                q = index >> 4
-                spot = jnp.where(q < 2, jnp.where(q == 0, at[0], at[1]), jnp.where(q == 2, at[2], at[3]))
-                live = s < length
-                ghost = jnp.logical_and(live, column >= ROWS)
-                home = jnp.logical_and(live, column < ROWS)
-                slow = jnp.logical_or(spot == FAR_BY[0], spot == FAR_BY[1])
-                first = jnp.logical_and(ghost, slow)
-                second = jnp.logical_and(ghost, jnp.logical_not(slow))
-                base = jnp.where(
-                    home, NEAR + near, jnp.where(first, FAR + far, jnp.where(second, MID + mid, REST))
-                )
-                table[base] = jnp.where(ghost, (spot << 4) + (index & 15), column)
-                table[base + LIST] = b * SLOTS + s
-                table[base + 2 * LIST] = b
-                near = near + home.astype(jnp.int32)
-                far = far + first.astype(jnp.int32)
-                mid = mid + second.astype(jnp.int32)
         for s in range(2 * SLOTS):
             slot = pair * 2 * SLOTS + s
             high, rest = split(jnp.transpose(blocks[slot]))
             turned[slot, :, 0:BLK] = high
             turned[slot, :, BLK : 2 * BLK] = rest
-        return near, far, mid
+        return carry
 
     zero = jnp.int32(0)
-    counts = lax.fori_loop(0, ROWS // 2, rows, (zero, zero, zero))
+    counts = lax.fori_loop(0, ROWS, listed, (zero, zero, zero))
+    lax.fori_loop(0, ROWS // 2, turn, 0)
     for i, base in enumerate((NEAR, FAR, MID)):
         table[COUNTS + i] = counts[i]
         for g in range(GROUPS[i]):
@@ -217,8 +217,8 @@
     return (sums[0][...] + sums[1][...]) + (sums[2][...] + sums[3][...])
 
 
-def middle_part(table, turned, near, g0, g1, g4, g5, out, *scratch):
-    fill((g0, g1, g4, g5), MID_BY, *scratch)
+def middle_part(table, turned, near, g0, g1, out, *scratch):
+    fill((g0, g1), MID_BY, *scratch)
     out[...] = near[...] - product(table, 2, turned, *scratch)
 
 
@@ -241,16 +241,25 @@
     send_out(table, out, packets)
 
 
+def inner_products(basis, pairs, rows, at):
+    for k, (a, b) in enumerate(pairs):
+        both = basis[a][...] * basis[b][...]
+        rows[at + k : at + k + 1, :] = jnp.sum(both, axis=0, keepdims=True)
+
+
+def gram_part(*refs):
+    basis, rows = refs[:DEGREE], refs[DEGREE]
+    rows[...] = jnp.zeros(rows.shape, f32)
+    inner_products(basis, PAIRS[:-DEGREE], rows, 0)
+
+
 def last_part(table, turned, near, g2, g3, *rest):
     basis = rest[:DEGREE]
-    sums, out, rows, *scratch = rest[DEGREE:]
+    early, sums, out, rows, *scratch = rest[DEGREE:]
     fill((g2, g3), FAR_BY, *scratch)
     out[...] = (near[...] - product(table, 1, turned, *scratch)) * SCALE
-    basis = basis + (out,)
-    rows[...] = jnp.zeros(rows.shape, f32)
-    for k, (a, b) in enumerate(PAIRS):
-        both = basis[a][...] * basis[b][...]
-        rows[k : k + 1, :] = jnp.sum(both, axis=0, keepdims=True)
+    rows[...] = early[...]
+    inner_products(basis + (out,), PAIRS[-DEGREE:], rows, len(PAIRS) - DEGREE)
     line = jnp.sum(jnp.transpose(rows[...]), axis=0, keepdims=True)
     sums[...] = jnp.broadcast_to(line, sums.shape)
 
@@ -407,7 +416,7 @@
         return pl.pallas_call(
             middle_part,
             out_shape=FIELD,
-            in_specs=smem() + vmem(6),
+            in_specs=smem() + vmem(2 + len(MID_BY)),
             out_specs=vmem()[0],
             scratch_shapes=PARTIAL,
             compiler_params=params(),
@@ -479,15 +488,24 @@
             name="near_part",
         )(table, turned, field, rate, concentration)
         near = middle(near, arrived)
+    early = pl.pallas_call(
+        gram_part,
+        out_shape=FIELD,
+        in_specs=vmem(DEGREE),
+        out_specs=vmem()[0],
+        compiler_params=params(),
+        cost_estimate=cost(10**9),
+        name="gram_part",
+    )(*basis)
     sums = pl.pallas_call(
         last_part,
         out_shape=jax.ShapeDtypeStruct((devices, ROWS), f32),
-        in_specs=smem() + vmem(4 + DEGREE),
+        in_specs=smem() + vmem(5 + DEGREE),
         out_specs=vmem()[0],
         scratch_shapes=[pltpu.VMEM((ROWS, BLK), f32), pltpu.VMEM((ROWS, BLK), f32)] + PARTIAL,
         compiler_params=params(),
         name="last_part",
-    )(table, turned, near, *[arrived[t] for t in FAR_BY], *basis)
+    )(table, turned, near, *[arrived[t] for t in FAR_BY], *basis, early)
     everyone = lax.all_to_all(sums, "dom", split_axis=0, concat_axis=0, tiled=True)
     return pl.pallas_call(
         finish,

time: 169 us -> 103 us (0.61)
  starting transfers between devices: 108 us -> 40 us
  waiting for transfers between devices: 35.7 us -> 39.9 us
    ppermute x40 -> x28, starting transfers between devices: 104 us -> 35.4 us  [exchange(): arrived.append(lax.ppermute(packets[t], 'dom', by[t]))]
    ppermute x40 -> x28, waiting for transfers between devices: 27 us -> 31.2 us  [exchange(): arrived.append(lax.ppermute(packets[t], 'dom', by[t]))]
  transfers between devices with their start and end apart: 41 -> 29, of which waited for: 7 -> 13; matrix products, arithmetic and copies ran while one was open for 0% -> 0% of each run, Pallas kernels for 10% -> 15%
where the time goes in v7:
time: 103 us
  starting transfers between devices  40 us (39%)
  waiting for transfers between devices  39.9 us (39%)
  Pallas kernels  21.9 us (21%)
    ppermute x28, starting transfers between devices, exchange(): arrived.append(lax.ppermute(packets[t], 'dom', by[t]))  35.4 us
    ppermute x28, waiting for transfers between devices, exchange(): arrived.append(lax.ppermute(packets[t], 'dom', by[t]))  31.2 us
    all_to_all x1, waiting for transfers between devices, shards(): lax.all_to_all(sums, 'dom', split_axis=0, concat_axis=0, tiled=True)  8.67 us
    pallas_call x1, Pallas kernels, shards(): pl.pallas_call(setup, out_shape=[pltpu.VMEM((ENTRIES, BLK, 2 * BLK), bf16...  7.95 us
    pallas_call x6, Pallas kernels, shards(): pl.pallas_call(near_part, out_shape=FIELD, in_specs=smem() + vmem(4), out...  4.97 us
    all_to_all x1, starting transfers between devices, shards(): lax.all_to_all(sums, 'dom', split_axis=0, concat_axis=0, tiled=True)  4.59 us
    pallas_call x6, Pallas kernels, shards(): pl.pallas_call(far_part if k else first_far_part, out_shape=[FIELD] + [PA...  3.25 us
    pallas_call x6, Pallas kernels, middle(): pl.pallas_call(middle_part, out_shape=FIELD, in_specs=smem() + vmem(2 + l...  2.44 us
  transfers between devices with their start and end apart: 29, of which 13 were waited for; matrix products, arithmetic and copies ran while one was open for 0% of the time, Pallas kernels for 15%

profile of v7, /device:TPU:0, one launch (start us, length us, event | category | flops | bytes accessed | tf_op | source)
XLA Modules:
  0.0 102.7 jit_solution(5489516837487109346)
XLA Ops:
  0.9 1.7 %collective-permute-start.1 = (f32[16,128]{1,0:T(8,128)S(1)}, f32[16,128]{1,0:T(8,128)S(1)}, u32[]{:S(2)}, u32[]{:S(2)}) collective-permute-start(f32[16,128]{1,0:T(8,128)S(1)} %get-tuple-element.52), channel_id=1, source_target_pairs={{0,2},{1,3},{2,4},{3,5},{4,6},{5,7},{6,8},{7,9},{8,10},{9,11},{10,... | collective-permute-start | bytes 24584 | tf_op jit(solution)/shard_map/ppermute | solution.py:412
  2.6 7.3 %collective-permute-start.2 = (f32[16,128]{1,0:T(8,128)S(1)}, f32[16,128]{1,0:T(8,128)S(1)}, u32[]{:S(2)}, u32[]{:S(2)}) collective-permute-start(f32[16,128]{1,0:T(8,128)S(1)} %get-tuple-element.53), channel_id=1, source_target_pairs={{0,126},{1,127},{2,0},{3,1},{4,2},{5,3},{6,4},{7,5},{8,6},{9,7},{1... | collective-permute-start | bytes 24584 | tf_op jit(solution)/shard_map/ppermute | solution.py:412
  9.8 1.3 %collective-permute-start.3 = (f32[16,128]{1,0:T(8,128)S(1)}, f32[16,128]{1,0:T(8,128)S(1)}, u32[]{:S(2)}, u32[]{:S(2)}) collective-permute-start(f32[16,128]{1,0:T(8,128)S(1)} %get-tuple-element.54), channel_id=1, source_target_pairs={{0,127},{1,0},{2,1},{3,2},{4,3},{5,4},{6,5},{7,6},{8,7},{9,8},{10,... | collective-permute-start | bytes 24584 | tf_op jit(solution)/shard_map/ppermute | solution.py:412
  11.2 8.0 %setup.1 = (bf16[160,128,256]{2,1,0:T(8,128)(2,1)S(1)}, s32[2952]{0:T(1024)S(4)}, f32[32,128]{1,0:T(8,128)S(1)}) custom-call(s32[5,32]{1,0:T(8,128)} %bitcast.8, s32[32]{0:T(128)} %lengths.1, s32[1,4,16]{2,1,0:T(4,128)S(4)} %get-tuple-element.45.send, f32[160,128,128]{2,1,0:T(8,128)} %bitcast.7, f32[32,128]{1,0:T(8,128)S(1)} %get-tuple-element.46.field.concentration, ...), custom_call_target="tpu_custom_call" | custom-call | flops 10000000000 | tf_op jit(solution)/shard_map/setup/pallas_call | solution.py:442
  20.1 1.5 %collective-permute-start.5 = (f32[16,128]{1,0:T(8,128)S(1)}, f32[16,128]{1,0:T(8,128)S(1)}, u32[]{:S(2)}, u32[]{:S(2)}) collective-permute-start(f32[16,128]{1,0:T(8,128)S(1)} %get-tuple-element.57), channel_id=1, source_target_pairs={{0,127},{1,3},{2,1},{3,4},{4,2},{5,6},{6,5},{7,8},{8,7},{9,11},{10... | collective-permute-start | bytes 24584 | tf_op jit(solution)/shard_map/ppermute | solution.py:412
  23.6 1.5 %collective-permute-start.7 = (f32[16,128]{1,0:T(8,128)S(1)}, f32[16,128]{1,0:T(8,128)S(1)}, u32[]{:S(2)}, u32[]{:S(2)}) collective-permute-start(f32[16,128]{1,0:T(8,128)S(1)} %get-tuple-element.59), channel_id=1, source_target_pairs={{0,2},{1,0},{2,3},{3,1},{4,5},{5,4},{6,7},{7,6},{8,10},{9,8},{10,1... | collective-permute-start | bytes 24584 | tf_op jit(solution)/shard_map/ppermute | solution.py:412
  25.1 3.6 %collective-permute-done.5.g1 = f32[16,128]{1,0:T(8,128)S(1)} collective-permute-done((f32[16,128]{1,0:T(8,128)S(1)}, f32[16,128]{1,0:T(8,128)S(1)}, u32[]{:S(2)}, u32[]{:S(2)}) %collective-permute-start.5) | collective-permute-done | bytes 8224 | tf_op jit(solution)/shard_map/ppermute | solution.py:412
  29.1 2.4 %collective-permute-done.6.g2 = f32[16,128]{1,0:T(8,128)S(1)} collective-permute-done((f32[16,128]{1,0:T(8,128)S(1)}, f32[16,128]{1,0:T(8,128)S(1)}, u32[]{:S(2)}, u32[]{:S(2)}) %collective-permute-start.6) | collective-permute-done | bytes 8224 | tf_op jit(solution)/shard_map/ppermute | solution.py:412
  34.3 2.8 %collective-permute-start.11 = (f32[16,128]{1,0:T(8,128)S(1)}, f32[16,128]{1,0:T(8,128)S(1)}, u32[]{:S(2)}, u32[]{:S(2)}) collective-permute-start(f32[16,128]{1,0:T(8,128)S(1)} %get-tuple-element.64), channel_id=1, source_target_pairs={{0,2},{1,0},{2,3},{3,1},{4,5},{5,4},{6,7},{7,6},{8,10},{9,8},{10,1... | collective-permute-start | bytes 24584 | tf_op jit(solution)/shard_map/ppermute | solution.py:412
  37.1 3.6 %collective-permute-done.9.g1 = f32[16,128]{1,0:T(8,128)S(1)} collective-permute-done((f32[16,128]{1,0:T(8,128)S(1)}, f32[16,128]{1,0:T(8,128)S(1)}, u32[]{:S(2)}, u32[]{:S(2)}) %collective-permute-start.9) | collective-permute-done | bytes 8224 | tf_op jit(solution)/shard_map/ppermute | solution.py:412
  45.0 2.8 %collective-permute-start.15 = (f32[16,128]{1,0:T(8,128)S(1)}, f32[16,128]{1,0:T(8,128)S(1)}, u32[]{:S(2)}, u32[]{:S(2)}) collective-permute-start(f32[16,128]{1,0:T(8,128)S(1)} %get-tuple-element.69), channel_id=1, source_target_pairs={{0,2},{1,0},{2,3},{3,1},{4,5},{5,4},{6,7},{7,6},{8,10},{9,8},{10,1... | collective-permute-start | bytes 24584 | tf_op jit(solution)/shard_map/ppermute | solution.py:412
  47.8 3.6 %collective-permute-done.13.g1 = f32[16,128]{1,0:T(8,128)S(1)} collective-permute-done((f32[16,128]{1,0:T(8,128)S(1)}, f32[16,128]{1,0:T(8,128)S(1)}, u32[]{:S(2)}, u32[]{:S(2)}) %collective-permute-start.13) | collective-permute-done | bytes 8224 | tf_op jit(solution)/shard_map/ppermute | solution.py:412
  51.8 1.9 %collective-permute-done.14.g2 = f32[16,128]{1,0:T(8,128)S(1)} collective-permute-done((f32[16,128]{1,0:T(8,128)S(1)}, f32[16,128]{1,0:T(8,128)S(1)}, u32[]{:S(2)}, u32[]{:S(2)}) %collective-permute-start.14) | collective-permute-done | bytes 8224 | tf_op jit(solution)/shard_map/ppermute | solution.py:412
  55.6 3.6 %collective-permute-start.19 = (f32[16,128]{1,0:T(8,128)S(1)}, f32[16,128]{1,0:T(8,128)S(1)}, u32[]{:S(2)}, u32[]{:S(2)}) collective-permute-start(f32[16,128]{1,0:T(8,128)S(1)} %get-tuple-element.74), channel_id=1, source_target_pairs={{0,2},{1,0},{2,3},{3,1},{4,5},{5,4},{6,7},{7,6},{8,10},{9,8},{10,1... | collective-permute-start | bytes 24584 | tf_op jit(solution)/shard_map/ppermute | solution.py:412
  59.2 3.6 %collective-permute-done.17.g1 = f32[16,128]{1,0:T(8,128)S(1)} collective-permute-done((f32[16,128]{1,0:T(8,128)S(1)}, f32[16,128]{1,0:T(8,128)S(1)}, u32[]{:S(2)}, u32[]{:S(2)}) %collective-permute-start.17) | collective-permute-done | bytes 8224 | tf_op jit(solution)/shard_map/ppermute | solution.py:412
  66.9 3.0 %collective-permute-start.23 = (f32[16,128]{1,0:T(8,128)S(1)}, f32[16,128]{1,0:T(8,128)S(1)}, u32[]{:S(2)}, u32[]{:S(2)}) collective-permute-start(f32[16,128]{1,0:T(8,128)S(1)} %get-tuple-element.79), channel_id=1, source_target_pairs={{0,2},{1,0},{2,3},{3,1},{4,5},{5,4},{6,7},{7,6},{8,10},{9,8},{10,1... | collective-permute-start | bytes 24584 | tf_op jit(solution)/shard_map/ppermute | solution.py:412
  69.9 3.6 %collective-permute-done.21.g1 = f32[16,128]{1,0:T(8,128)S(1)} collective-permute-done((f32[16,128]{1,0:T(8,128)S(1)}, f32[16,128]{1,0:T(8,128)S(1)}, u32[]{:S(2)}, u32[]{:S(2)}) %collective-permute-start.21) | collective-permute-done | bytes 8224 | tf_op jit(solution)/shard_map/ppermute | solution.py:412
  74.0 1.7 %collective-permute-done.22.g2 = f32[16,128]{1,0:T(8,128)S(1)} collective-permute-done((f32[16,128]{1,0:T(8,128)S(1)}, f32[16,128]{1,0:T(8,128)S(1)}, u32[]{:S(2)}, u32[]{:S(2)}) %collective-permute-start.22) | collective-permute-done | bytes 8224 | tf_op jit(solution)/shard_map/ppermute | solution.py:412
  77.6 3.6 %collective-permute-start.27 = (f32[16,128]{1,0:T(8,128)S(1)}, f32[16,128]{1,0:T(8,128)S(1)}, u32[]{:S(2)}, u32[]{:S(2)}) collective-permute-start(f32[16,128]{1,0:T(8,128)S(1)} %get-tuple-element.84), channel_id=1, source_target_pairs={{0,2},{1,0},{2,3},{3,1},{4,5},{5,4},{6,7},{7,6},{8,10},{9,8},{10,1... | collective-permute-start | bytes 24584 | tf_op jit(solution)/shard_map/ppermute | solution.py:412
  81.2 3.6 %collective-permute-done.25.g1 = f32[16,128]{1,0:T(8,128)S(1)} collective-permute-done((f32[16,128]{1,0:T(8,128)S(1)}, f32[16,128]{1,0:T(8,128)S(1)}, u32[]{:S(2)}, u32[]{:S(2)}) %collective-permute-start.25) | collective-permute-done | bytes 8224 | tf_op jit(solution)/shard_map/ppermute | solution.py:412
  85.2 1.2 %collective-permute-done.26.g2 = f32[16,128]{1,0:T(8,128)S(1)} collective-permute-done((f32[16,128]{1,0:T(8,128)S(1)}, f32[16,128]{1,0:T(8,128)S(1)}, u32[]{:S(2)}, u32[]{:S(2)}) %collective-permute-start.26) | collective-permute-done | bytes 8224 | tf_op jit(solution)/shard_map/ppermute | solution.py:412
  87.6 4.6 %all-to-all-start = ((f32[128,1,32]{2,1,0:T(1,128)}), f32[128,1,32]{2,1,0:T(1,128)S(1)}, u32[]{:S(2)}, u32[]{:S(2)}) async-start(f32[128,1,32]{2,1,0:T(1,128)} %bitcast.3), calls=%async_computation | async-start | bytes 131072 | tf_op jit(solution)/shard_map/all_to_all | solution.py:509
  92.8 8.7 %all-to-all-done = f32[128,1,32]{2,1,0:T(1,128)S(1)} async-done(((f32[128,1,32]{2,1,0:T(1,128)}), f32[128,1,32]{2,1,0:T(1,128)S(1)}, u32[]{:S(2)}, u32[]{:S(2)}) %all-to-all-start) | async-done | bytes 16416 | tf_op jit(solution)/shard_map/all_to_all | solution.py:509
  101.5 1.3 %finish.1 = f32[32,128]{1,0:T(8,128)} custom-call(f32[1]{0:T(128)S(6)} %copy.9.step, f32[128,32]{1,0:T(8,128)S(1)} %bitcast.6, f32[32,128]{1,0:T(8,128)S(1)} %get-tuple-element.46.field.concentration, f32[32,128]{1,0:T(8,128)S(1)} %get-tuple-element.55.field.refs_0_.rest_0_, f32[32,128]{1,0:T(8,128)S(1)} %get-tuple-element.60.field.refs_1_.rest_1_, ...), custom_call_target="tpu_custom_call" | custom-call | tf_op jit(solution)/shard_map/finish/pallas_call | solution.py:510
  (57 shorter events, 21.4 us)
Async XLA Ops:
  0.8 18.3 %collective-permute-start = (f32[16,128]{1,0:T(8,128)S(1)}, f32[16,128]{1,0:T(8,128)S(1)}, u32[]{:S(2)}, u32[]{:S(2)}) collective-permute-start(f32[16,128]{1,0:T(8,128)S(1)} %get-tuple-element.51), channel_id=1, source_target_pairs={{0,1},{1,2},{2,3},{3,4},{4,5},{5,6},{6,7},{7,8},{8,9},{9,10},{10,1... | collective-permute-start | bytes 24584 | tf_op jit(solution)/shard_map/ppermute | solution.py:412
  0.9 18.2 %collective-permute-start.1 = (f32[16,128]{1,0:T(8,128)S(1)}, f32[16,128]{1,0:T(8,128)S(1)}, u32[]{:S(2)}, u32[]{:S(2)}) collective-permute-start(f32[16,128]{1,0:T(8,128)S(1)} %get-tuple-element.52), channel_id=1, source_target_pairs={{0,2},{1,3},{2,4},{3,5},{4,6},{5,7},{6,8},{7,9},{8,10},{9,11},{10,... | collective-permute-start | bytes 24584 | tf_op jit(solution)/shard_map/ppermute | solution.py:412
  2.6 16.6 %collective-permute-start.2 = (f32[16,128]{1,0:T(8,128)S(1)}, f32[16,128]{1,0:T(8,128)S(1)}, u32[]{:S(2)}, u32[]{:S(2)}) collective-permute-start(f32[16,128]{1,0:T(8,128)S(1)} %get-tuple-element.53), channel_id=1, source_target_pairs={{0,126},{1,127},{2,0},{3,1},{4,2},{5,3},{6,4},{7,5},{8,6},{9,7},{1... | collective-permute-start | bytes 24584 | tf_op jit(solution)/shard_map/ppermute | solution.py:412
  9.8 9.3 %collective-permute-start.3 = (f32[16,128]{1,0:T(8,128)S(1)}, f32[16,128]{1,0:T(8,128)S(1)}, u32[]{:S(2)}, u32[]{:S(2)}) collective-permute-start(f32[16,128]{1,0:T(8,128)S(1)} %get-tuple-element.54), channel_id=1, source_target_pairs={{0,127},{1,0},{2,1},{3,2},{4,3},{5,4},{6,5},{7,6},{8,7},{9,8},{10,... | collective-permute-start | bytes 24584 | tf_op jit(solution)/shard_map/ppermute | solution.py:412
  20.1 8.6 %collective-permute-start.5 = (f32[16,128]{1,0:T(8,128)S(1)}, f32[16,128]{1,0:T(8,128)S(1)}, u32[]{:S(2)}, u32[]{:S(2)}) collective-permute-start(f32[16,128]{1,0:T(8,128)S(1)} %get-tuple-element.57), channel_id=1, source_target_pairs={{0,127},{1,3},{2,1},{3,4},{4,2},{5,6},{6,5},{7,8},{8,7},{9,11},{10... | collective-permute-start | bytes 24584 | tf_op jit(solution)/shard_map/ppermute | solution.py:412
  22.4 9.2 %collective-permute-start.6 = (f32[16,128]{1,0:T(8,128)S(1)}, f32[16,128]{1,0:T(8,128)S(1)}, u32[]{:S(2)}, u32[]{:S(2)}) collective-permute-start(f32[16,128]{1,0:T(8,128)S(1)} %get-tuple-element.58), channel_id=1, source_target_pairs={{0,126},{1,2},{2,4},{3,5},{4,3},{5,7},{6,8},{7,9},{8,6},{9,10},{10... | collective-permute-start | bytes 24584 | tf_op jit(solution)/shard_map/ppermute | solution.py:412
  23.6 8.0 %collective-permute-start.7 = (f32[16,128]{1,0:T(8,128)S(1)}, f32[16,128]{1,0:T(8,128)S(1)}, u32[]{:S(2)}, u32[]{:S(2)}) collective-permute-start(f32[16,128]{1,0:T(8,128)S(1)} %get-tuple-element.59), channel_id=1, source_target_pairs={{0,2},{1,0},{2,3},{3,1},{4,5},{5,4},{6,7},{7,6},{8,10},{9,8},{10,1... | collective-permute-start | bytes 24584 | tf_op jit(solution)/shard_map/ppermute | solution.py:412
  32.2 8.6 %collective-permute-start.9 = (f32[16,128]{1,0:T(8,128)S(1)}, f32[16,128]{1,0:T(8,128)S(1)}, u32[]{:S(2)}, u32[]{:S(2)}) collective-permute-start(f32[16,128]{1,0:T(8,128)S(1)} %get-tuple-element.62), channel_id=1, source_target_pairs={{0,127},{1,3},{2,1},{3,4},{4,2},{5,6},{6,5},{7,8},{8,7},{9,11},{10... | collective-permute-start | bytes 24584 | tf_op jit(solution)/shard_map/ppermute | solution.py:412
  33.1 9.2 %collective-permute-start.10 = (f32[16,128]{1,0:T(8,128)S(1)}, f32[16,128]{1,0:T(8,128)S(1)}, u32[]{:S(2)}, u32[]{:S(2)}) collective-permute-start(f32[16,128]{1,0:T(8,128)S(1)} %get-tuple-element.63), channel_id=1, source_target_pairs={{0,126},{1,2},{2,4},{3,5},{4,3},{5,7},{6,8},{7,9},{8,6},{9,10},{10... | collective-permute-start | bytes 24584 | tf_op jit(solution)/shard_map/ppermute | solution.py:412
  34.3 8.0 %collective-permute-start.11 = (f32[16,128]{1,0:T(8,128)S(1)}, f32[16,128]{1,0:T(8,128)S(1)}, u32[]{:S(2)}, u32[]{:S(2)}) collective-permute-start(f32[16,128]{1,0:T(8,128)S(1)} %get-tuple-element.64), channel_id=1, source_target_pairs={{0,2},{1,0},{2,3},{3,1},{4,5},{5,4},{6,7},{7,6},{8,10},{9,8},{10,1... | collective-permute-start | bytes 24584 | tf_op jit(solution)/shard_map/ppermute | solution.py:412
  42.8 8.6 %collective-permute-start.13 = (f32[16,128]{1,0:T(8,128)S(1)}, f32[16,128]{1,0:T(8,128)S(1)}, u32[]{:S(2)}, u32[]{:S(2)}) collective-permute-start(f32[16,128]{1,0:T(8,128)S(1)} %get-tuple-element.67), channel_id=1, source_target_pairs={{0,127},{1,3},{2,1},{3,4},{4,2},{5,6},{6,5},{7,8},{8,7},{9,11},{10... | collective-permute-start | bytes 24584 | tf_op jit(solution)/shard_map/ppermute | solution.py:412
  44.6 9.2 %collective-permute-start.14 = (f32[16,128]{1,0:T(8,128)S(1)}, f32[16,128]{1,0:T(8,128)S(1)}, u32[]{:S(2)}, u32[]{:S(2)}) collective-permute-start(f32[16,128]{1,0:T(8,128)S(1)} %get-tuple-element.68), channel_id=1, source_target_pairs={{0,126},{1,2},{2,4},{3,5},{4,3},{5,7},{6,8},{7,9},{8,6},{9,10},{10... | collective-permute-start | bytes 24584 | tf_op jit(solution)/shard_map/ppermute | solution.py:412
  45.0 8.8 %collective-permute-start.15 = (f32[16,128]{1,0:T(8,128)S(1)}, f32[16,128]{1,0:T(8,128)S(1)}, u32[]{:S(2)}, u32[]{:S(2)}) collective-permute-start(f32[16,128]{1,0:T(8,128)S(1)} %get-tuple-element.69), channel_id=1, source_target_pairs={{0,2},{1,0},{2,3},{3,1},{4,5},{5,4},{6,7},{7,6},{8,10},{9,8},{10,1... | collective-permute-start | bytes 24584 | tf_op jit(solution)/shard_map/ppermute | solution.py:412
  54.3 8.6 %collective-permute-start.17 = (f32[16,128]{1,0:T(8,128)S(1)}, f32[16,128]{1,0:T(8,128)S(1)}, u32[]{:S(2)}, u32[]{:S(2)}) collective-permute-start(f32[16,128]{1,0:T(8,128)S(1)} %get-tuple-element.72), channel_id=1, source_target_pairs={{0,127},{1,3},{2,1},{3,4},{4,2},{5,6},{6,5},{7,8},{8,7},{9,11},{10... | collective-permute-start | bytes 24584 | tf_op jit(solution)/shard_map/ppermute | solution.py:412
  55.2 9.2 %collective-permute-start.18 = (f32[16,128]{1,0:T(8,128)S(1)}, f32[16,128]{1,0:T(8,128)S(1)}, u32[]{:S(2)}, u32[]{:S(2)}) collective-permute-start(f32[16,128]{1,0:T(8,128)S(1)} %get-tuple-element.73), channel_id=1, source_target_pairs={{0,126},{1,2},{2,4},{3,5},{4,3},{5,7},{6,8},{7,9},{8,6},{9,10},{10... | collective-permute-start | bytes 24584 | tf_op jit(solution)/shard_map/ppermute | solution.py:412
  55.6 8.8 %collective-permute-start.19 = (f32[16,128]{1,0:T(8,128)S(1)}, f32[16,128]{1,0:T(8,128)S(1)}, u32[]{:S(2)}, u32[]{:S(2)}) collective-permute-start(f32[16,128]{1,0:T(8,128)S(1)} %get-tuple-element.74), channel_id=1, source_target_pairs={{0,2},{1,0},{2,3},{3,1},{4,5},{5,4},{6,7},{7,6},{8,10},{9,8},{10,1... | collective-permute-start | bytes 24584 | tf_op jit(solution)/shard_map/ppermute | solution.py:412
  65.0 8.6 %collective-permute-start.21 = (f32[16,128]{1,0:T(8,128)S(1)}, f32[16,128]{1,0:T(8,128)S(1)}, u32[]{:S(2)}, u32[]{:S(2)}) collective-permute-start(f32[16,128]{1,0:T(8,128)S(1)} %get-tuple-element.77), channel_id=1, source_target_pairs={{0,127},{1,3},{2,1},{3,4},{4,2},{5,6},{6,5},{7,8},{8,7},{9,11},{10... | collective-permute-start | bytes 24584 | tf_op jit(solution)/shard_map/ppermute | solution.py:412
  66.5 9.2 %collective-permute-start.22 = (f32[16,128]{1,0:T(8,128)S(1)}, f32[16,128]{1,0:T(8,128)S(1)}, u32[]{:S(2)}, u32[]{:S(2)}) collective-permute-start(f32[16,128]{1,0:T(8,128)S(1)} %get-tuple-element.78), channel_id=1, source_target_pairs={{0,126},{1,2},{2,4},{3,5},{4,3},{5,7},{6,8},{7,9},{8,6},{9,10},{10... | collective-permute-start | bytes 24584 | tf_op jit(solution)/shard_map/ppermute | solution.py:412
  66.9 8.7 %collective-permute-start.23 = (f32[16,128]{1,0:T(8,128)S(1)}, f32[16,128]{1,0:T(8,128)S(1)}, u32[]{:S(2)}, u32[]{:S(2)}) collective-permute-start(f32[16,128]{1,0:T(8,128)S(1)} %get-tuple-element.79), channel_id=1, source_target_pairs={{0,2},{1,0},{2,3},{3,1},{4,5},{5,4},{6,7},{7,6},{8,10},{9,8},{10,1... | collective-permute-start | bytes 24584 | tf_op jit(solution)/shard_map/ppermute | solution.py:412
  76.1 5.1 %collective-permute-start.24 = (f32[16,128]{1,0:T(8,128)S(1)}, f32[16,128]{1,0:T(8,128)S(1)}, u32[]{:S(2)}, u32[]{:S(2)}) collective-permute-start(f32[16,128]{1,0:T(8,128)S(1)} %get-tuple-element.81), channel_id=1, source_target_pairs={{0,1},{1,127},{2,0},{3,2},{4,6},{5,3},{6,4},{7,5},{8,9},{9,7},{10,... | collective-permute-start | bytes 24584 | tf_op jit(solution)/shard_map/ppermute | solution.py:412
  76.2 8.6 %collective-permute-start.25 = (f32[16,128]{1,0:T(8,128)S(1)}, f32[16,128]{1,0:T(8,128)S(1)}, u32[]{:S(2)}, u32[]{:S(2)}) collective-permute-start(f32[16,128]{1,0:T(8,128)S(1)} %get-tuple-element.82), channel_id=1, source_target_pairs={{0,127},{1,3},{2,1},{3,4},{4,2},{5,6},{6,5},{7,8},{8,7},{9,11},{10... | collective-permute-start | bytes 24584 | tf_op jit(solution)/shard_map/ppermute | solution.py:412
  77.2 9.2 %collective-permute-start.26 = (f32[16,128]{1,0:T(8,128)S(1)}, f32[16,128]{1,0:T(8,128)S(1)}, u32[]{:S(2)}, u32[]{:S(2)}) collective-permute-start(f32[16,128]{1,0:T(8,128)S(1)} %get-tuple-element.83), channel_id=1, source_target_pairs={{0,126},{1,2},{2,4},{3,5},{4,3},{5,7},{6,8},{7,9},{8,6},{9,10},{10... | collective-permute-start | bytes 24584 | tf_op jit(solution)/shard_map/ppermute | solution.py:412
  77.6 8.8 %collective-permute-start.27 = (f32[16,128]{1,0:T(8,128)S(1)}, f32[16,128]{1,0:T(8,128)S(1)}, u32[]{:S(2)}, u32[]{:S(2)}) collective-permute-start(f32[16,128]{1,0:T(8,128)S(1)} %get-tuple-element.84), channel_id=1, source_target_pairs={{0,2},{1,0},{2,3},{3,1},{4,5},{5,4},{6,7},{7,6},{8,10},{9,8},{10,1... | collective-permute-start | bytes 24584 | tf_op jit(solution)/shard_map/ppermute | solution.py:412
  87.6 13.9 %all-to-all-start = ((f32[128,1,32]{2,1,0:T(1,128)}), f32[128,1,32]{2,1,0:T(1,128)S(1)}, u32[]{:S(2)}, u32[]{:S(2)}) async-start(f32[128,1,32]{2,1,0:T(1,128)} %bitcast.3), calls=%async_computation | async-start | bytes 131072 | tf_op jit(solution)/shard_map/all_to_all | solution.py:509
  (5 other events, 25.2 us)

commit v8 on v7

--- a/solution.py
+++ b/solution.py
@@ -1,3 +1,5 @@
+import math
+
 import jax
 import jax.numpy as jnp
 from jax import lax
@@ -131,41 +133,39 @@
 
     spots = (at[0] | (at[1] << 8)) | ((at[2] << 16) | (at[3] << 24))
 
-    def listed(b, carry):
+    def rows(pair, carry):
         near, far, mid = carry
-        length = length_of[b]
-        for s in range(SLOTS):
-            column = where[s, b]
-            index = jnp.maximum(column - ROWS, 0)
-            spot = (spots >> ((index >> 4) << 3)) & 7
-            live = s < length
-            ghost = jnp.logical_and(live, column >= ROWS)
-            home = jnp.logical_and(live, column < ROWS)
-            first = jnp.logical_and(ghost, spot >= FAR_BY[0])
-            second = jnp.logical_and(ghost, spot < FAR_BY[0])
-            base = jnp.where(
-                home, NEAR + near, jnp.where(first, FAR + far, jnp.where(second, MID + mid, REST))
-            )
-            table[base] = jnp.where(ghost, (spot << 4) + (index & 15), column)
-            table[base + LIST] = b * SLOTS + s
-            table[base + 2 * LIST] = b
-            near = near + home.astype(jnp.int32)
-            far = far + first.astype(jnp.int32)
-            mid = mid + second.astype(jnp.int32)
-        return near, far, mid
-
-    def turn(pair, carry):
         fetch(pair).wait()
+        for half in range(2):
+            b = pair * 2 + half
+            length = length_of[b]
+            for s in range(SLOTS):
+                column = where[s, b]
+                index = jnp.maximum(column - ROWS, 0)
+                spot = (spots >> ((index >> 4) << 3)) & 7
+                live = s < length
+                ghost = jnp.logical_and(live, column >= ROWS)
+                home = jnp.logical_and(live, column < ROWS)
+                first = jnp.logical_and(ghost, spot >= FAR_BY[0])
+                second = jnp.logical_and(ghost, spot < FAR_BY[0])
+                base = jnp.where(
+                    home, NEAR + near, jnp.where(first, FAR + far, jnp.where(second, MID + mid, REST))
+                )
+                table[base] = jnp.where(ghost, (spot << 4) + (index & 15), column)
+                table[base + LIST] = b * SLOTS + s
+                table[base + 2 * LIST] = b
+                near = near + home.astype(jnp.int32)
+                far = far + first.astype(jnp.int32)
+                mid = mid + second.astype(jnp.int32)
         for s in range(2 * SLOTS):
             slot = pair * 2 * SLOTS + s
             high, rest = split(jnp.transpose(blocks[slot]))
             turned[slot, :, 0:BLK] = high
             turned[slot, :, BLK : 2 * BLK] = rest
-        return carry
+        return near, far, mid
 
     zero = jnp.int32(0)
-    counts = lax.fori_loop(0, ROWS, listed, (zero, zero, zero))
-    lax.fori_loop(0, ROWS // 2, turn, 0)
+    counts = lax.fori_loop(0, ROWS // 2, rows, (zero, zero, zero))
     for i, base in enumerate((NEAR, FAR, MID)):
         table[COUNTS + i] = counts[i]
         for g in range(GROUPS[i]):
@@ -288,9 +288,17 @@
     return out
 
 
+def tree(terms):
+    terms = list(terms)
+    while len(terms) > 1:
+        odd = [terms[-1]] if len(terms) % 2 else []
+        terms = [x + y for x, y in zip(terms[::2], terms[1::2])] + odd
+    return terms[0] if terms else None
+
+
 def through(gram, v):
     return [
-        (lambda terms: None if not terms else sum(terms[1:], terms[0]))(
+        tree(
             [gram[min(a, b), max(a, b)] * v[b] for b in range(DEGREE + 1) if v[b] is not None and (a, b) != (DEGREE, DEGREE)]
         )
         for a in range(DEGREE + 1)
@@ -298,8 +306,7 @@
 
 
 def dot(u, v):
-    terms = [x * y for x, y in zip(u, v) if x is not None and y is not None]
-    return sum(terms[1:], terms[0])
+    return tree([x * y for x, y in zip(u, v) if x is not None and y is not None])
 
 
 def scaled(v, x):
@@ -308,37 +315,42 @@
 
 def phi_weights(h, substep):
     n = len(h)
-    reduced = [[None if x is None else x * substep * (1.0 / 64.0) for x in r] for r in h]
-    matmul = lambda p, q: [
-        [
-            (lambda ts: None if not ts else sum(ts[1:], ts[0]))(
-                [p[i][k] * q[k][j] for k in range(n) if p[i][k] is not None and q[k][j] is not None]
-            )
-            for j in range(n)
-        ]
+    one = [[None if x is None else x * substep * (1.0 / 64.0) for x in r] for r in h]
+
+    def matmul(p, q):
+        pick = lambda i, j: [p[i][k] * q[k][j] for k in range(n) if p[i][k] is not None]
+        return [[tree(pick(i, j)) for j in range(n)] for i in range(n)]
+
+    def apply(p, q):
+        return [tree([p[i][k] * q[k] for k in range(n)]) for i in range(n)]
+
+    two = [
+        [tree([one[i][k] * one[k][j] for k in range(n) if one[i][k] is not None and one[k][j] is not None]) for j in range(n)]
         for i in range(n)
     ]
-    apply = lambda p, q: [
-        (lambda ts: None if not ts else sum(ts[1:], ts[0]))(
-            [p[i][k] * q[k] for k in range(n) if p[i][k] is not None and q[k] is not None]
-        )
-        for i in range(n)
-    ]
-    block = [[1.0 if i == j else None for j in range(n)] for i in range(n)]
-    column = [None] * n
-    for degree in range(12, 0, -1):
-        inverse = 1.0 / degree
-        block = matmul(reduced, block)
-        block = [[None if x is None else x * inverse for x in r] for r in block]
-        for i in range(n):
-            block[i][i] = add(block[i][i], 1.0)
-        column = apply(reduced, column)
-        column[0] = add(column[0], 1.0 / 64.0)
-        column = [None if x is None else x * inverse for x in column]
-    for _ in range(6):
+    three = matmul(one, two)
+    factor = [1.0 / math.factorial(k) for k in range(13)]
+
+    def low(i, j, k):
+        total = add(None if one[i][j] is None else one[i][j] * factor[k + 1], two[i][j] * factor[k + 2])
+        return total + factor[k] if i == j else total
+
+    def low_column(i, k):
+        total = add(None if one[i][0] is None else one[i][0] * factor[k + 1], two[i][0] * factor[k + 2])
+        return total + factor[k] if i == 0 else total
+
+    block = [[three[i][j] * factor[12] + low(i, j, 9) for j in range(n)] for i in range(n)]
+    column = [low_column(i, 10) for i in range(n)]
+    for k in (6, 3, 0):
+        block, column = matmul(three, block), apply(three, column)
+        block = [[block[i][j] + low(i, j, k) for j in range(n)] for i in range(n)]
+        column = [column[i] + low_column(i, k + 1) for i in range(n)]
+    column = [x * (1.0 / 64.0) for x in column]
+    for turn in range(6):
         moved = apply(block, column)
-        column = [add(x, y) for x, y in zip(moved, column)]
-        block = matmul(block, block)
+        column = [x + y for x, y in zip(moved, column)]
+        if turn < 5:
+            block = matmul(block, block)
     return column
 
 

time: 103 us -> 103 us (level)
  no operation moved by 1% of the time
where the time goes in v8:
time: 103 us; the launch traced here: 102 us
  starting transfers between devices  40 us (39%)
  waiting for transfers between devices  39.9 us (39%)
  Pallas kernels  21.5 us (21%)
    ppermute x28, starting transfers between devices, exchange(): arrived.append(lax.ppermute(packets[t], 'dom', by[t]))  35.4 us
    ppermute x28, waiting for transfers between devices, exchange(): arrived.append(lax.ppermute(packets[t], 'dom', by[t]))  31.2 us
    all_to_all x1, waiting for transfers between devices, shards(): lax.all_to_all(sums, 'dom', split_axis=0, concat_axis=0, tiled=True)  8.67 us
    pallas_call x1, Pallas kernels, shards(): pl.pallas_call(setup, out_shape=[pltpu.VMEM((ENTRIES, BLK, 2 * BLK), bf16...  7.72 us
    pallas_call x6, Pallas kernels, shards(): pl.pallas_call(near_part, out_shape=FIELD, in_specs=smem() + vmem(4), out...  4.97 us
    all_to_all x1, starting transfers between devices, shards(): lax.all_to_all(sums, 'dom', split_axis=0, concat_axis=0, tiled=True)  4.59 us
    pallas_call x6, Pallas kernels, shards(): pl.pallas_call(far_part if k else first_far_part, out_shape=[FIELD] + [PA...  3.25 us
    pallas_call x6, Pallas kernels, middle(): pl.pallas_call(middle_part, out_shape=FIELD, in_specs=smem() + vmem(2 + l...  2.44 us
  transfers between devices with their start and end apart: 29, of which 13 were waited for; matrix products, arithmetic and copies ran while one was open for 0% of the time, Pallas kernels for 15%

profile of v8, /device:TPU:0, one launch (start us, length us, event | category | flops | bytes accessed | tf_op | source)
XLA Modules:
  0.0 102.4 jit_solution(13010594852110032558)
XLA Ops:
  0.9 1.7 %collective-permute-start.1 = (f32[16,128]{1,0:T(8,128)S(1)}, f32[16,128]{1,0:T(8,128)S(1)}, u32[]{:S(2)}, u32[]{:S(2)}) collective-permute-start(f32[16,128]{1,0:T(8,128)S(1)} %get-tuple-element.52), channel_id=1, source_target_pairs={{0,2},{1,3},{2,4},{3,5},{4,6},{5,7},{6,8},{7,9},{8,10},{9,11},{10,... | collective-permute-start | bytes 24584 | tf_op jit(solution)/shard_map/ppermute | solution.py:424
  2.6 7.3 %collective-permute-start.2 = (f32[16,128]{1,0:T(8,128)S(1)}, f32[16,128]{1,0:T(8,128)S(1)}, u32[]{:S(2)}, u32[]{:S(2)}) collective-permute-start(f32[16,128]{1,0:T(8,128)S(1)} %get-tuple-element.53), channel_id=1, source_target_pairs={{0,126},{1,127},{2,0},{3,1},{4,2},{5,3},{6,4},{7,5},{8,6},{9,7},{1... | collective-permute-start | bytes 24584 | tf_op jit(solution)/shard_map/ppermute | solution.py:424
  9.8 1.3 %collective-permute-start.3 = (f32[16,128]{1,0:T(8,128)S(1)}, f32[16,128]{1,0:T(8,128)S(1)}, u32[]{:S(2)}, u32[]{:S(2)}) collective-permute-start(f32[16,128]{1,0:T(8,128)S(1)} %get-tuple-element.54), channel_id=1, source_target_pairs={{0,127},{1,0},{2,1},{3,2},{4,3},{5,4},{6,5},{7,6},{8,7},{9,8},{10,... | collective-permute-start | bytes 24584 | tf_op jit(solution)/shard_map/ppermute | solution.py:424
  11.2 7.7 %setup.1 = (bf16[160,128,256]{2,1,0:T(8,128)(2,1)S(1)}, s32[2952]{0:T(1024)S(4)}, f32[32,128]{1,0:T(8,128)S(1)}) custom-call(s32[5,32]{1,0:T(8,128)} %bitcast.8, s32[32]{0:T(128)} %lengths.1, s32[1,4,16]{2,1,0:T(4,128)S(4)} %get-tuple-element.45.send, f32[160,128,128]{2,1,0:T(8,128)} %bitcast.7, f32[32,128]{1,0:T(8,128)S(1)} %get-tuple-element.46.field.concentration, ...), custom_call_target="tpu_custom_call" | custom-call | flops 10000000000 | tf_op jit(solution)/shard_map/setup/pallas_call | solution.py:454
  19.9 1.5 %collective-permute-start.5 = (f32[16,128]{1,0:T(8,128)S(1)}, f32[16,128]{1,0:T(8,128)S(1)}, u32[]{:S(2)}, u32[]{:S(2)}) collective-permute-start(f32[16,128]{1,0:T(8,128)S(1)} %get-tuple-element.57), channel_id=1, source_target_pairs={{0,127},{1,3},{2,1},{3,4},{4,2},{5,6},{6,5},{7,8},{8,7},{9,11},{10... | collective-permute-start | bytes 24584 | tf_op jit(solution)/shard_map/ppermute | solution.py:424
  23.4 1.5 %collective-permute-start.7 = (f32[16,128]{1,0:T(8,128)S(1)}, f32[16,128]{1,0:T(8,128)S(1)}, u32[]{:S(2)}, u32[]{:S(2)}) collective-permute-start(f32[16,128]{1,0:T(8,128)S(1)} %get-tuple-element.59), channel_id=1, source_target_pairs={{0,2},{1,0},{2,3},{3,1},{4,5},{5,4},{6,7},{7,6},{8,10},{9,8},{10,1... | collective-permute-start | bytes 24584 | tf_op jit(solution)/shard_map/ppermute | solution.py:424
  24.9 3.6 %collective-permute-done.5.g1 = f32[16,128]{1,0:T(8,128)S(1)} collective-permute-done((f32[16,128]{1,0:T(8,128)S(1)}, f32[16,128]{1,0:T(8,128)S(1)}, u32[]{:S(2)}, u32[]{:S(2)}) %collective-permute-start.5) | collective-permute-done | bytes 8224 | tf_op jit(solution)/shard_map/ppermute | solution.py:424
  28.9 2.4 %collective-permute-done.6.g2 = f32[16,128]{1,0:T(8,128)S(1)} collective-permute-done((f32[16,128]{1,0:T(8,128)S(1)}, f32[16,128]{1,0:T(8,128)S(1)}, u32[]{:S(2)}, u32[]{:S(2)}) %collective-permute-start.6) | collective-permute-done | bytes 8224 | tf_op jit(solution)/shard_map/ppermute | solution.py:424
  32.9 1.2 %collective-permute-start.10 = (f32[16,128]{1,0:T(8,128)S(1)}, f32[16,128]{1,0:T(8,128)S(1)}, u32[]{:S(2)}, u32[]{:S(2)}) collective-permute-start(f32[16,128]{1,0:T(8,128)S(1)} %get-tuple-element.63), channel_id=1, source_target_pairs={{0,126},{1,2},{2,4},{3,5},{4,3},{5,7},{6,8},{7,9},{8,6},{9,10},{10... | collective-permute-start | bytes 24584 | tf_op jit(solution)/shard_map/ppermute | solution.py:424
  34.1 2.8 %collective-permute-start.11 = (f32[16,128]{1,0:T(8,128)S(1)}, f32[16,128]{1,0:T(8,128)S(1)}, u32[]{:S(2)}, u32[]{:S(2)}) collective-permute-start(f32[16,128]{1,0:T(8,128)S(1)} %get-tuple-element.64), channel_id=1, source_target_pairs={{0,2},{1,0},{2,3},{3,1},{4,5},{5,4},{6,7},{7,6},{8,10},{9,8},{10,1... | collective-permute-start | bytes 24584 | tf_op jit(solution)/shard_map/ppermute | solution.py:424
  36.9 3.6 %collective-permute-done.9.g1 = f32[16,128]{1,0:T(8,128)S(1)} collective-permute-done((f32[16,128]{1,0:T(8,128)S(1)}, f32[16,128]{1,0:T(8,128)S(1)}, u32[]{:S(2)}, u32[]{:S(2)}) %collective-permute-start.9) | collective-permute-done | bytes 8224 | tf_op jit(solution)/shard_map/ppermute | solution.py:424
  44.7 2.8 %collective-permute-start.15 = (f32[16,128]{1,0:T(8,128)S(1)}, f32[16,128]{1,0:T(8,128)S(1)}, u32[]{:S(2)}, u32[]{:S(2)}) collective-permute-start(f32[16,128]{1,0:T(8,128)S(1)} %get-tuple-element.69), channel_id=1, source_target_pairs={{0,2},{1,0},{2,3},{3,1},{4,5},{5,4},{6,7},{7,6},{8,10},{9,8},{10,1... | collective-permute-start | bytes 24584 | tf_op jit(solution)/shard_map/ppermute | solution.py:424
  47.5 3.6 %collective-permute-done.13.g1 = f32[16,128]{1,0:T(8,128)S(1)} collective-permute-done((f32[16,128]{1,0:T(8,128)S(1)}, f32[16,128]{1,0:T(8,128)S(1)}, u32[]{:S(2)}, u32[]{:S(2)}) %collective-permute-start.13) | collective-permute-done | bytes 8224 | tf_op jit(solution)/shard_map/ppermute | solution.py:424
  51.6 1.9 %collective-permute-done.14.g2 = f32[16,128]{1,0:T(8,128)S(1)} collective-permute-done((f32[16,128]{1,0:T(8,128)S(1)}, f32[16,128]{1,0:T(8,128)S(1)}, u32[]{:S(2)}, u32[]{:S(2)}) %collective-permute-start.14) | collective-permute-done | bytes 8224 | tf_op jit(solution)/shard_map/ppermute | solution.py:424
  55.4 3.6 %collective-permute-start.19 = (f32[16,128]{1,0:T(8,128)S(1)}, f32[16,128]{1,0:T(8,128)S(1)}, u32[]{:S(2)}, u32[]{:S(2)}) collective-permute-start(f32[16,128]{1,0:T(8,128)S(1)} %get-tuple-element.74), channel_id=1, source_target_pairs={{0,2},{1,0},{2,3},{3,1},{4,5},{5,4},{6,7},{7,6},{8,10},{9,8},{10,1... | collective-permute-start | bytes 24584 | tf_op jit(solution)/shard_map/ppermute | solution.py:424
  59.0 3.6 %collective-permute-done.17.g1 = f32[16,128]{1,0:T(8,128)S(1)} collective-permute-done((f32[16,128]{1,0:T(8,128)S(1)}, f32[16,128]{1,0:T(8,128)S(1)}, u32[]{:S(2)}, u32[]{:S(2)}) %collective-permute-start.17) | collective-permute-done | bytes 8224 | tf_op jit(solution)/shard_map/ppermute | solution.py:424
  66.7 3.0 %collective-permute-start.23 = (f32[16,128]{1,0:T(8,128)S(1)}, f32[16,128]{1,0:T(8,128)S(1)}, u32[]{:S(2)}, u32[]{:S(2)}) collective-permute-start(f32[16,128]{1,0:T(8,128)S(1)} %get-tuple-element.79), channel_id=1, source_target_pairs={{0,2},{1,0},{2,3},{3,1},{4,5},{5,4},{6,7},{7,6},{8,10},{9,8},{10,1... | collective-permute-start | bytes 24584 | tf_op jit(solution)/shard_map/ppermute | solution.py:424
  69.7 3.6 %collective-permute-done.21.g1 = f32[16,128]{1,0:T(8,128)S(1)} collective-permute-done((f32[16,128]{1,0:T(8,128)S(1)}, f32[16,128]{1,0:T(8,128)S(1)}, u32[]{:S(2)}, u32[]{:S(2)}) %collective-permute-start.21) | collective-permute-done | bytes 8224 | tf_op jit(solution)/shard_map/ppermute | solution.py:424
  73.7 1.7 %collective-permute-done.22.g2 = f32[16,128]{1,0:T(8,128)S(1)} collective-permute-done((f32[16,128]{1,0:T(8,128)S(1)}, f32[16,128]{1,0:T(8,128)S(1)}, u32[]{:S(2)}, u32[]{:S(2)}) %collective-permute-start.22) | collective-permute-done | bytes 8224 | tf_op jit(solution)/shard_map/ppermute | solution.py:424
  77.4 3.6 %collective-permute-start.27 = (f32[16,128]{1,0:T(8,128)S(1)}, f32[16,128]{1,0:T(8,128)S(1)}, u32[]{:S(2)}, u32[]{:S(2)}) collective-permute-start(f32[16,128]{1,0:T(8,128)S(1)} %get-tuple-element.84), channel_id=1, source_target_pairs={{0,2},{1,0},{2,3},{3,1},{4,5},{5,4},{6,7},{7,6},{8,10},{9,8},{10,1... | collective-permute-start | bytes 24584 | tf_op jit(solution)/shard_map/ppermute | solution.py:424
  81.0 3.6 %collective-permute-done.25.g1 = f32[16,128]{1,0:T(8,128)S(1)} collective-permute-done((f32[16,128]{1,0:T(8,128)S(1)}, f32[16,128]{1,0:T(8,128)S(1)}, u32[]{:S(2)}, u32[]{:S(2)}) %collective-permute-start.25) | collective-permute-done | bytes 8224 | tf_op jit(solution)/shard_map/ppermute | solution.py:424
  85.0 1.2 %collective-permute-done.26.g2 = f32[16,128]{1,0:T(8,128)S(1)} collective-permute-done((f32[16,128]{1,0:T(8,128)S(1)}, f32[16,128]{1,0:T(8,128)S(1)}, u32[]{:S(2)}, u32[]{:S(2)}) %collective-permute-start.26) | collective-permute-done | bytes 8224 | tf_op jit(solution)/shard_map/ppermute | solution.py:424
  87.3 4.6 %all-to-all-start = ((f32[128,1,32]{2,1,0:T(1,128)}), f32[128,1,32]{2,1,0:T(1,128)S(1)}, u32[]{:S(2)}, u32[]{:S(2)}) async-start(f32[128,1,32]{2,1,0:T(1,128)} %bitcast.3), calls=%async_computation | async-start | bytes 131072 | tf_op jit(solution)/shard_map/all_to_all | solution.py:521
  92.6 8.7 %all-to-all-done = f32[128,1,32]{2,1,0:T(1,128)S(1)} async-done(((f32[128,1,32]{2,1,0:T(1,128)}), f32[128,1,32]{2,1,0:T(1,128)S(1)}, u32[]{:S(2)}, u32[]{:S(2)}) %all-to-all-start) | async-done | bytes 16416 | tf_op jit(solution)/shard_map/all_to_all | solution.py:521
  (57 shorter events, 21.4 us)
Async XLA Ops:
  0.8 18.1 %collective-permute-start = (f32[16,128]{1,0:T(8,128)S(1)}, f32[16,128]{1,0:T(8,128)S(1)}, u32[]{:S(2)}, u32[]{:S(2)}) collective-permute-start(f32[16,128]{1,0:T(8,128)S(1)} %get-tuple-element.51), channel_id=1, source_target_pairs={{0,1},{1,2},{2,3},{3,4},{4,5},{5,6},{6,7},{7,8},{8,9},{9,10},{10,1... | collective-permute-start | bytes 24584 | tf_op jit(solution)/shard_map/ppermute | solution.py:424
  0.9 18.0 %collective-permute-start.1 = (f32[16,128]{1,0:T(8,128)S(1)}, f32[16,128]{1,0:T(8,128)S(1)}, u32[]{:S(2)}, u32[]{:S(2)}) collective-permute-start(f32[16,128]{1,0:T(8,128)S(1)} %get-tuple-element.52), channel_id=1, source_target_pairs={{0,2},{1,3},{2,4},{3,5},{4,6},{5,7},{6,8},{7,9},{8,10},{9,11},{10,... | collective-permute-start | bytes 24584 | tf_op jit(solution)/shard_map/ppermute | solution.py:424
  2.6 16.3 %collective-permute-start.2 = (f32[16,128]{1,0:T(8,128)S(1)}, f32[16,128]{1,0:T(8,128)S(1)}, u32[]{:S(2)}, u32[]{:S(2)}) collective-permute-start(f32[16,128]{1,0:T(8,128)S(1)} %get-tuple-element.53), channel_id=1, source_target_pairs={{0,126},{1,127},{2,0},{3,1},{4,2},{5,3},{6,4},{7,5},{8,6},{9,7},{1... | collective-permute-start | bytes 24584 | tf_op jit(solution)/shard_map/ppermute | solution.py:424
  9.8 9.1 %collective-permute-start.3 = (f32[16,128]{1,0:T(8,128)S(1)}, f32[16,128]{1,0:T(8,128)S(1)}, u32[]{:S(2)}, u32[]{:S(2)}) collective-permute-start(f32[16,128]{1,0:T(8,128)S(1)} %get-tuple-element.54), channel_id=1, source_target_pairs={{0,127},{1,0},{2,1},{3,2},{4,3},{5,4},{6,5},{7,6},{8,7},{9,8},{10,... | collective-permute-start | bytes 24584 | tf_op jit(solution)/shard_map/ppermute | solution.py:424
  19.9 8.6 %collective-permute-start.5 = (f32[16,128]{1,0:T(8,128)S(1)}, f32[16,128]{1,0:T(8,128)S(1)}, u32[]{:S(2)}, u32[]{:S(2)}) collective-permute-start(f32[16,128]{1,0:T(8,128)S(1)} %get-tuple-element.57), channel_id=1, source_target_pairs={{0,127},{1,3},{2,1},{3,4},{4,2},{5,6},{6,5},{7,8},{8,7},{9,11},{10... | collective-permute-start | bytes 24584 | tf_op jit(solution)/shard_map/ppermute | solution.py:424
  22.2 9.2 %collective-permute-start.6 = (f32[16,128]{1,0:T(8,128)S(1)}, f32[16,128]{1,0:T(8,128)S(1)}, u32[]{:S(2)}, u32[]{:S(2)}) collective-permute-start(f32[16,128]{1,0:T(8,128)S(1)} %get-tuple-element.58), channel_id=1, source_target_pairs={{0,126},{1,2},{2,4},{3,5},{4,3},{5,7},{6,8},{7,9},{8,6},{9,10},{10... | collective-permute-start | bytes 24584 | tf_op jit(solution)/shard_map/ppermute | solution.py:424
  23.4 8.0 %collective-permute-start.7 = (f32[16,128]{1,0:T(8,128)S(1)}, f32[16,128]{1,0:T(8,128)S(1)}, u32[]{:S(2)}, u32[]{:S(2)}) collective-permute-start(f32[16,128]{1,0:T(8,128)S(1)} %get-tuple-element.59), channel_id=1, source_target_pairs={{0,2},{1,0},{2,3},{3,1},{4,5},{5,4},{6,7},{7,6},{8,10},{9,8},{10,1... | collective-permute-start | bytes 24584 | tf_op jit(solution)/shard_map/ppermute | solution.py:424
  31.9 8.6 %collective-permute-start.9 = (f32[16,128]{1,0:T(8,128)S(1)}, f32[16,128]{1,0:T(8,128)S(1)}, u32[]{:S(2)}, u32[]{:S(2)}) collective-permute-start(f32[16,128]{1,0:T(8,128)S(1)} %get-tuple-element.62), channel_id=1, source_target_pairs={{0,127},{1,3},{2,1},{3,4},{4,2},{5,6},{6,5},{7,8},{8,7},{9,11},{10... | collective-permute-start | bytes 24584 | tf_op jit(solution)/shard_map/ppermute | solution.py:424
  32.9 9.2 %collective-permute-start.10 = (f32[16,128]{1,0:T(8,128)S(1)}, f32[16,128]{1,0:T(8,128)S(1)}, u32[]{:S(2)}, u32[]{:S(2)}) collective-permute-start(f32[16,128]{1,0:T(8,128)S(1)} %get-tuple-element.63), channel_id=1, source_target_pairs={{0,126},{1,2},{2,4},{3,5},{4,3},{5,7},{6,8},{7,9},{8,6},{9,10},{10... | collective-permute-start | bytes 24584 | tf_op jit(solution)/shard_map/ppermute | solution.py:424
  34.1 8.0 %collective-permute-start.11 = (f32[16,128]{1,0:T(8,128)S(1)}, f32[16,128]{1,0:T(8,128)S(1)}, u32[]{:S(2)}, u32[]{:S(2)}) collective-permute-start(f32[16,128]{1,0:T(8,128)S(1)} %get-tuple-element.64), channel_id=1, source_target_pairs={{0,2},{1,0},{2,3},{3,1},{4,5},{5,4},{6,7},{7,6},{8,10},{9,8},{10,1... | collective-permute-start | bytes 24584 | tf_op jit(solution)/shard_map/ppermute | solution.py:424
  42.6 8.6 %collective-permute-start.13 = (f32[16,128]{1,0:T(8,128)S(1)}, f32[16,128]{1,0:T(8,128)S(1)}, u32[]{:S(2)}, u32[]{:S(2)}) collective-permute-start(f32[16,128]{1,0:T(8,128)S(1)} %get-tuple-element.67), channel_id=1, source_target_pairs={{0,127},{1,3},{2,1},{3,4},{4,2},{5,6},{6,5},{7,8},{8,7},{9,11},{10... | collective-permute-start | bytes 24584 | tf_op jit(solution)/shard_map/ppermute | solution.py:424
  44.3 9.2 %collective-permute-start.14 = (f32[16,128]{1,0:T(8,128)S(1)}, f32[16,128]{1,0:T(8,128)S(1)}, u32[]{:S(2)}, u32[]{:S(2)}) collective-permute-start(f32[16,128]{1,0:T(8,128)S(1)} %get-tuple-element.68), channel_id=1, source_target_pairs={{0,126},{1,2},{2,4},{3,5},{4,3},{5,7},{6,8},{7,9},{8,6},{9,10},{10... | collective-permute-start | bytes 24584 | tf_op jit(solution)/shard_map/ppermute | solution.py:424
  44.7 8.8 %collective-permute-start.15 = (f32[16,128]{1,0:T(8,128)S(1)}, f32[16,128]{1,0:T(8,128)S(1)}, u32[]{:S(2)}, u32[]{:S(2)}) collective-permute-start(f32[16,128]{1,0:T(8,128)S(1)} %get-tuple-element.69), channel_id=1, source_target_pairs={{0,2},{1,0},{2,3},{3,1},{4,5},{5,4},{6,7},{7,6},{8,10},{9,8},{10,1... | collective-permute-start | bytes 24584 | tf_op jit(solution)/shard_map/ppermute | solution.py:424
  54.1 8.6 %collective-permute-start.17 = (f32[16,128]{1,0:T(8,128)S(1)}, f32[16,128]{1,0:T(8,128)S(1)}, u32[]{:S(2)}, u32[]{:S(2)}) collective-permute-start(f32[16,128]{1,0:T(8,128)S(1)} %get-tuple-element.72), channel_id=1, source_target_pairs={{0,127},{1,3},{2,1},{3,4},{4,2},{5,6},{6,5},{7,8},{8,7},{9,11},{10... | collective-permute-start | bytes 24584 | tf_op jit(solution)/shard_map/ppermute | solution.py:424
  55.0 9.2 %collective-permute-start.18 = (f32[16,128]{1,0:T(8,128)S(1)}, f32[16,128]{1,0:T(8,128)S(1)}, u32[]{:S(2)}, u32[]{:S(2)}) collective-permute-start(f32[16,128]{1,0:T(8,128)S(1)} %get-tuple-element.73), channel_id=1, source_target_pairs={{0,126},{1,2},{2,4},{3,5},{4,3},{5,7},{6,8},{7,9},{8,6},{9,10},{10... | collective-permute-start | bytes 24584 | tf_op jit(solution)/shard_map/ppermute | solution.py:424
  55.4 8.8 %collective-permute-start.19 = (f32[16,128]{1,0:T(8,128)S(1)}, f32[16,128]{1,0:T(8,128)S(1)}, u32[]{:S(2)}, u32[]{:S(2)}) collective-permute-start(f32[16,128]{1,0:T(8,128)S(1)} %get-tuple-element.74), channel_id=1, source_target_pairs={{0,2},{1,0},{2,3},{3,1},{4,5},{5,4},{6,7},{7,6},{8,10},{9,8},{10,1... | collective-permute-start | bytes 24584 | tf_op jit(solution)/shard_map/ppermute | solution.py:424
  64.7 8.6 %collective-permute-start.21 = (f32[16,128]{1,0:T(8,128)S(1)}, f32[16,128]{1,0:T(8,128)S(1)}, u32[]{:S(2)}, u32[]{:S(2)}) collective-permute-start(f32[16,128]{1,0:T(8,128)S(1)} %get-tuple-element.77), channel_id=1, source_target_pairs={{0,127},{1,3},{2,1},{3,4},{4,2},{5,6},{6,5},{7,8},{8,7},{9,11},{10... | collective-permute-start | bytes 24584 | tf_op jit(solution)/shard_map/ppermute | solution.py:424
  66.2 9.2 %collective-permute-start.22 = (f32[16,128]{1,0:T(8,128)S(1)}, f32[16,128]{1,0:T(8,128)S(1)}, u32[]{:S(2)}, u32[]{:S(2)}) collective-permute-start(f32[16,128]{1,0:T(8,128)S(1)} %get-tuple-element.78), channel_id=1, source_target_pairs={{0,126},{1,2},{2,4},{3,5},{4,3},{5,7},{6,8},{7,9},{8,6},{9,10},{10... | collective-permute-start | bytes 24584 | tf_op jit(solution)/shard_map/ppermute | solution.py:424
  66.7 8.7 %collective-permute-start.23 = (f32[16,128]{1,0:T(8,128)S(1)}, f32[16,128]{1,0:T(8,128)S(1)}, u32[]{:S(2)}, u32[]{:S(2)}) collective-permute-start(f32[16,128]{1,0:T(8,128)S(1)} %get-tuple-element.79), channel_id=1, source_target_pairs={{0,2},{1,0},{2,3},{3,1},{4,5},{5,4},{6,7},{7,6},{8,10},{9,8},{10,1... | collective-permute-start | bytes 24584 | tf_op jit(solution)/shard_map/ppermute | solution.py:424
  75.9 5.1 %collective-permute-start.24 = (f32[16,128]{1,0:T(8,128)S(1)}, f32[16,128]{1,0:T(8,128)S(1)}, u32[]{:S(2)}, u32[]{:S(2)}) collective-permute-start(f32[16,128]{1,0:T(8,128)S(1)} %get-tuple-element.81), channel_id=1, source_target_pairs={{0,1},{1,127},{2,0},{3,2},{4,6},{5,3},{6,4},{7,5},{8,9},{9,7},{10,... | collective-permute-start | bytes 24584 | tf_op jit(solution)/shard_map/ppermute | solution.py:424
  76.0 8.6 %collective-permute-start.25 = (f32[16,128]{1,0:T(8,128)S(1)}, f32[16,128]{1,0:T(8,128)S(1)}, u32[]{:S(2)}, u32[]{:S(2)}) collective-permute-start(f32[16,128]{1,0:T(8,128)S(1)} %get-tuple-element.82), channel_id=1, source_target_pairs={{0,127},{1,3},{2,1},{3,4},{4,2},{5,6},{6,5},{7,8},{8,7},{9,11},{10... | collective-permute-start | bytes 24584 | tf_op jit(solution)/shard_map/ppermute | solution.py:424
  77.0 9.2 %collective-permute-start.26 = (f32[16,128]{1,0:T(8,128)S(1)}, f32[16,128]{1,0:T(8,128)S(1)}, u32[]{:S(2)}, u32[]{:S(2)}) collective-permute-start(f32[16,128]{1,0:T(8,128)S(1)} %get-tuple-element.83), channel_id=1, source_target_pairs={{0,126},{1,2},{2,4},{3,5},{4,3},{5,7},{6,8},{7,9},{8,6},{9,10},{10... | collective-permute-start | bytes 24584 | tf_op jit(solution)/shard_map/ppermute | solution.py:424
  77.4 8.8 %collective-permute-start.27 = (f32[16,128]{1,0:T(8,128)S(1)}, f32[16,128]{1,0:T(8,128)S(1)}, u32[]{:S(2)}, u32[]{:S(2)}) collective-permute-start(f32[16,128]{1,0:T(8,128)S(1)} %get-tuple-element.84), channel_id=1, source_target_pairs={{0,2},{1,0},{2,3},{3,1},{4,5},{5,4},{6,7},{7,6},{8,10},{9,8},{10,1... | collective-permute-start | bytes 24584 | tf_op jit(solution)/shard_map/ppermute | solution.py:424
  87.3 13.9 %all-to-all-start = ((f32[128,1,32]{2,1,0:T(1,128)}), f32[128,1,32]{2,1,0:T(1,128)S(1)}, u32[]{:S(2)}, u32[]{:S(2)}) async-start(f32[128,1,32]{2,1,0:T(1,128)} %bitcast.3), calls=%async_computation | async-start | bytes 131072 | tf_op jit(solution)/shard_map/all_to_all | solution.py:521
  (5 other events, 25.2 us)
